TPU v7x, 8 devices: a whole 2x2x1 slice. The times are simulated.
8 devices in a mesh: dp: 2 (over z, y), sp: 4 (over x, core).
Axes of the slice: x: 2, y: 2, z: 1, core: 2. Of those that a mesh axis runs over, the one named last changes fastest.
Arguments:
- hidden: bfloat16 [1024, 2048], P('dp'), parts along dimension 0
- w_norm: bfloat16 [2048], replicated
- w_q: bfloat16 [2048, 2048], replicated
- w_k: bfloat16 [2048, 256], replicated
- w_v: bfloat16 [2048, 256], replicated
- w_o: bfloat16 [2048, 2048], replicated
- k_cache: bfloat16 [1024, 512, 256], P('dp', 'sp'), parts along dimension 0
- v_cache: bfloat16 [1024, 512, 256], P('dp', 'sp'), parts along dimension 0
- cache_len: int32 [1024], P('dp'), parts along dimension 0
Outputs:
- output 1: bfloat16 [1024, 2048], P('dp'), parts along dimension 0
- output 2: bfloat16 [1024, 512, 256], P('dp', 'sp'), parts along dimension 0
- output 3: bfloat16 [1024, 512, 256], P('dp', 'sp'), parts along dimension 0
There are 2 independent parts. A program takes and returns all parts, laid end to end along the dimension named above; an argument that names none is the same for every part.
All inputs are finite; a program needn't handle non-finite values.
Results may differ from a plain program's by a relative error of at most 0.0126525.
Values sent between devices are 32-bit elements.
A program may use at most 1 GiB of HBM per device.

v0:
```python
import functools

import jax
import jax.numpy as jnp
import numpy as np
from jax import lax
from jax.experimental import pallas as pl
from jax.experimental.pallas import tpu as pltpu
from jax.sharding import PartitionSpec as P

ROPE_BASE = 10000.0
EPSILON = 1e-6
HEADS = 8
HEAD = 256
GROUP = 16
LOWEST = float(jnp.finfo(jnp.float32).min)
CHUNKS = (32, 48, 80, 64, 32)
HBM = pl.BlockSpec(memory_space=pltpu.HBM)
ANY = pl.BlockSpec(memory_space=pl.ANY)
VMEM = pl.BlockSpec(memory_space=pltpu.VMEM)
SMEM = pl.BlockSpec(memory_space=pltpu.SMEM)


def project_kernel(hidden, w_norm, w_q, w_k, w_v, lengths, freq, q_out, k_out, v_out, x, wide, narrow, xn, cos_t, sin_t, q_low, q_high, sem):
    rows = hidden.shape[0]
    half = HEAD // 2
    tiles = ([pltpu.make_async_copy(w_k, narrow.at[0], sem.at[0]), pltpu.make_async_copy(w_v, narrow.at[1], sem.at[1])]
             + [pltpu.make_async_copy(w_q.at[:, h * HEAD:(h + 1) * HEAD], wide.at[h], sem.at[2 + h]) for h in range(HEADS)])
    first = pltpu.make_async_copy(hidden, x, sem.at[2 + HEADS])
    first.start()
    for copy in tiles:
        copy.start()
    angles = lengths[...].astype(jnp.float32) * freq[...]
    cos_t[...] = jnp.cos(angles)
    sin_t[...] = jnp.sin(angles)
    gain = 1.0 + w_norm[...].astype(jnp.float32)
    first.wait()

    def norm(i, carry):
        at = pl.ds(pl.multiple_of(i * 32, 32), 32)
        row = x[at, :].astype(jnp.float32)
        scale = lax.rsqrt(jnp.mean(row * row, axis=-1, keepdims=True) + EPSILON)
        xn[at, :] = (row * scale * gain).astype(jnp.bfloat16)
        return carry

    lax.fori_loop(0, rows // 32, norm, 0)

    def product(w):
        return jnp.dot(xn[...], w, preferred_element_type=jnp.float32).astype(jnp.bfloat16).astype(jnp.float32)

    def rotated(u):
        lower, upper = u[:, :half], u[:, half:]
        return lower * cos_t[...] - upper * sin_t[...], upper * cos_t[...] + lower * sin_t[...]

    tiles[0].wait()
    lower, upper = rotated(product(narrow[0]))
    k_out[:, :half] = lower.astype(jnp.bfloat16).astype(jnp.float32)
    k_out[:, half:] = upper.astype(jnp.bfloat16).astype(jnp.float32)
    tiles[1].wait()
    v_out[...] = product(narrow[1])

    def head(h, carry):
        pltpu.make_async_copy(w_k, wide.at[h], sem.at[2 + h]).wait()
        lower, upper = rotated(product(wide[h]))
        q_low[pl.ds(h, rows, stride=HEADS), :] = lower * HEAD ** -0.5
        q_high[pl.ds(h, rows, stride=HEADS), :] = upper * HEAD ** -0.5
        return carry

    lax.fori_loop(0, HEADS, head, 0)

    def pack(i, carry):
        at = pl.ds(pl.multiple_of(i * 128, 128), 128)
        q_out[at, :half] = q_low[at, :].astype(jnp.bfloat16)
        q_out[at, half:] = q_high[at, :].astype(jnp.bfloat16)
        return carry

    lax.fori_loop(0, rows * HEADS // 128, pack, 0)


def project_call(hidden, w_norm, w_q, w_k, w_v, cache_len):
    rows, dim = hidden.shape
    freq = (ROPE_BASE ** (-np.arange(HEAD // 2, dtype=np.float32) * np.float32(2.0) / np.float32(HEAD))).astype(np.float32)
    half_row = pltpu.VMEM((rows, HEAD // 2), jnp.float32)
    half_q = pltpu.VMEM((rows * HEADS, HEAD // 2), jnp.float32)
    return pl.pallas_call(
        project_kernel,
        in_specs=[HBM, VMEM, HBM, HBM, HBM, VMEM, VMEM],
        out_specs=(VMEM, VMEM, VMEM),
        out_shape=(jax.ShapeDtypeStruct((rows * HEADS, HEAD), jnp.bfloat16), jax.ShapeDtypeStruct((rows, HEAD), jnp.float32),
                   jax.ShapeDtypeStruct((rows, HEAD), jnp.float32)),
        scratch_shapes=[pltpu.VMEM((rows, dim), jnp.bfloat16), pltpu.VMEM((HEADS, dim, HEAD), jnp.bfloat16),
                        pltpu.VMEM((2, dim, HEAD), jnp.bfloat16), pltpu.VMEM((rows, dim), jnp.bfloat16), half_row, half_row, half_q, half_q,
                        pltpu.SemaphoreType.DMA((3 + HEADS,))],
        compiler_params=pltpu.CompilerParams(vmem_limit_bytes=40 << 20),
        cost_estimate=pl.CostEstimate(flops=2 * rows * dim * 10 * HEAD, bytes_accessed=24 << 20, transcendentals=0),
        name="project",
    )(hidden, w_norm.reshape(1, dim), w_q, w_k, w_v, cache_len.reshape(rows, 1), jnp.asarray(freq).reshape(1, HEAD // 2))


def attend_group(kbuf, vbuf, q, plane, slot_base, store):
    slots = kbuf.shape[1]
    lane = lax.broadcasted_iota(jnp.int32, (slots, 128), 1)
    scores = jnp.zeros((slots, 128), jnp.float32)
    for half in range(2):
        rows = GROUP // 2
        keys = kbuf[pl.ds(half * rows, rows)].reshape(rows * slots, HEAD)
        product = lax.dot_general(keys, q, (((1,), (1,)), ((), ())), preferred_element_type=jnp.float32)
        for i in range(rows):
            b = half * rows + i
            scores = jnp.where(lane // HEADS == b, product[i * slots:(i + 1) * slots], scores)
    position = slot_base + lax.broadcasted_iota(jnp.int32, (slots, 128), 0)
    valid = position <= plane
    scores = jnp.where(valid, scores, LOWEST)
    top = jnp.max(scores, axis=0, keepdims=True)
    weights = jnp.where(valid, jnp.exp(scores - top), 0.0)
    total = jnp.sum(weights, axis=0, keepdims=True)
    by_head = weights.T.astype(jnp.bfloat16)
    for pair in range(GROUP // 2):
        lhs = by_head[pair * 16:(pair + 1) * 16]
        first = jnp.dot(lhs, vbuf[2 * pair], preferred_element_type=jnp.float32)
        second = jnp.dot(lhs, vbuf[2 * pair + 1], preferred_element_type=jnp.float32)
        store(pair, jnp.concatenate([first[:8], second[8:]], axis=0))
    return top, total


def attention_kernel(groups, after, chained, scalars, lengths, plane, q, k_new, v_new, k_in, v_in, *rest):
    rest = rest[2 * chained + after:]
    k_out, v_out, sent, kept, kbuf, vbuf, qbuf, k_row, v_row, in_sem, out_sem, small_sem = rest
    send_row, keep_row = pl.multiple_of(scalars[0], GROUP), pl.multiple_of(scalars[1], GROUP)
    slot_base = scalars[2]
    depth, _, slots, _ = kbuf.shape
    total_groups = 2 * groups
    ahead = depth - 3 if total_groups > depth else total_groups

    def row_of(g):
        return pl.multiple_of(jnp.where(g < groups, send_row + g * GROUP, keep_row + (g - groups) * GROUP), GROUP)

    def fetch(g):
        slot = lax.rem(g, depth)
        at = pl.ds(row_of(g), GROUP)
        return (pltpu.make_async_copy(k_in.at[at], kbuf.at[slot], in_sem.at[0, slot]),
                pltpu.make_async_copy(v_in.at[at], vbuf.at[slot], in_sem.at[1, slot]))

    def flush(g):
        slot = lax.rem(g, depth)
        at = pl.ds(row_of(g), GROUP)
        return (pltpu.make_async_copy(kbuf.at[slot], k_out.at[at], out_sem.at[0, slot]),
                pltpu.make_async_copy(vbuf.at[slot], v_out.at[at], out_sem.at[1, slot]))

    rows = groups * GROUP
    small = []
    for side, start in enumerate((send_row, keep_row)):
        small.append(pltpu.make_async_copy(q.at[pl.ds(pl.multiple_of(start * HEADS, 128), rows * HEADS)], qbuf.at[side], small_sem.at[3 * side]))
        small.append(pltpu.make_async_copy(k_new.at[pl.ds(start, rows)], k_row.at[side], small_sem.at[3 * side + 1]))
        small.append(pltpu.make_async_copy(v_new.at[pl.ds(start, rows)], v_row.at[side], small_sem.at[3 * side + 2]))
    for copy in small:
        copy.start()
    for g in range(ahead):
        for copy in fetch(g):
            copy.start()
    for copy in small:
        copy.wait()
    row_in_tile = lax.broadcasted_iota(jnp.int32, (16, HEAD), 0)

    def one(g, out, side, place):
        slot = lax.rem(g, depth)
        row0 = row_of(g)
        for copy in fetch(g):
            copy.wait()
        for b in range(GROUP):
            local = lengths[row0 + b] - slot_base

            @pl.when(jnp.logical_and(local >= 0, local < slots))
            def _():
                tile = pl.multiple_of(local // 16 * 16, 16)
                hit = row_in_tile == local - tile
                for buf, new in ((kbuf, k_row), (vbuf, v_row)):
                    old = buf[slot, b, pl.ds(tile, 16), :].astype(jnp.float32)
                    row = new[side, pl.ds(place * GROUP + b, 1), :]
                    buf[slot, b, pl.ds(tile, 16), :] = jnp.where(hit, row, old).astype(jnp.bfloat16)

        def store(pair, value):
            out[pl.ds(pl.multiple_of(place * 128, 128) + pair * 16, 16), :] = value

        queries = qbuf[side, pl.ds(pl.multiple_of(place * 128, 128), 128), :]
        top, total = attend_group(kbuf.at[slot], vbuf.at[slot], queries, plane[pl.ds(row0 // GROUP, 1), :], slot_base, store)
        mine = lax.broadcasted_iota(jnp.int32, (8, HEAD), 0) == place
        out[groups * 128:, :] = jnp.where(mine, jnp.concatenate([top, total], axis=1), out[groups * 128:, :])
        for copy in flush(g):
            copy.start()
        if total_groups > depth:
            @pl.when(g + ahead < total_groups)
            def _():
                @pl.when(g + ahead >= depth)
                def _():
                    for copy in flush(g + ahead - depth):
                        copy.wait()

                for copy in fetch(g + ahead):
                    copy.start()

    def send_body(g, carry):
        one(g, sent, 0, g)
        return carry

    def keep_body(g, carry):
        one(g, kept, 1, g - groups)
        return carry

    for out in (sent, kept):
        out[groups * 128:, :] = jnp.zeros((8, HEAD), jnp.float32)
    lax.fori_loop(0, groups, send_body, 0)
    lax.fori_loop(groups, total_groups, keep_body, 0)
    for g in range(max(total_groups - depth, 0), total_groups):
        for copy in flush(g):
            copy.wait()


def attention_call(rows, scalars, lengths, plane, q, k_new, v_new, k_block, v_block, outs, after):
    groups = rows // GROUP
    depth = min(2 * groups, 8)
    slots = k_block.shape[1]
    operands = [scalars, lengths, plane, q, k_new, v_new, k_block, v_block, *outs, *after]
    part = jax.ShapeDtypeStruct((rows * HEADS + 8, HEAD), jnp.float32)
    return pl.pallas_call(
        functools.partial(attention_kernel, groups, len(after), bool(outs)),
        out_shape=(jax.ShapeDtypeStruct(k_block.shape, k_block.dtype), jax.ShapeDtypeStruct(v_block.shape, v_block.dtype), part, part),
        in_specs=[SMEM, SMEM, VMEM] + [HBM] * (5 + len(outs)) + [ANY] * len(after),
        out_specs=(HBM, HBM, VMEM, VMEM),
        input_output_aliases={8: 0, 9: 1} if outs else {},
        scratch_shapes=[
            pltpu.VMEM((depth, GROUP, slots, HEAD), jnp.bfloat16),
            pltpu.VMEM((depth, GROUP, slots, HEAD), jnp.bfloat16),
            pltpu.VMEM((2, rows * HEADS, HEAD), jnp.bfloat16),
            pltpu.VMEM((2, rows, HEAD), jnp.float32),
            pltpu.VMEM((2, rows, HEAD), jnp.float32),
            pltpu.SemaphoreType.DMA((2, depth)),
            pltpu.SemaphoreType.DMA((2, depth)),
            pltpu.SemaphoreType.DMA((6,)),
        ],
        compiler_params=pltpu.CompilerParams(vmem_limit_bytes=30 << 20),
        cost_estimate=pl.CostEstimate(flops=rows * 20_000_000, bytes_accessed=rows * 524288, transcendentals=rows * 16 * slots),
    )(*operands)


def merge_scales(one, two, groups, normalize):
    at = pl.ds(groups * 128, 8)
    top_a, top_b = one[at, :128], two[at, :128]
    top = jnp.maximum(top_a, top_b)
    scale_a, scale_b = jnp.exp(top_a - top), jnp.exp(top_b - top)
    total = one[at, 128:] * scale_a + two[at, 128:] * scale_b
    if normalize:
        scale_a, scale_b = scale_a / total, scale_b / total
    stacked = jnp.concatenate([scale_a, scale_b, jnp.zeros((112, 128), jnp.float32)], axis=0)
    return stacked.T, top, total


def merge_kernel(groups, one, two, out):
    columns, top, total = merge_scales(one, two, groups, False)
    for g in range(groups):
        at = pl.ds(g * 128, 128)
        out[at, :] = one[at, :] * columns[:, g:g + 1] + two[at, :] * columns[:, 8 + g:9 + g]
    out[groups * 128:, :128] = top
    out[groups * 128:, 128:] = total


def merge_call(rows, one, two):
    return pl.pallas_call(
        functools.partial(merge_kernel, rows // GROUP),
        out_shape=jax.ShapeDtypeStruct(one.shape, one.dtype),
        in_specs=[VMEM, VMEM],
        out_specs=VMEM,
        compiler_params=pltpu.CompilerParams(vmem_limit_bytes=8 << 20),
        cost_estimate=pl.CostEstimate(flops=rows * 2_000_000, bytes_accessed=rows * 24576, transcendentals=0),
    )(one, two)


def finish_kernel(chunks, *refs):
    parts = refs[:2 * len(chunks)]
    w_o, y, low, high, attended = refs[2 * len(chunks):]
    first = 0
    for i, rows in enumerate(chunks):
        groups = rows // GROUP
        one, two = parts[2 * i], parts[2 * i + 1]
        columns, _, _ = merge_scales(one, two, groups, True)
        for g in range(groups):
            at = pl.ds(g * 128, 128)
            value = one[at, :] * columns[:, g:g + 1] + two[at, :] * columns[:, 8 + g:9 + g]
            low[at, :] = value[:, :128]
            high[at, :] = value[:, 128:]
        for h in range(HEADS):
            for side, source in enumerate((low, high)):
                column = h * HEAD + side * 128
                attended[first:first + rows, column:column + 128] = source[pl.ds(h, rows, stride=HEADS), :].astype(jnp.bfloat16)
        first += rows

    @pl.loop(0, y.shape[1] // 256)
    def _(n):
        at = pl.ds(pl.multiple_of(n * 256, 256), 256)
        y[:, at] = jnp.dot(attended[...], w_o[:, at], preferred_element_type=jnp.float32)


def finish_call(chunks, parts, w_o):
    total = sum(chunks)
    return pl.pallas_call(
        functools.partial(finish_kernel, chunks),
        out_shape=jax.ShapeDtypeStruct((total, w_o.shape[1]), jnp.float32),
        in_specs=[VMEM] * (len(parts) + 1),
        out_specs=VMEM,
        scratch_shapes=[pltpu.VMEM((max(chunks) * HEADS, 128), jnp.float32), pltpu.VMEM((max(chunks) * HEADS, 128), jnp.float32), pltpu.VMEM((total, w_o.shape[0]), jnp.bfloat16)],
        compiler_params=pltpu.CompilerParams(vmem_limit_bytes=32 << 20),
        cost_estimate=pl.CostEstimate(flops=2 * total * w_o.shape[0] * w_o.shape[1], bytes_accessed=10 << 20, transcendentals=0),
    )(*parts, w_o)


def local_step(hidden, w_norm, w_q, w_k, w_v, w_o, k_block, v_block, cache_len):
    num_rows = hidden.shape[0]
    half = num_rows // 2
    slots = k_block.shape[1]
    me = lax.axis_index('sp')
    core = lax.rem(me, 2)
    sibling = [(0, 1), (1, 0), (2, 3), (3, 2)]
    across = [(0, 2), (2, 0), (1, 3), (3, 1)]
    q, k_new, v_new = project_call(hidden, w_norm, w_q, w_k, w_v, cache_len)
    plane = jnp.repeat(cache_len, HEADS).reshape(num_rows // GROUP, 128)
    outs, merged, theirs = (), [], []
    first = 0
    last = len(CHUNKS) - 1

    def join(i, kept, taken):
        merged.append(merge_call(CHUNKS[i], kept, taken))
        theirs.append(lax.ppermute(merged[-1], 'sp', across))

    pending = None
    for i, rows in enumerate(CHUNKS):
        scalars = jnp.stack([(1 - core) * half + first, core * half + first, me * slots]).astype(jnp.int32)
        k_out, v_out, sent, kept = attention_call(rows, scalars, cache_len, plane, q, k_new, v_new, k_block, v_block, outs, merged[-1:])
        outs = (k_out, v_out)
        if pending is not None:
            join(i - 1, *pending)
        pending = (kept, lax.ppermute(sent, 'sp', sibling))
        first += rows
    join(last, *pending)
    early = [p for pair in list(zip(merged, theirs))[:-1] for p in pair]
    ys = [finish_call(CHUNKS[:-1], early, w_o)]
    ys.append(finish_call(CHUNKS[-1:], [merged[-1], theirs[-1]], w_o))
    others = []
    for y in ys:
        others.append(lax.ppermute(y, 'sp', sibling))
    mine, other = jnp.concatenate(ys), jnp.concatenate(others)
    delta = jnp.where(core == 0, jnp.concatenate([mine, other]), jnp.concatenate([other, mine]))
    return (hidden.astype(jnp.float32) + delta).astype(jnp.bfloat16), outs[0], outs[1]


def solution(mesh):
    cache_spec = P('dp', 'sp', None)
    return jax.shard_map(local_step, mesh=mesh, in_specs=(P('dp', None), P(None), P(None, None), P(None, None), P(None, None), P(None, None), cache_spec, cache_spec, P('dp')), out_specs=(P('dp', None), cache_spec, cache_spec), check_vma=False)
```

profile of v0, /device:TPU:0, one launch (start us, length us, event | category | flops | bytes accessed | tf_op | source)
XLA Modules:
  0.0 161.2 jit_solution(16409025796703732003)
XLA Ops:
  0.6 0.8 broadcast_in_dim.7
  1.5 0.7 reshape.17.w_norm
  2.3 0.8 copy.22.lengths
  3.2 1.6 copy-done.2
  4.8 1.2 copy-done.11
  6.0 1.2 copy-done.12
  7.9 12.4 %project.1 = (bf16[4096,256]{1,0:T(8,128)(2,1)S(1)}, f32[512,256]{1,0:T(8,128)S(1)}, f32[512,256]{1,0:T(8,128)S(1)}) custom-call(bf16[512,2048]{1,0:T(8,128)(2,1)S(1)} %copy-done.2, bf16[1,2048]{1,0:T(2,128)(2,1)S(1)} %reshape.17.w_norm, bf16[2048,2048]{1,0:T(8,128)(2,1)} %w_q.1, bf16[2048,256]{1,0:T(8,128)(2,1)S(1)} %copy-done.11, ...), custom_call_target="tpu_custom_call" | custom-call | flops 5368709120 | bytes 25165824 | tf_op jit(solution)/shard_map/project/pallas_call | solution.py:85
  20.3 8.9 %shard_map.121 = (bf16[512,128,256]{2,1,0:T(8,128)(2,1)}, bf16[512,128,256]{2,1,0:T(8,128)(2,1)}, f32[264,256]{1,0:T(8,128)}, f32[264,256]{1,0:T(8,128)S(1)}) custom-call(s32[3]{0:T(128)S(1)} %get-tuple-element.49.scalars, s32[512]{0:T(512)S(1)} %copy-done.10, s32[32,128]{1,0:T(8,128)S(1)} %copy.23.plane, bf16[4096,256]{1,0:T(8,128)(2,1)S(1)} %get-tuple-element.26.q, ...), custom_call_target="tpu_custom_call" | custom-call | flops 640000000 | bytes 16777216 | tf_op jit(solution)/shard_map/pallas_call | solution.py:225
  29.3 0.9 collective-permute-start
  30.2 11.5 %shard_map.123 = (bf16[512,128,256]{2,1,0:T(8,128)(2,1)}, bf16[512,128,256]{2,1,0:T(8,128)(2,1)}, f32[392,256]{1,0:T(8,128)}, f32[392,256]{1,0:T(8,128)S(1)}) custom-call(s32[3]{0:T(128)S(1)} %get-tuple-element.50.scalars, s32[512]{0:T(512)S(1)} %copy-done.10, s32[32,128]{1,0:T(8,128)S(1)} %copy.23.plane, ...), custom_call_target="tpu_custom_call", output_to_operand_aliasing={{0}: (8, {}), {1}: (9, {})} | custom-call | flops 960000000 | bytes 25165824 | tf_op jit(solution)/shard_map/pallas_call | solution.py:225
  41.7 0.7 copy-done.6
  42.7 1.0 copy-done.9
  43.6 1.2 shard_map.122.rest_2_.refs_0_
  44.9 17.4 %shard_map.125 = (bf16[512,128,256]{2,1,0:T(8,128)(2,1)}, bf16[512,128,256]{2,1,0:T(8,128)(2,1)}, f32[648,256]{1,0:T(8,128)}, f32[648,256]{1,0:T(8,128)S(1)}) custom-call(s32[3]{0:T(128)S(1)} %add_add_fusion.2.scalars, s32[512]{0:T(512)S(1)} %copy-done.10, s32[32,128]{1,0:T(8,128)S(1)} %copy.23.plane, ...), custom_call_target="tpu_custom_call", output_to_operand_aliasing={{0}: (8, {}), {1}: (9, {})} | custom-call | flops 1600000000 | bytes 41943040 | tf_op jit(solution)/shard_map/pallas_call | solution.py:225
  62.3 0.9 copy-done.4
  63.6 1.0 copy-done.7
  64.6 1.3 shard_map.124.rest_2_.refs_2_
  65.9 13.5 %shard_map.127 = (bf16[512,128,256]{2,1,0:T(8,128)(2,1)}, bf16[512,128,256]{2,1,0:T(8,128)(2,1)}, f32[520,256]{1,0:T(8,128)S(1)}, f32[520,256]{1,0:T(8,128)S(1)}) custom-call(s32[3]{0:T(128)S(1)} %add_add_fusion.3.scalars, s32[512]{0:T(512)S(1)} %copy-done.10, s32[32,128]{1,0:T(8,128)S(1)} %copy.23.plane, ...), custom_call_target="tpu_custom_call", output_to_operand_aliasing={{0}: (8, {}), {1}: (9, {})} | custom-call | flops 1280000000 | bytes 33554432 | tf_op jit(solution)/shard_map/pallas_call | solution.py:225
  79.4 0.7 collective-permute-start.6
  80.2 1.5 shard_map.126.refs_4_.rest_2_
  81.7 3.2 %collective-permute-start.5 = (f32[648,256]{1,0:T(8,128)S(1)}, f32[648,256]{1,0:T(8,128)S(1)}, u32[]{:S(2)}, u32[]{:S(2)}) collective-permute-start(f32[648,256]{1,0:T(8,128)S(1)} %shard_map.126.refs_4_.rest_2_), channel_id=1, source_target_pairs={{0,2},{2,0},{1,3},{3,1},{4,6},{6,4},{5,7},{7,5}} | collective-permute-start | bytes 1990664 | tf_op jit(solution)/shard_map/ppermute | solution.py:332
  85.3 1.9 %collective-permute-start.3 = (f32[392,256]{1,0:T(8,128)S(1)}, f32[392,256]{1,0:T(8,128)S(1)}, u32[]{:S(2)}, u32[]{:S(2)}) collective-permute-start(f32[392,256]{1,0:T(8,128)S(1)} %shard_map.124.rest_2_.refs_2_), channel_id=1, source_target_pairs={{0,2},{2,0},{1,3},{3,1},{4,6},{6,4},{5,7},{7,5}} | collective-permute-start | bytes 1204232 | tf_op jit(solution)/shard_map/ppermute | solution.py:332
  87.3 38.6 %collective-permute-done.1.refs_1_ = f32[264,256]{1,0:T(8,128)S(1)} collective-permute-done((f32[264,256]{1,0:T(8,128)S(1)}, f32[264,256]{1,0:T(8,128)S(1)}, u32[]{:S(2)}, u32[]{:S(2)}) %collective-permute-start.1) | collective-permute-done | bytes 270368 | tf_op jit(solution)/shard_map/ppermute | solution.py:332
  125.9 6.0 %shard_map.129 = f32[224,2048]{1,0:T(8,128)} custom-call(f32[264,256]{1,0:T(8,128)S(1)} %shard_map.122.rest_2_.refs_0_, f32[264,256]{1,0:T(8,128)S(1)} %collective-permute-done.1.refs_1_, f32[392,256]{1,0:T(8,128)S(1)} %shard_map.124.rest_2_.refs_2_, f32[392,256]{1,0:T(8,128)S(1)} %collective-permute-done.3.refs_3_, ...), custom_call_target="tpu_custom_call" | custom-call | flops 1879048192 | bytes 10485760 | tf_op jit(solution)/shard_map/pallas_call | solution.py:305
  132.0 1.2 copy-done.1
  133.2 7.9 %shard_map.130 = (bf16[512,128,256]{2,1,0:T(8,128)(2,1)}, bf16[512,128,256]{2,1,0:T(8,128)(2,1)}, f32[264,256]{1,0:T(8,128)S(1)}, f32[264,256]{1,0:T(8,128)S(1)}) custom-call(s32[3]{0:T(128)S(1)} %add_add_fusion.4.scalars, s32[512]{0:T(512)S(1)} %copy-done.10, s32[32,128]{1,0:T(8,128)S(1)} %copy.23.plane, ...), custom_call_target="tpu_custom_call", output_to_operand_aliasing={{0}: (8, {}), {1}: (9, {})} | custom-call | flops 640000000 | bytes 16777216 | tf_op jit(solution)/shard_map/pallas_call | solution.py:225
  141.8 1.2 collective-permute-done.8.two
  143.3 1.8 %collective-permute-start.9 = (f32[264,256]{1,0:T(8,128)S(1)}, f32[264,256]{1,0:T(8,128)S(1)}, u32[]{:S(2)}, u32[]{:S(2)}) collective-permute-start(f32[264,256]{1,0:T(8,128)S(1)} %shard_map.131.refs_0_), channel_id=1, source_target_pairs={{0,2},{2,0},{1,3},{3,1},{4,6},{6,4},{5,7},{7,5}} | collective-permute-start | bytes 811016 | tf_op jit(solution)/shard_map/ppermute | solution.py:332
  145.1 7.0 %collective-permute-done.9.refs_1_ = f32[264,256]{1,0:T(8,128)S(1)} collective-permute-done((f32[264,256]{1,0:T(8,128)S(1)}, f32[264,256]{1,0:T(8,128)S(1)}, u32[]{:S(2)}, u32[]{:S(2)}) %collective-permute-start.9) | collective-permute-done | bytes 270368 | tf_op jit(solution)/shard_map/ppermute | solution.py:332
  152.1 2.7 %shard_map.132 = f32[32,2048]{1,0:T(8,128)S(1)} custom-call(f32[264,256]{1,0:T(8,128)S(1)} %shard_map.131.refs_0_, f32[264,256]{1,0:T(8,128)S(1)} %collective-permute-done.9.refs_1_, bf16[2048,2048]{1,0:T(8,128)(2,1)S(1)} %bitcast.17), custom_call_target="tpu_custom_call" | custom-call | flops 268435456 | bytes 10485760 | tf_op jit(solution)/shard_map/pallas_call | solution.py:305
  154.8 1.5 collective-permute-done.11
  156.4 4.8 %fusion.1 = bf16[512,2048]{1,0:T(8,128)(2,1)} fusion(f32[32,2048]{1,0:T(8,128)S(1)} %collective-permute-done.11, f32[224,2048]{1,0:T(8,128)} %collective-permute-done.10, f32[32,2048]{1,0:T(8,128)S(1)} %shard_map.132, f32[224,2048]{1,0:T(8,128)} %shard_map.129, bf16[512,2048]{1,0:T(8,128)(2,1)S(1)} %copy-done.3, pred[]{:T(512)S(6)} %eq.3), kind=kLoop, calls=%fused_computation.2 | loop fusion | flops 10485760 | bytes 8388609 | tf_op jit(solution)/shard_map/convert_element_type | solution.py:352
  (54 shorter events, 3.2 us)
Async XLA Ops:
  3.2 1.6 copy-start.2
  4.8 1.2 copy-start.11
  6.0 1.2 copy-start.12
  7.2 0.7 copy-start.13
  7.9 12.5 %copy-start.10 = (s32[512]{0:T(512)S(1)}, s32[512]{0:T(512)}, u32[]{:S(2)}) copy-start(s32[512]{0:T(512)} %lengths.9) | copy-start | bytes 6148
  29.3 12.4 %copy-start.8 = (f32[264,256]{1,0:T(8,128)}, f32[264,256]{1,0:T(8,128)S(1)}, u32[]{:S(2)}) copy-start(f32[264,256]{1,0:T(8,128)S(1)} %get-tuple-element.29.one) | copy-start | bytes 811012
  29.3 13.4 %collective-permute-start = (f32[264,256]{1,0:T(8,128)}, f32[264,256]{1,0:T(8,128)}, u32[]{:S(2)}, u32[]{:S(2)}) collective-permute-start(f32[264,256]{1,0:T(8,128)} %get-tuple-element.30), channel_id=1, source_target_pairs={{0,1},{1,0},{2,3},{3,2},{4,5},{5,4},{6,7},{7,6}} | collective-permute-start | bytes 811016 | tf_op jit(solution)/shard_map/ppermute | solution.py:341
  41.7 0.7 copy-start.6
  42.4 21.1 %collective-permute-start.2 = (f32[392,256]{1,0:T(8,128)}, f32[392,256]{1,0:T(8,128)}, u32[]{:S(2)}, u32[]{:S(2)}) collective-permute-start(f32[392,256]{1,0:T(8,128)} %get-tuple-element.34), channel_id=1, source_target_pairs={{0,1},{1,0},{2,3},{3,2},{4,5},{5,4},{6,7},{7,6}} | collective-permute-start | bytes 1204232 | tf_op jit(solution)/shard_map/ppermute | solution.py:341
  42.7 1.0 copy-start.9
  62.3 0.9 copy-start.4
  63.1 17.1 %collective-permute-start.4 = (f32[648,256]{1,0:T(8,128)}, f32[648,256]{1,0:T(8,128)}, u32[]{:S(2)}, u32[]{:S(2)}) collective-permute-start(f32[648,256]{1,0:T(8,128)} %get-tuple-element.38), channel_id=1, source_target_pairs={{0,1},{1,0},{2,3},{3,2},{4,5},{5,4},{6,7},{7,6}} | collective-permute-start | bytes 1990664 | tf_op jit(solution)/shard_map/ppermute | solution.py:341
  63.6 1.0 copy-start.7
  65.9 60.0 %slice-start = ((s8[8388608]{0:T(1024)(128)(4,1)}), s8[4194304]{0:T(1024)(128)(4,1)S(1)}, s32[]{:S(2)}) async-start(s8[8388608]{0:T(1024)(128)(4,1)} %bitcast.14), calls=%async_computation | async-start | bytes 8388608
  65.9 14.3 %copy-start.5 = (f32[648,256]{1,0:T(8,128)S(1)}, f32[648,256]{1,0:T(8,128)}, u32[]{:S(2)}) copy-start(f32[648,256]{1,0:T(8,128)} %copy-done.4) | copy-start | bytes 1990660
  65.9 60.0 %slice-start.1 = ((s8[8388608]{0:T(1024)(128)(4,1)}), s8[4194304]{0:T(1024)(128)(4,1)S(1)}, s32[]{:S(2)}) async-start(s8[8388608]{0:T(1024)(128)(4,1)} %bitcast.14), calls=%async_computation.1 | async-start | bytes 8388608
  79.4 5.4 %collective-permute-start.6 = (f32[520,256]{1,0:T(8,128)S(1)}, f32[520,256]{1,0:T(8,128)S(1)}, u32[]{:S(2)}, u32[]{:S(2)}) collective-permute-start(f32[520,256]{1,0:T(8,128)S(1)} %get-tuple-element.42), channel_id=1, source_target_pairs={{0,1},{1,0},{2,3},{3,2},{4,5},{5,4},{6,7},{7,6}} | collective-permute-start | bytes 1597448 | tf_op jit(solution)/shard_map/ppermute | solution.py:341
  81.7 50.2 %copy-start = (f32[648,256]{1,0:T(8,128)}, f32[648,256]{1,0:T(8,128)S(1)}, u32[]{:S(2)}) copy-start(f32[648,256]{1,0:T(8,128)S(1)} %shard_map.126.refs_4_.rest_2_) | copy-start | bytes 1990660
  81.7 44.2 %collective-permute-start.5 = (f32[648,256]{1,0:T(8,128)S(1)}, f32[648,256]{1,0:T(8,128)S(1)}, u32[]{:S(2)}, u32[]{:S(2)}) collective-permute-start(f32[648,256]{1,0:T(8,128)S(1)} %shard_map.126.refs_4_.rest_2_), channel_id=1, source_target_pairs={{0,2},{2,0},{1,3},{3,1},{4,6},{6,4},{5,7},{7,5}} | collective-permute-start | bytes 1990664 | tf_op jit(solution)/shard_map/ppermute | solution.py:332
  85.2 40.7 %collective-permute-start.7 = (f32[520,256]{1,0:T(8,128)S(1)}, f32[520,256]{1,0:T(8,128)S(1)}, u32[]{:S(2)}, u32[]{:S(2)}) collective-permute-start(f32[520,256]{1,0:T(8,128)S(1)} %shard_map.128.refs_6_), channel_id=1, source_target_pairs={{0,2},{2,0},{1,3},{3,1},{4,6},{6,4},{5,7},{7,5}} | collective-permute-start | bytes 1597448 | tf_op jit(solution)/shard_map/ppermute | solution.py:332
  85.3 40.6 %collective-permute-start.3 = (f32[392,256]{1,0:T(8,128)S(1)}, f32[392,256]{1,0:T(8,128)S(1)}, u32[]{:S(2)}, u32[]{:S(2)}) collective-permute-start(f32[392,256]{1,0:T(8,128)S(1)} %shard_map.124.rest_2_.refs_2_), channel_id=1, source_target_pairs={{0,2},{2,0},{1,3},{3,1},{4,6},{6,4},{5,7},{7,5}} | collective-permute-start | bytes 1204232 | tf_op jit(solution)/shard_map/ppermute | solution.py:332
  87.2 38.7 %collective-permute-start.1 = (f32[264,256]{1,0:T(8,128)S(1)}, f32[264,256]{1,0:T(8,128)S(1)}, u32[]{:S(2)}, u32[]{:S(2)}) collective-permute-start(f32[264,256]{1,0:T(8,128)S(1)} %shard_map.122.rest_2_.refs_0_), channel_id=1, source_target_pairs={{0,2},{2,0},{1,3},{3,1},{4,6},{6,4},{5,7},{7,5}} | collective-permute-start | bytes 811016 | tf_op jit(solution)/shard_map/ppermute | solution.py:332
  131.9 24.4 %collective-permute-start.10 = (f32[224,2048]{1,0:T(8,128)}, f32[224,2048]{1,0:T(8,128)}, u32[]{:S(2)}, u32[]{:S(2)}) collective-permute-start(f32[224,2048]{1,0:T(8,128)} %shard_map.129), channel_id=1, source_target_pairs={{0,1},{1,0},{2,3},{3,2},{4,5},{5,4},{6,7},{7,6}} | collective-permute-start | bytes 5505032 | tf_op jit(solution)/shard_map/ppermute | solution.py:349
  132.0 20.1 %slice-start.2 = ((s8[8388608]{0:T(1024)(128)(4,1)}), s8[4194304]{0:T(1024)(128)(4,1)S(1)}, s32[]{:S(2)}) async-start(s8[8388608]{0:T(1024)(128)(4,1)} %bitcast.16), calls=%async_computation.2 | async-start | bytes 8388608
  132.0 1.2 copy-start.1
  133.2 18.9 %slice-start.3 = ((s8[8388608]{0:T(1024)(128)(4,1)}), s8[4194304]{0:T(1024)(128)(4,1)S(1)}, s32[]{:S(2)}) async-start(s8[8388608]{0:T(1024)(128)(4,1)} %bitcast.16), calls=%async_computation.3 | async-start | bytes 8388608
  141.1 1.9 %collective-permute-start.8 = (f32[264,256]{1,0:T(8,128)S(1)}, f32[264,256]{1,0:T(8,128)S(1)}, u32[]{:S(2)}, u32[]{:S(2)}) collective-permute-start(f32[264,256]{1,0:T(8,128)S(1)} %get-tuple-element.46), channel_id=1, source_target_pairs={{0,1},{1,0},{2,3},{3,2},{4,5},{5,4},{6,7},{7,6}} | collective-permute-start | bytes 811016 | tf_op jit(solution)/shard_map/ppermute | solution.py:341
  143.2 13.1 %copy-start.3 = (bf16[512,2048]{1,0:T(8,128)(2,1)S(1)}, bf16[512,2048]{1,0:T(8,128)(2,1)}, u32[]{:S(2)}) copy-start(bf16[512,2048]{1,0:T(8,128)(2,1)} %hidden.1) | copy-start | bytes 6291460
  143.3 8.9 %collective-permute-start.9 = (f32[264,256]{1,0:T(8,128)S(1)}, f32[264,256]{1,0:T(8,128)S(1)}, u32[]{:S(2)}, u32[]{:S(2)}) collective-permute-start(f32[264,256]{1,0:T(8,128)S(1)} %shard_map.131.refs_0_), channel_id=1, source_target_pairs={{0,2},{2,0},{1,3},{3,1},{4,6},{6,4},{5,7},{7,5}} | collective-permute-start | bytes 811016 | tf_op jit(solution)/shard_map/ppermute | solution.py:332
  154.8 1.5 collective-permute-start.11
where the time goes:
time: 162 us; the launch traced here: 161 us
  Pallas kernels  84.9 us (52%)
  waiting for transfers between devices  48.3 us (30%)
  local copies, waits for them, and re-layouts  12 us (7%)
  starting transfers between devices  10 us (6%)
  other arithmetic  5.11 us (3%)
    pallas_call x5, Pallas kernels, attention_call(): pl.pallas_call(functools.partial(attention_kernel, groups, len(after), bo...  59.2 us
    ppermute x5, waiting for transfers between devices, join(): theirs.append(lax.ppermute(merged[-1], 'sp', across))  45.6 us
    pallas_call x1, Pallas kernels, project_call(): pl.pallas_call(project_kernel, in_specs=[HBM, VMEM, HBM, HBM, HBM, VMEM,...  12.4 us
    unnamed x36, local copies, waits for them, and re-layouts  9.54 us
    pallas_call x2, Pallas kernels, finish_call(): pl.pallas_call(functools.partial(finish_kernel, chunks), out_shape=jax.Sh...  8.64 us
    ppermute x5, starting transfers between devices, join(): theirs.append(lax.ppermute(merged[-1], 'sp', across))  7.13 us
    convert_element_type x1, other arithmetic, local_step(): (hidden.astype(jnp.float32) + delta).astype(jnp.bfloat16)  4.8 us
    pallas_call x5, Pallas kernels, merge_call(): pl.pallas_call(functools.partial(merge_kernel, rows // GROUP), out_shape=...  4.55 us
  transfers between devices with their start and end apart: 12, of which 4 were waited for; matrix products, arithmetic and copies ran while one was open for 0% of the time, Pallas kernels for 36%

commit v1 on v0

v1 whole, which is shorter than its diff:
```python
import functools
import math

import jax
import jax.numpy as jnp
from jax import lax
from jax.experimental import pallas as pl
from jax.experimental.pallas import tpu as pltpu
from jax.sharding import PartitionSpec as P

ROPE_BASE = 10000.0
EPSILON = 1e-6
HEADS = 8
HEAD = 256
GROUP = 16
LOWEST = float(jnp.finfo(jnp.float32).min)
CHUNKS = (16, 48, 80, 80, 32)
HBM = pl.BlockSpec(memory_space=pltpu.HBM)
ANY = pl.BlockSpec(memory_space=pl.ANY)
VMEM = pl.BlockSpec(memory_space=pltpu.VMEM)
SMEM = pl.BlockSpec(memory_space=pltpu.SMEM)


def project_kernel(hidden, w_norm, w_q, w_k, w_v, lengths, q_out, k_out, v_out, x, wide, narrow, xn, cos_t, sin_t, q_low, q_high, sem):
    rows = hidden.shape[0]
    half = HEAD // 2
    tiles = ([pltpu.make_async_copy(w_k, narrow.at[0], sem.at[0]), pltpu.make_async_copy(w_v, narrow.at[1], sem.at[1])]
             + [pltpu.make_async_copy(w_q.at[:, h * HEAD:(h + 1) * HEAD], wide.at[h], sem.at[2 + h]) for h in range(HEADS)])
    first = pltpu.make_async_copy(hidden, x, sem.at[2 + HEADS])
    first.start()
    for copy in tiles:
        copy.start()
    count = lengths.shape[0]
    positions = jnp.concatenate([lengths[...], jnp.zeros((8 - count, 128), jnp.int32)], axis=0).astype(jnp.float32).T
    lane = lax.broadcasted_iota(jnp.int32, (1, half), 1).astype(jnp.float32)
    freq = jnp.exp(lane * (-2.0 / HEAD * math.log(ROPE_BASE)))
    for i in range(count):
        angles = positions[:, i:i + 1] * freq
        cos_t[i * 128:(i + 1) * 128, :] = jnp.cos(angles)
        sin_t[i * 128:(i + 1) * 128, :] = jnp.sin(angles)
    gain = 1.0 + w_norm[...].astype(jnp.float32)
    gain = jnp.concatenate([gain[i:i + 1] for i in range(w_norm.shape[0])], axis=1)
    first.wait()

    def norm(i, carry):
        at = pl.ds(pl.multiple_of(i * 32, 32), 32)
        row = x[at, :].astype(jnp.float32)
        scale = lax.rsqrt(jnp.mean(row * row, axis=-1, keepdims=True) + EPSILON)
        xn[at, :] = (row * scale * gain).astype(jnp.bfloat16)
        return carry

    lax.fori_loop(0, rows // 32, norm, 0)

    def product(w):
        return jnp.dot(xn[...], w, preferred_element_type=jnp.float32).astype(jnp.bfloat16).astype(jnp.float32)

    def rotated(u):
        lower, upper = u[:, :half], u[:, half:]
        return lower * cos_t[...] - upper * sin_t[...], upper * cos_t[...] + lower * sin_t[...]

    tiles[0].wait()
    lower, upper = rotated(product(narrow[0]))
    k_out[:, :half] = lower.astype(jnp.bfloat16).astype(jnp.float32)
    k_out[:, half:] = upper.astype(jnp.bfloat16).astype(jnp.float32)
    tiles[1].wait()
    v_out[...] = product(narrow[1])

    def head(h, carry):
        pltpu.make_async_copy(w_k, wide.at[h], sem.at[2 + h]).wait()
        lower, upper = rotated(product(wide[h]))
        q_low[pl.ds(h, rows, stride=HEADS), :] = lower * HEAD ** -0.5
        q_high[pl.ds(h, rows, stride=HEADS), :] = upper * HEAD ** -0.5
        return carry

    lax.fori_loop(0, HEADS, head, 0)

    def pack(i, carry):
        at = pl.ds(pl.multiple_of(i * 128, 128), 128)
        q_out[at, :half] = q_low[at, :].astype(jnp.bfloat16)
        q_out[at, half:] = q_high[at, :].astype(jnp.bfloat16)
        return carry

    lax.fori_loop(0, rows * HEADS // 128, pack, 0)


def project_call(hidden, w_norm, w_q, w_k, w_v, cache_len):
    rows, dim = hidden.shape
    half_row = pltpu.VMEM((rows, HEAD // 2), jnp.float32)
    half_q = pltpu.VMEM((rows * HEADS, HEAD // 2), jnp.float32)
    return pl.pallas_call(
        project_kernel,
        in_specs=[HBM, VMEM, HBM, HBM, HBM, VMEM],
        out_specs=(VMEM, VMEM, VMEM),
        out_shape=(jax.ShapeDtypeStruct((rows * HEADS, HEAD), jnp.bfloat16), jax.ShapeDtypeStruct((rows, HEAD), jnp.float32),
                   jax.ShapeDtypeStruct((rows, HEAD), jnp.float32)),
        scratch_shapes=[pltpu.VMEM((rows, dim), jnp.bfloat16), pltpu.VMEM((HEADS, dim, HEAD), jnp.bfloat16),
                        pltpu.VMEM((2, dim, HEAD), jnp.bfloat16), pltpu.VMEM((rows, dim), jnp.bfloat16), half_row, half_row, half_q, half_q,
                        pltpu.SemaphoreType.DMA((3 + HEADS,))],
        compiler_params=pltpu.CompilerParams(vmem_limit_bytes=62 << 20),
        cost_estimate=pl.CostEstimate(flops=2 * rows * dim * 10 * HEAD, bytes_accessed=24 << 20, transcendentals=0),
        name="project",
    )(hidden, w_norm.reshape(dim // 128, 128), w_q, w_k, w_v, cache_len.reshape(rows // 128, 128))


def attend_group(kbuf, vbuf, q, plane, slot_base, store):
    slots = kbuf.shape[1]
    lane = lax.broadcasted_iota(jnp.int32, (slots, 128), 1)
    scores = jnp.zeros((slots, 128), jnp.float32)
    for half in range(2):
        rows = GROUP // 2
        keys = kbuf[pl.ds(half * rows, rows)].reshape(rows * slots, HEAD)
        product = lax.dot_general(keys, q, (((1,), (1,)), ((), ())), preferred_element_type=jnp.float32)
        for i in range(rows):
            b = half * rows + i
            scores = jnp.where(lane // HEADS == b, product[i * slots:(i + 1) * slots], scores)
    position = slot_base + lax.broadcasted_iota(jnp.int32, (slots, 128), 0)
    valid = position <= plane
    scores = jnp.where(valid, scores, LOWEST)
    top = jnp.max(scores, axis=0, keepdims=True)
    weights = jnp.where(valid, jnp.exp(scores - top), 0.0)
    total = jnp.sum(weights, axis=0, keepdims=True)
    by_head = weights.T.astype(jnp.bfloat16)
    for pair in range(GROUP // 2):
        lhs = by_head[pair * 16:(pair + 1) * 16]
        first = jnp.dot(lhs, vbuf[2 * pair], preferred_element_type=jnp.float32)
        second = jnp.dot(lhs, vbuf[2 * pair + 1], preferred_element_type=jnp.float32)
        store(pair, jnp.concatenate([first[:8], second[8:]], axis=0))
    return top, total


def attention_kernel(keep_groups, send_groups, after, chained, scalars, lengths, q, k_new, v_new, k_in, v_in, *rest):
    rest = list(rest[2 * chained + after:])
    k_out, v_out = rest[:2]
    parts = rest[2:2 + (keep_groups > 0) + (send_groups > 0)]
    kbuf, vbuf, qbuf, k_row, v_row, in_sem, out_sem, small_sem = rest[2 + len(parts):]
    starts = [pl.multiple_of(scalars[0], GROUP), pl.multiple_of(scalars[1], GROUP)]
    slot_base = scalars[2]
    depth, _, slots, _ = kbuf.shape
    groups = keep_groups + send_groups
    ahead = (depth + 1) // 2 if groups > depth else groups

    def row_of(g):
        return pl.multiple_of(jnp.where(g < keep_groups, starts[0] + g * GROUP, starts[1] + (g - keep_groups) * GROUP), GROUP)

    def fetch(g):
        slot = lax.rem(g, depth)
        at = pl.ds(row_of(g), GROUP)
        return (pltpu.make_async_copy(k_in.at[at], kbuf.at[slot], in_sem.at[0, slot]),
                pltpu.make_async_copy(v_in.at[at], vbuf.at[slot], in_sem.at[1, slot]))

    def flush(g):
        slot = lax.rem(g, depth)
        at = pl.ds(row_of(g), GROUP)
        return (pltpu.make_async_copy(kbuf.at[slot], k_out.at[at], out_sem.at[0, slot]),
                pltpu.make_async_copy(vbuf.at[slot], v_out.at[at], out_sem.at[1, slot]))

    segments = []
    if keep_groups:
        segments.append((parts[0], 0, keep_groups, starts[0]))
    if send_groups:
        segments.append((parts[-1], keep_groups, send_groups, starts[1]))
    small = []
    for i, (_, first, count, start) in enumerate(segments):
        rows = pl.ds(first * GROUP, count * GROUP)
        small += [
            pltpu.make_async_copy(q.at[pl.ds(pl.multiple_of(start * HEADS, 128), count * 128)], qbuf.at[pl.ds(first * 128, count * 128)], small_sem.at[3 * i]),
            pltpu.make_async_copy(k_new.at[pl.ds(start, count * GROUP)], k_row.at[rows], small_sem.at[3 * i + 1]),
            pltpu.make_async_copy(v_new.at[pl.ds(start, count * GROUP)], v_row.at[rows], small_sem.at[3 * i + 2])]
    for copy in small:
        copy.start()
    for g in range(ahead):
        for copy in fetch(g):
            copy.start()
    for part, _, count, _ in segments:
        part[count * 128:, :] = jnp.zeros((8, HEAD), jnp.float32)
    for copy in small:
        copy.wait()
    row_in_tile = lax.broadcasted_iota(jnp.int32, (16, HEAD), 0)
    lane = lax.broadcasted_iota(jnp.int32, (1, 128), 1) // HEADS
    stat_row = lax.broadcasted_iota(jnp.int32, (8, HEAD), 0)

    def one(part, first, count, g):
        slot = lax.rem(g, depth)
        row0 = row_of(g)
        place = g - first
        for copy in fetch(g):
            copy.wait()
        plane = jnp.zeros((1, 128), jnp.int32)
        for b in range(GROUP):
            length = lengths[row0 + b]
            plane = jnp.where(lane == b, length, plane)
            local = length - slot_base

            @pl.when(jnp.logical_and(local >= 0, local < slots))
            def _():
                tile = pl.multiple_of(local // 16 * 16, 16)
                hit = row_in_tile == local - tile
                for buf, new in ((kbuf, k_row), (vbuf, v_row)):
                    old = buf[slot, b, pl.ds(tile, 16), :].astype(jnp.float32)
                    row = new[pl.ds(g * GROUP + b, 1), :]
                    buf[slot, b, pl.ds(tile, 16), :] = jnp.where(hit, row, old).astype(jnp.bfloat16)

        def store(pair, value):
            part[pl.ds(pl.multiple_of(place * 128, 128) + pair * 16, 16), :] = value

        queries = qbuf[pl.ds(pl.multiple_of(g * 128, 128), 128), :]
        top, total = attend_group(kbuf.at[slot], vbuf.at[slot], queries, plane, slot_base, store)
        part[count * 128:, :] = jnp.where(stat_row == place, jnp.concatenate([top, total], axis=1), part[count * 128:, :])
        for copy in flush(g):
            copy.start()
        if groups > depth:
            @pl.when(g + ahead < groups)
            def _():
                @pl.when(g + ahead >= depth)
                def _():
                    for copy in flush(g + ahead - depth):
                        copy.wait()

                for copy in fetch(g + ahead):
                    copy.start()

    for part, first, count, _ in segments:
        def body(g, carry, part=part, first=first, count=count):
            one(part, first, count, g)
            return carry

        lax.fori_loop(first, first + count, body, 0)
    for g in range(max(groups - depth, 0), groups):
        for copy in flush(g):
            copy.wait()


def attention_call(keep, send, scalars, lengths, q, k_new, v_new, k_block, v_block, outs, after):
    rows = keep + send
    groups = rows // GROUP
    depth = min(groups, 8)
    slots = k_block.shape[1]
    operands = [scalars, lengths, q, k_new, v_new, k_block, v_block, *outs, *after]
    parts = tuple(jax.ShapeDtypeStruct((n * HEADS + 8, HEAD), jnp.float32) for n in (keep, send) if n)
    return pl.pallas_call(
        functools.partial(attention_kernel, keep // GROUP, send // GROUP, len(after), bool(outs)),
        out_shape=(jax.ShapeDtypeStruct(k_block.shape, k_block.dtype), jax.ShapeDtypeStruct(v_block.shape, v_block.dtype), *parts),
        in_specs=[SMEM, SMEM] + [HBM] * (5 + len(outs)) + [ANY] * len(after),
        out_specs=(HBM, HBM) + (VMEM,) * len(parts),
        input_output_aliases={7: 0, 8: 1} if outs else {},
        scratch_shapes=[
            pltpu.VMEM((depth, GROUP, slots, HEAD), jnp.bfloat16),
            pltpu.VMEM((depth, GROUP, slots, HEAD), jnp.bfloat16),
            pltpu.VMEM((rows * HEADS, HEAD), jnp.bfloat16),
            pltpu.VMEM((rows, HEAD), jnp.float32),
            pltpu.VMEM((rows, HEAD), jnp.float32),
            pltpu.SemaphoreType.DMA((2, depth)),
            pltpu.SemaphoreType.DMA((2, depth)),
            pltpu.SemaphoreType.DMA((6,)),
        ],
        compiler_params=pltpu.CompilerParams(vmem_limit_bytes=24 << 20),
        cost_estimate=pl.CostEstimate(flops=rows * 10_000_000, bytes_accessed=rows * 262144, transcendentals=rows * 8 * slots),
    )(*operands)


def merge_scales(one, two, groups, normalize):
    at = pl.ds(groups * 128, 8)
    top_a, top_b = one[at, :128], two[at, :128]
    top = jnp.maximum(top_a, top_b)
    scale_a, scale_b = jnp.exp(top_a - top), jnp.exp(top_b - top)
    total = one[at, 128:] * scale_a + two[at, 128:] * scale_b
    if normalize:
        scale_a, scale_b = scale_a / total, scale_b / total
    stacked = jnp.concatenate([scale_a, scale_b, jnp.zeros((112, 128), jnp.float32)], axis=0)
    return stacked.T, top, total


def merge_kernel(groups, one, two, out):
    columns, top, total = merge_scales(one, two, groups, False)
    for g in range(groups):
        at = pl.ds(g * 128, 128)
        out[at, :] = one[at, :] * columns[:, g:g + 1] + two[at, :] * columns[:, 8 + g:9 + g]
    out[groups * 128:, :128] = top
    out[groups * 128:, 128:] = total


def merge_call(rows, one, two):
    return pl.pallas_call(
        functools.partial(merge_kernel, rows // GROUP),
        out_shape=jax.ShapeDtypeStruct(one.shape, one.dtype),
        in_specs=[VMEM, VMEM],
        out_specs=VMEM,
        compiler_params=pltpu.CompilerParams(vmem_limit_bytes=8 << 20),
        cost_estimate=pl.CostEstimate(flops=rows * 2_000_000, bytes_accessed=rows * 24576, transcendentals=0),
    )(one, two)


def finish_kernel(chunks, late, *refs):
    refs = list(refs)
    row0 = pl.multiple_of(refs.pop(0)[0], GROUP)
    parts = refs[:2 * len(chunks)]
    w_o, hidden = refs[2 * len(chunks):2 * len(chunks) + 2]
    rest = refs[2 * len(chunks) + 2 + late:]
    y, out = rest[:2]
    low, high, attended, x, done, sem = rest[-6:]
    weights = w_o if late else rest[2]
    total = sum(chunks)
    tiles = y.shape[1] // HEAD

    def tile_load(n):
        at = pl.ds(pl.multiple_of(n * HEAD, HEAD), HEAD)
        return pltpu.make_async_copy(w_o.at[:, at], weights.at[:, at], sem.at[2 + n])

    load = pltpu.make_async_copy(hidden.at[pl.ds(row0, total)], x, sem.at[0])
    load.start()
    if not late:
        for n in range(tiles):
            tile_load(n).start()
    first = 0
    for i, rows in enumerate(chunks):
        groups = rows // GROUP
        one, two = parts[2 * i], parts[2 * i + 1]
        columns, _, _ = merge_scales(one, two, groups, True)
        for g in range(groups):
            at = pl.ds(g * 128, 128)
            value = one[at, :] * columns[:, g:g + 1] + two[at, :] * columns[:, 8 + g:9 + g]
            low[at, :] = value[:, :128]
            high[at, :] = value[:, 128:]
        for h in range(HEADS):
            for side, source in enumerate((low, high)):
                column = h * HEAD + side * 128
                attended[first:first + rows, column:column + 128] = source[pl.ds(h, rows, stride=HEADS), :].astype(jnp.bfloat16)
        first += rows
    load.wait()

    @pl.loop(0, tiles)
    def _(n):
        at = pl.ds(pl.multiple_of(n * HEAD, HEAD), HEAD)
        if not late:
            tile_load(n).wait()
        value = jnp.dot(attended[...], weights[:, at], preferred_element_type=jnp.float32)
        y[:, at] = value
        done[:, at] = (x[:, at].astype(jnp.float32) + value).astype(jnp.bfloat16)

    save = pltpu.make_async_copy(done, out.at[pl.ds(row0, total)], sem.at[1])
    save.start()
    save.wait()


def finish_call(chunks, row0, parts, w_o, hidden, out):
    total = sum(chunks)
    dim = w_o.shape[1]
    late = out is not None
    shapes = (jax.ShapeDtypeStruct((total, dim), jnp.float32), jax.ShapeDtypeStruct(hidden.shape, hidden.dtype))
    specs = (VMEM, HBM)
    if not late:
        shapes += (jax.ShapeDtypeStruct(w_o.shape, w_o.dtype),)
        specs += (VMEM,)
    return pl.pallas_call(
        functools.partial(finish_kernel, chunks, late),
        out_shape=shapes,
        in_specs=[SMEM] + [VMEM] * len(parts) + ([VMEM, HBM, HBM] if late else [HBM, HBM]),
        out_specs=specs,
        input_output_aliases={len(parts) + 3: 1} if late else {},
        scratch_shapes=[pltpu.VMEM((max(chunks) * HEADS, 128), jnp.float32), pltpu.VMEM((max(chunks) * HEADS, 128), jnp.float32),
                        pltpu.VMEM((total, w_o.shape[0]), jnp.bfloat16), pltpu.VMEM((total, dim), jnp.bfloat16),
                        pltpu.VMEM((total, dim), jnp.bfloat16), pltpu.SemaphoreType.DMA((2 + dim // HEAD,))],
        compiler_params=pltpu.CompilerParams(vmem_limit_bytes=(24 if late else 40) << 20),
        cost_estimate=pl.CostEstimate(flops=2 * total * w_o.shape[0] * dim, bytes_accessed=10 << 20, transcendentals=0),
    )(row0, *parts, w_o, hidden, *([out] if late else []))


def place_kernel(row, y, hidden, _, out, x, done, sem):
    rows = y.shape[0]
    row0 = pl.multiple_of(row[0], GROUP)
    load = pltpu.make_async_copy(hidden.at[pl.ds(row0, rows)], x, sem.at[0])
    load.start()
    load.wait()

    @pl.loop(0, rows // GROUP)
    def _(i):
        at = pl.ds(pl.multiple_of(i * GROUP, GROUP), GROUP)
        done[at, :] = (x[at, :].astype(jnp.float32) + y[at, :]).astype(jnp.bfloat16)

    save = pltpu.make_async_copy(done, out.at[pl.ds(row0, rows)], sem.at[1])
    save.start()
    save.wait()


def place_call(row0, y, hidden, out):
    rows, dim = y.shape
    return pl.pallas_call(
        place_kernel,
        out_shape=jax.ShapeDtypeStruct(out.shape, out.dtype),
        in_specs=[SMEM, VMEM, HBM, HBM],
        out_specs=HBM,
        input_output_aliases={3: 0},
        scratch_shapes=[pltpu.VMEM((rows, dim), jnp.bfloat16), pltpu.VMEM((rows, dim), jnp.bfloat16), pltpu.SemaphoreType.DMA((2,))],
        compiler_params=pltpu.CompilerParams(vmem_limit_bytes=16 << 20),
        cost_estimate=pl.CostEstimate(flops=rows * 2_000_000, bytes_accessed=rows * 16384, transcendentals=0),
    )(row0, y, hidden, out)


def local_step(hidden, w_norm, w_q, w_k, w_v, w_o, k_block, v_block, cache_len):
    num_rows = hidden.shape[0]
    half = num_rows // 2
    slots = k_block.shape[1]
    me = lax.axis_index('sp')
    core = lax.rem(me, 2)
    sibling = [(0, 1), (1, 0), (2, 3), (3, 2)]
    across = [(0, 2), (2, 0), (1, 3), (3, 1)]
    q, k_new, v_new = project_call(hidden, w_norm, w_q, w_k, w_v, cache_len)
    outs, merged, theirs = (), [], []
    chunks = (0,) + CHUNKS + (0,)
    firsts = [sum(chunks[:i]) for i in range(len(chunks))]
    taken = None
    for i in range(len(chunks) - 1):
        keep, send = chunks[i], chunks[i + 1]
        scalars = jnp.stack([core * half + firsts[i], (1 - core) * half + firsts[i + 1], me * slots]).astype(jnp.int32)
        results = attention_call(keep, send, scalars, cache_len, q, k_new, v_new, k_block, v_block, outs, merged[-1:])
        outs, parts = results[:2], list(results[2:])
        if keep:
            merged.append(merge_call(keep, parts.pop(0), taken))
            theirs.append(lax.ppermute(merged[-1], 'sp', across))
        if send:
            taken = lax.ppermute(parts.pop(0), 'sp', sibling)
    early = [p for pair in list(zip(merged, theirs))[:-1] for p in pair]
    late_first = half - CHUNKS[-1]
    mine, other = core * half, (1 - core) * half
    rows_of = lambda start: jnp.reshape(start, (1,)).astype(jnp.int32)
    y_early, out, w_loaded = finish_call(CHUNKS[:-1], rows_of(mine), early, w_o, hidden, None)
    other_early = lax.ppermute(y_early, 'sp', sibling)
    y_late, out = finish_call(CHUNKS[-1:], rows_of(mine + late_first), [merged[-1], theirs[-1]], w_loaded, hidden, out)
    other_late = lax.ppermute(y_late, 'sp', sibling)
    out = place_call(rows_of(other), other_early, hidden, out)
    out = place_call(rows_of(other + late_first), other_late, hidden, out)
    return out, outs[0], outs[1]


def solution(mesh):
    cache_spec = P('dp', 'sp', None)
    return jax.shard_map(local_step, mesh=mesh, in_specs=(P('dp', None), P(None), P(None, None), P(None, None), P(None, None), P(None, None), cache_spec, cache_spec, P('dp')), out_specs=(P('dp', None), cache_spec, cache_spec), check_vma=False)
```

time: 162 us -> 158 us (0.975)
  Pallas kernels: 84.9 us -> 102 us
  waiting for transfers between devices: 48.3 us -> 35.6 us
  other arithmetic: 5.11 us -> 0.38 us
  starting transfers between devices: 10 us -> 7.19 us
    pallas_call x8 -> x11, Pallas kernels: 80.3 us -> 97.3 us  [the longest x6 64.7 us: attention_call(): pl.pallas_call(functools.partial(attention_kernel, keep // GROUP, send //...]
    ppermute x12, waiting for transfers between devices: 48.3 us -> 35.6 us  [the longest x5 33.8 us: local_step(): theirs.append(lax.ppermute(merged[-1], 'sp', across))]
    convert_element_type x1 -> x0, other arithmetic: 4.8 us -> none  [local_step(): (hidden.astype(jnp.float32) + delta).astype(jnp.bfloat16)]
    ppermute x12, starting transfers between devices: 10 us -> 7.19 us  [the longest x5 5.42 us: local_step(): theirs.append(lax.ppermute(merged[-1], 'sp', across))]
    unnamed x36 -> x42, local copies, waits for them, and re-layouts: 9.54 us -> 10.7 us
  transfers between devices with their start and end apart: 12 -> 12, of which waited for: 4 -> 3; matrix products, arithmetic and copies ran while one was open for 0% -> 0% of each run, Pallas kernels for 36% -> 40%
where the time goes in v1:
time: 158 us; the launch traced here: 157 us
  Pallas kernels  102 us (65%)
  waiting for transfers between devices  35.6 us (23%)
  local copies, waits for them, and re-layouts  10.7 us (7%)
  starting transfers between devices  7.19 us (5%)
    pallas_call x6, Pallas kernels, attention_call(): pl.pallas_call(functools.partial(attention_kernel, keep // GROUP, send //...  64.7 us
    ppermute x5, waiting for transfers between devices, local_step(): theirs.append(lax.ppermute(merged[-1], 'sp', across))  33.8 us
    pallas_call x1, Pallas kernels, project_call(): pl.pallas_call(project_kernel, in_specs=[HBM, VMEM, HBM, HBM, HBM, VMEM],...  15.2 us
    pallas_call x2, Pallas kernels, finish_call(): pl.pallas_call(functools.partial(finish_kernel, chunks, late), out_shape=...  13.7 us
    unnamed x42, local copies, waits for them, and re-layouts  10.7 us
    ppermute x5, starting transfers between devices, local_step(): theirs.append(lax.ppermute(merged[-1], 'sp', across))  5.42 us
    pallas_call x5, Pallas kernels, merge_call(): pl.pallas_call(functools.partial(merge_kernel, rows // GROUP), out_shape=...  4.59 us
    pallas_call x2, Pallas kernels, place_call(): pl.pallas_call(place_kernel, out_shape=jax.ShapeDtypeStruct(out.shape, ou...  3.76 us
  transfers between devices with their start and end apart: 12, of which 3 were waited for; matrix products, arithmetic and copies ran while one was open for 0% of the time, Pallas kernels for 40%

profile of v1, /device:TPU:0, one launch (start us, length us, event | category | flops | bytes accessed | tf_op | source)
XLA Modules:
  0.0 157.0 jit_solution(12743323935848908986)
XLA Ops:
  0.7 15.2 %project.1 = (bf16[4096,256]{1,0:T(8,128)(2,1)}, f32[512,256]{1,0:T(8,128)}, f32[512,256]{1,0:T(8,128)}) custom-call(bf16[512,2048]{1,0:T(8,128)(2,1)} %hidden.5, bf16[16,128]{1,0:T(8,128)(2,1)} %bitcast.15, bf16[2048,2048]{1,0:T(8,128)(2,1)} %w_q.1, bf16[2048,256]{1,0:T(8,128)(2,1)} %w_k.1, bf16[2048,256]{1,0:T(8,128)(2,1)} %w_v.1, s32[4,128]{1,0:T(4,128)} %bitcast.14), custom_call_target="tpu_custom_call" | custom-call | flops 5368709120 | bytes 25165824 | tf_op jit(solution)/shard_map/project/pallas_call | solution.py:90
  15.9 1.6 %copy-done = bf16[4096,256]{1,0:T(8,128)(2,1)S(1)} copy-done((bf16[4096,256]{1,0:T(8,128)(2,1)S(1)}, bf16[4096,256]{1,0:T(8,128)(2,1)}, u32[]{:S(2)}) %copy-start) | copy-done | bytes 2097176
  17.5 1.0 copy-done.4
  18.6 1.0 copy-done.6
  19.6 0.7 copy-done.19
  20.3 4.4 %shard_map.112 = (bf16[512,128,256]{2,1,0:T(8,128)(2,1)}, bf16[512,128,256]{2,1,0:T(8,128)(2,1)}, f32[136,256]{1,0:T(8,128)}) custom-call(s32[3]{0:T(128)S(1)} %get-tuple-element.64.scalars, s32[512]{0:T(512)S(1)} %copy-done.19, bf16[4096,256]{1,0:T(8,128)(2,1)S(1)} %copy-done, f32[512,256]{1,0:T(8,128)S(1)} %copy-done.4, f32[512,256]{1,0:T(8,128)S(1)} %copy-done.6, ...), custom_call_target="tpu_custom_call" | custom-call | flops 160000000 | bytes 4194304 | tf_op jit(solution)/shard_map/pallas_call | solution.py:240
  24.7 8.8 %shard_map.113 = (bf16[512,128,256]{2,1,0:T(8,128)(2,1)}, bf16[512,128,256]{2,1,0:T(8,128)(2,1)}, f32[136,256]{1,0:T(8,128)S(1)}, f32[392,256]{1,0:T(8,128)}) custom-call(s32[3]{0:T(128)S(1)} %get-tuple-element.63.scalars, s32[512]{0:T(512)S(1)} %copy-done.19, bf16[4096,256]{1,0:T(8,128)(2,1)S(1)} %copy-done, ...), custom_call_target="tpu_custom_call", output_to_operand_aliasing={{0}: (7, {}), {1}: (8, {})} | custom-call | flops 640000000 | bytes 16777216 | tf_op jit(solution)/shard_map/pallas_call | solution.py:240
  33.5 0.6 copy-done.17
  34.1 0.7 collective-permute-start.1
  35.0 1.7 %collective-permute-done.two = f32[136,256]{1,0:T(8,128)} collective-permute-done((f32[136,256]{1,0:T(8,128)}, f32[136,256]{1,0:T(8,128)}, u32[]{:S(2)}, u32[]{:S(2)}) %collective-permute-start) | collective-permute-done | bytes 139296 | tf_op jit(solution)/shard_map/ppermute | solution.py:421
  36.7 0.9 copy-done.18
  37.6 1.1 shard_map.114.rest_2_.refs_1_
  38.8 14.7 %shard_map.115 = (bf16[512,128,256]{2,1,0:T(8,128)(2,1)}, bf16[512,128,256]{2,1,0:T(8,128)(2,1)}, f32[392,256]{1,0:T(8,128)S(1)}, f32[648,256]{1,0:T(8,128)}) custom-call(s32[3]{0:T(128)S(1)} %add_add_fusion.3.scalars, s32[512]{0:T(512)S(1)} %copy-done.20, bf16[4096,256]{1,0:T(8,128)(2,1)S(1)} %copy-done.1, ...), custom_call_target="tpu_custom_call", output_to_operand_aliasing={{0}: (7, {}), {1}: (8, {})} | custom-call | flops 1280000000 | bytes 33554432 | tf_op jit(solution)/shard_map/pallas_call | solution.py:240
  53.9 0.8 copy-done.15
  54.6 1.0 copy-done.16
  55.9 17.7 %shard_map.117 = (bf16[512,128,256]{2,1,0:T(8,128)(2,1)}, bf16[512,128,256]{2,1,0:T(8,128)(2,1)}, f32[648,256]{1,0:T(8,128)S(1)}, f32[648,256]{1,0:T(8,128)}) custom-call(s32[3]{0:T(128)S(1)} %add_add_fusion.2.scalars, s32[512]{0:T(512)S(1)} %copy-done.20, bf16[4096,256]{1,0:T(8,128)(2,1)S(1)} %copy-done.1, ...), custom_call_target="tpu_custom_call", output_to_operand_aliasing={{0}: (7, {}), {1}: (8, {})} | custom-call | flops 1600000000 | bytes 41943040 | tf_op jit(solution)/shard_map/pallas_call | solution.py:240
  73.6 0.8 copy-done.13
  74.8 1.1 copy-done.14
  75.9 1.5 shard_map.118.rest_2_.refs_5_
  77.3 2.6 %collective-permute-start.8 = (f32[648,256]{1,0:T(8,128)S(1)}, f32[648,256]{1,0:T(8,128)S(1)}, u32[]{:S(2)}, u32[]{:S(2)}) collective-permute-start(f32[648,256]{1,0:T(8,128)S(1)} %shard_map.118.rest_2_.refs_5_), channel_id=1, source_target_pairs={{0,2},{2,0},{1,3},{3,1},{4,6},{6,4},{5,7},{7,5}} | collective-permute-start | bytes 1990664 | tf_op jit(solution)/shard_map/ppermute | solution.py:419
  79.9 13.2 %shard_map.119 = (bf16[512,128,256]{2,1,0:T(8,128)(2,1)}, bf16[512,128,256]{2,1,0:T(8,128)(2,1)}, f32[648,256]{1,0:T(8,128)S(1)}, f32[264,256]{1,0:T(8,128)}) custom-call(s32[3]{0:T(128)S(1)} %add_add_fusion.1.scalars, s32[512]{0:T(512)S(1)} %copy-done.20, bf16[4096,256]{1,0:T(8,128)(2,1)S(1)} %copy-done.1, ...), custom_call_target="tpu_custom_call", output_to_operand_aliasing={{0}: (7, {}), {1}: (8, {})} | custom-call | flops 1120000000 | bytes 29360128 | tf_op jit(solution)/shard_map/pallas_call | solution.py:240
  93.1 1.5 shard_map.120.rest_2_.refs_7_
  94.7 2.0 %collective-permute-start.7 = (f32[392,256]{1,0:T(8,128)S(1)}, f32[392,256]{1,0:T(8,128)S(1)}, u32[]{:S(2)}, u32[]{:S(2)}) collective-permute-start(f32[392,256]{1,0:T(8,128)S(1)} %shard_map.116.rest_2_.refs_3_), channel_id=1, source_target_pairs={{0,2},{2,0},{1,3},{3,1},{4,6},{6,4},{5,7},{7,5}} | collective-permute-start | bytes 1204232 | tf_op jit(solution)/shard_map/ppermute | solution.py:419
  96.7 26.1 %collective-permute-done.6.refs_2_ = f32[136,256]{1,0:T(8,128)S(1)} collective-permute-done((f32[136,256]{1,0:T(8,128)S(1)}, f32[136,256]{1,0:T(8,128)S(1)}, u32[]{:S(2)}, u32[]{:S(2)}) %collective-permute-start.6) | collective-permute-done | bytes 139296 | tf_op jit(solution)/shard_map/ppermute | solution.py:419
  122.9 10.1 %shard_map.123 = (f32[224,2048]{1,0:T(8,128)}, bf16[512,2048]{1,0:T(8,128)(2,1)}, bf16[2048,2048]{1,0:T(8,128)(2,1)}) custom-call(s32[1]{0:T(128)} %bitcast.11.refs_0_, f32[136,256]{1,0:T(8,128)S(1)} %copy-done.12, f32[136,256]{1,0:T(8,128)S(1)} %collective-permute-done.6.refs_2_, f32[392,256]{1,0:T(8,128)S(1)} %shard_map.116.rest_2_.refs_3_, ...), custom_call_target="tpu_custom_call" | custom-call | flops 1879048192 | bytes 10485760 | tf_op jit(solution)/shard_map/pallas_call | solution.py:354
  133.6 1.1 copy-done.10
  134.7 5.9 %shard_map.121 = (bf16[512,128,256]{2,1,0:T(8,128)(2,1)}, bf16[512,128,256]{2,1,0:T(8,128)(2,1)}, f32[264,256]{1,0:T(8,128)S(1)}) custom-call(s32[3]{0:T(128)S(1)} %add_add_fusion.scalars, s32[512]{0:T(512)S(1)} %copy-done.20, bf16[4096,256]{1,0:T(8,128)(2,1)S(1)} %copy-done.1, ...), custom_call_target="tpu_custom_call", output_to_operand_aliasing={{0}: (7, {}), {1}: (8, {})} | custom-call | flops 320000000 | bytes 8388608 | tf_op jit(solution)/shard_map/pallas_call | solution.py:240
  140.9 0.8 collective-permute-start.5
  141.6 7.7 %collective-permute-done.5.refs_2_ = f32[264,256]{1,0:T(8,128)S(1)} collective-permute-done((f32[264,256]{1,0:T(8,128)S(1)}, f32[264,256]{1,0:T(8,128)S(1)}, u32[]{:S(2)}, u32[]{:S(2)}) %collective-permute-start.5) | collective-permute-done | bytes 270368 | tf_op jit(solution)/shard_map/ppermute | solution.py:419
  149.4 3.6 %shard_map.124 = (f32[32,2048]{1,0:T(8,128)S(1)}, bf16[512,2048]{1,0:T(8,128)(2,1)}) custom-call(s32[1]{0:T(128)} %bitcast.1.refs_0_, f32[264,256]{1,0:T(8,128)S(1)} %shard_map.122.refs_1_, f32[264,256]{1,0:T(8,128)S(1)} %collective-permute-done.5.refs_2_, bf16[2048,2048]{1,0:T(8,128)(2,1)S(1)} %copy-done.8, ...), custom_call_target="tpu_custom_call", output_to_operand_aliasing={{1}: (5, {})} | custom-call | flops 268435456 | bytes 10485760 | tf_op jit(solution)/shard_map/pallas_call | solution.py:354
  153.0 2.9 %shard_map.125._ = bf16[512,2048]{1,0:T(8,128)(2,1)} custom-call(s32[1]{0:T(128)} %bitcast.13.row, f32[224,2048]{1,0:T(8,128)} %collective-permute-done.11.y, bf16[512,2048]{1,0:T(8,128)(2,1)S(1)} %copy-done.3, bf16[512,2048]{1,0:T(8,128)(2,1)} %get-tuple-element.60._), custom_call_target="tpu_custom_call", output_to_operand_aliasing={{}: (3, {})} | custom-call | flops 448000000 | bytes 3670016 | tf_op jit(solution)/shard_map/pallas_call | solution.py:387
  155.9 0.9 shard_map.126
  (55 shorter events, 2.2 us)
Async XLA Ops:
  15.9 1.6 %copy-start = (bf16[4096,256]{1,0:T(8,128)(2,1)S(1)}, bf16[4096,256]{1,0:T(8,128)(2,1)}, u32[]{:S(2)}) copy-start(bf16[4096,256]{1,0:T(8,128)(2,1)} %get-tuple-element.33.q) | copy-start | bytes 6291460
  17.5 1.0 copy-start.4
  18.5 1.0 copy-start.6
  19.6 0.7 copy-start.19
  24.7 14.1 %copy-start.1 = (bf16[4096,256]{1,0:T(8,128)(2,1)S(1)}, bf16[4096,256]{1,0:T(8,128)(2,1)}, u32[]{:S(2)}) copy-start(bf16[4096,256]{1,0:T(8,128)(2,1)} %get-tuple-element.33.q) | copy-start | bytes 6291460
  24.7 14.1 %copy-start.5 = (f32[512,256]{1,0:T(8,128)S(1)}, f32[512,256]{1,0:T(8,128)}, u32[]{:S(2)}) copy-start(f32[512,256]{1,0:T(8,128)} %get-tuple-element.34.k_new) | copy-start | bytes 1572868
  24.7 14.1 %copy-start.7 = (f32[512,256]{1,0:T(8,128)S(1)}, f32[512,256]{1,0:T(8,128)}, u32[]{:S(2)}) copy-start(f32[512,256]{1,0:T(8,128)} %get-tuple-element.35.v_new) | copy-start | bytes 1572868
  24.7 14.1 %copy-start.20 = (s32[512]{0:T(512)S(1)}, s32[512]{0:T(512)}, u32[]{:S(2)}) copy-start(s32[512]{0:T(512)} %lengths.11) | copy-start | bytes 6148
  34.1 19.7 %collective-permute-start.1 = (f32[392,256]{1,0:T(8,128)}, f32[392,256]{1,0:T(8,128)S(1)}, u32[]{:S(2)}, u32[]{:S(2)}) collective-permute-start(f32[392,256]{1,0:T(8,128)} %get-tuple-element.45), channel_id=1, source_target_pairs={{0,1},{1,0},{2,3},{3,2},{4,5},{5,4},{6,7},{7,6}} | collective-permute-start | bytes 1204232 | tf_op jit(solution)/shard_map/ppermute | solution.py:421
  34.8 1.9 %collective-permute-start = (f32[136,256]{1,0:T(8,128)}, f32[136,256]{1,0:T(8,128)}, u32[]{:S(2)}, u32[]{:S(2)}) collective-permute-start(f32[136,256]{1,0:T(8,128)} %get-tuple-element.41), channel_id=1, source_target_pairs={{0,1},{1,0},{2,3},{3,2},{4,5},{5,4},{6,7},{7,6}} | collective-permute-start | bytes 417800 | tf_op jit(solution)/shard_map/ppermute | solution.py:421
  36.7 0.9 copy-start.18
  38.7 14.8 %copy-start.11 = (f32[136,256]{1,0:T(8,128)}, f32[136,256]{1,0:T(8,128)S(1)}, u32[]{:S(2)}) copy-start(f32[136,256]{1,0:T(8,128)S(1)} %shard_map.114.rest_2_.refs_1_) | copy-start | bytes 417796
  53.5 21.2 %collective-permute-start.2 = (f32[648,256]{1,0:T(8,128)}, f32[648,256]{1,0:T(8,128)}, u32[]{:S(2)}, u32[]{:S(2)}) collective-permute-start(f32[648,256]{1,0:T(8,128)} %get-tuple-element.49), channel_id=1, source_target_pairs={{0,1},{1,0},{2,3},{3,2},{4,5},{5,4},{6,7},{7,6}} | collective-permute-start | bytes 1990664 | tf_op jit(solution)/shard_map/ppermute | solution.py:421
  53.8 0.8 copy-start.15
  54.6 1.0 copy-start.16
  73.6 0.8 copy-start.13
  74.4 18.7 %collective-permute-start.3 = (f32[648,256]{1,0:T(8,128)}, f32[648,256]{1,0:T(8,128)}, u32[]{:S(2)}, u32[]{:S(2)}) collective-permute-start(f32[648,256]{1,0:T(8,128)} %get-tuple-element.53), channel_id=1, source_target_pairs={{0,1},{1,0},{2,3},{3,2},{4,5},{5,4},{6,7},{7,6}} | collective-permute-start | bytes 1990664 | tf_op jit(solution)/shard_map/ppermute | solution.py:421
  74.8 1.1 copy-start.14
  77.3 45.5 %collective-permute-start.8 = (f32[648,256]{1,0:T(8,128)S(1)}, f32[648,256]{1,0:T(8,128)S(1)}, u32[]{:S(2)}, u32[]{:S(2)}) collective-permute-start(f32[648,256]{1,0:T(8,128)S(1)} %shard_map.118.rest_2_.refs_5_), channel_id=1, source_target_pairs={{0,2},{2,0},{1,3},{3,1},{4,6},{6,4},{5,7},{7,5}} | collective-permute-start | bytes 1990664 | tf_op jit(solution)/shard_map/ppermute | solution.py:419
  79.9 16.8 %copy-start.12 = (f32[136,256]{1,0:T(8,128)S(1)}, f32[136,256]{1,0:T(8,128)}, u32[]{:S(2)}) copy-start(f32[136,256]{1,0:T(8,128)} %copy-done.11) | copy-start | bytes 417796
  79.9 42.9 %copy-start.2 = (bf16[512,2048]{1,0:T(8,128)(2,1)S(1)}, bf16[512,2048]{1,0:T(8,128)(2,1)}, u32[]{:S(2)}) copy-start(bf16[512,2048]{1,0:T(8,128)(2,1)} %hidden.5) | copy-start | bytes 6291460
  94.6 38.4 %copy-start.9 = (f32[648,256]{1,0:T(8,128)}, f32[648,256]{1,0:T(8,128)S(1)}, u32[]{:S(2)}) copy-start(f32[648,256]{1,0:T(8,128)S(1)} %shard_map.120.rest_2_.refs_7_) | copy-start | bytes 1990660
  94.6 28.2 %collective-permute-start.9 = (f32[648,256]{1,0:T(8,128)S(1)}, f32[648,256]{1,0:T(8,128)S(1)}, u32[]{:S(2)}, u32[]{:S(2)}) collective-permute-start(f32[648,256]{1,0:T(8,128)S(1)} %shard_map.120.rest_2_.refs_7_), channel_id=1, source_target_pairs={{0,2},{2,0},{1,3},{3,1},{4,6},{6,4},{5,7},{7,5}} | collective-permute-start | bytes 1990664 | tf_op jit(solution)/shard_map/ppermute | solution.py:419
  94.7 28.2 %collective-permute-start.7 = (f32[392,256]{1,0:T(8,128)S(1)}, f32[392,256]{1,0:T(8,128)S(1)}, u32[]{:S(2)}, u32[]{:S(2)}) collective-permute-start(f32[392,256]{1,0:T(8,128)S(1)} %shard_map.116.rest_2_.refs_3_), channel_id=1, source_target_pairs={{0,2},{2,0},{1,3},{3,1},{4,6},{6,4},{5,7},{7,5}} | collective-permute-start | bytes 1204232 | tf_op jit(solution)/shard_map/ppermute | solution.py:419
  96.7 26.2 %collective-permute-start.6 = (f32[136,256]{1,0:T(8,128)S(1)}, f32[136,256]{1,0:T(8,128)S(1)}, u32[]{:S(2)}, u32[]{:S(2)}) collective-permute-start(f32[136,256]{1,0:T(8,128)S(1)} %copy-done.12), channel_id=1, source_target_pairs={{0,2},{2,0},{1,3},{3,1},{4,6},{6,4},{5,7},{7,5}} | collective-permute-start | bytes 417800 | tf_op jit(solution)/shard_map/ppermute | solution.py:419
  133.0 20.0 %collective-permute-start.11 = (f32[224,2048]{1,0:T(8,128)}, f32[224,2048]{1,0:T(8,128)}, u32[]{:S(2)}, u32[]{:S(2)}) collective-permute-start(f32[224,2048]{1,0:T(8,128)} %get-tuple-element.59), channel_id=1, source_target_pairs={{0,1},{1,0},{2,3},{3,2},{4,5},{5,4},{6,7},{7,6}} | collective-permute-start | bytes 5505032 | tf_op jit(solution)/shard_map/ppermute | solution.py:427
  133.1 7.5 %collective-permute-start.4 = (f32[264,256]{1,0:T(8,128)}, f32[264,256]{1,0:T(8,128)S(1)}, u32[]{:S(2)}, u32[]{:S(2)}) collective-permute-start(f32[264,256]{1,0:T(8,128)} %get-tuple-element.55), channel_id=1, source_target_pairs={{0,1},{1,0},{2,3},{3,2},{4,5},{5,4},{6,7},{7,6}} | collective-permute-start | bytes 811016 | tf_op jit(solution)/shard_map/ppermute | solution.py:421
  133.6 1.1 copy-start.10
  134.7 14.6 %copy-start.3 = (bf16[512,2048]{1,0:T(8,128)(2,1)S(1)}, bf16[512,2048]{1,0:T(8,128)(2,1)}, u32[]{:S(2)}) copy-start(bf16[512,2048]{1,0:T(8,128)(2,1)} %hidden.5) | copy-start | bytes 6291460
  134.7 14.6 %copy-start.8 = (bf16[2048,2048]{1,0:T(8,128)(2,1)S(1)}, bf16[2048,2048]{1,0:T(8,128)(2,1)}, u32[]{:S(2)}) copy-start(bf16[2048,2048]{1,0:T(8,128)(2,1)} %get-tuple-element.56.refs_3_) | copy-start | bytes 25165828
  140.9 8.5 %collective-permute-start.5 = (f32[264,256]{1,0:T(8,128)S(1)}, f32[264,256]{1,0:T(8,128)S(1)}, u32[]{:S(2)}, u32[]{:S(2)}) collective-permute-start(f32[264,256]{1,0:T(8,128)S(1)} %shard_map.122.refs_1_), channel_id=1, source_target_pairs={{0,2},{2,0},{1,3},{3,1},{4,6},{6,4},{5,7},{7,5}} | collective-permute-start | bytes 811016 | tf_op jit(solution)/shard_map/ppermute | solution.py:419
  153.0 2.9 %collective-permute-start.10 = (f32[32,2048]{1,0:T(8,128)S(1)}, f32[32,2048]{1,0:T(8,128)S(1)}, u32[]{:S(2)}, u32[]{:S(2)}) collective-permute-start(f32[32,2048]{1,0:T(8,128)S(1)} %get-tuple-element.58), channel_id=1, source_target_pairs={{0,1},{1,0},{2,3},{3,2},{4,5},{5,4},{6,7},{7,6}} | collective-permute-start | bytes 786440 | tf_op jit(solution)/shard_map/ppermute | solution.py:429
  (1 other events, 0.7 us)

commit v2 on v1

--- a/solution.py
+++ b/solution.py
@@ -14,7 +14,7 @@
 HEAD = 256
 GROUP = 16
 LOWEST = float(jnp.finfo(jnp.float32).min)
-CHUNKS = (16, 48, 80, 80, 32)
+CHUNKS = (64, 80, 80, 32)
 HBM = pl.BlockSpec(memory_space=pltpu.HBM)
 ANY = pl.BlockSpec(memory_space=pl.ANY)
 VMEM = pl.BlockSpec(memory_space=pltpu.VMEM)
@@ -28,7 +28,7 @@
              + [pltpu.make_async_copy(w_q.at[:, h * HEAD:(h + 1) * HEAD], wide.at[h], sem.at[2 + h]) for h in range(HEADS)])
     first = pltpu.make_async_copy(hidden, x, sem.at[2 + HEADS])
     first.start()
-    for copy in tiles:
+    for copy in tiles[:2]:
         copy.start()
     count = lengths.shape[0]
     positions = jnp.concatenate([lengths[...], jnp.zeros((8 - count, 128), jnp.int32)], axis=0).astype(jnp.float32).T
@@ -41,6 +41,8 @@
     gain = 1.0 + w_norm[...].astype(jnp.float32)
     gain = jnp.concatenate([gain[i:i + 1] for i in range(w_norm.shape[0])], axis=1)
     first.wait()
+    for copy in tiles[2:]:
+        copy.start()
 
     def norm(i, carry):
         at = pl.ds(pl.multiple_of(i * 32, 32), 32)
@@ -137,7 +139,7 @@
     slot_base = scalars[2]
     depth, _, slots, _ = kbuf.shape
     groups = keep_groups + send_groups
-    ahead = (depth + 1) // 2 if groups > depth else groups
+    ahead = min(3, groups)
 
     def row_of(g):
         return pl.multiple_of(jnp.where(g < keep_groups, starts[0] + g * GROUP, starts[1] + (g - keep_groups) * GROUP), GROUP)
@@ -208,7 +210,7 @@
         part[count * 128:, :] = jnp.where(stat_row == place, jnp.concatenate([top, total], axis=1), part[count * 128:, :])
         for copy in flush(g):
             copy.start()
-        if groups > depth:
+        if groups > ahead:
             @pl.when(g + ahead < groups)
             def _():
                 @pl.when(g + ahead >= depth)
@@ -233,7 +235,7 @@
 def attention_call(keep, send, scalars, lengths, q, k_new, v_new, k_block, v_block, outs, after):
     rows = keep + send
     groups = rows // GROUP
-    depth = min(groups, 8)
+    depth = min(groups, 7)
     slots = k_block.shape[1]
     operands = [scalars, lengths, q, k_new, v_new, k_block, v_block, *outs, *after]
     parts = tuple(jax.ShapeDtypeStruct((n * HEADS + 8, HEAD), jnp.float32) for n in (keep, send) if n)
@@ -253,7 +255,7 @@
             pltpu.SemaphoreType.DMA((2, depth)),
             pltpu.SemaphoreType.DMA((6,)),
         ],
-        compiler_params=pltpu.CompilerParams(vmem_limit_bytes=24 << 20),
+        compiler_params=pltpu.CompilerParams(vmem_limit_bytes=62 << 20),
         cost_estimate=pl.CostEstimate(flops=rows * 10_000_000, bytes_accessed=rows * 262144, transcendentals=rows * 8 * slots),
     )(*operands)
 
@@ -297,20 +299,18 @@
     w_o, hidden = refs[2 * len(chunks):2 * len(chunks) + 2]
     rest = refs[2 * len(chunks) + 2 + late:]
     y, out = rest[:2]
-    low, high, attended, x, done, sem = rest[-6:]
-    weights = w_o if late else rest[2]
+    weights, low, high, attended, x, done, sem = rest[-7:]
     total = sum(chunks)
     tiles = y.shape[1] // HEAD
 
     def tile_load(n):
         at = pl.ds(pl.multiple_of(n * HEAD, HEAD), HEAD)
-        return pltpu.make_async_copy(w_o.at[:, at], weights.at[:, at], sem.at[2 + n])
+        return pltpu.make_async_copy(w_o.at[:, at], weights.at[n], sem.at[2 + n])
 
     load = pltpu.make_async_copy(hidden.at[pl.ds(row0, total)], x, sem.at[0])
     load.start()
-    if not late:
-        for n in range(tiles):
-            tile_load(n).start()
+    for n in range(3):
+        tile_load(n).start()
     first = 0
     for i, rows in enumerate(chunks):
         groups = rows // GROUP
@@ -331,9 +331,13 @@
     @pl.loop(0, tiles)
     def _(n):
         at = pl.ds(pl.multiple_of(n * HEAD, HEAD), HEAD)
-        if not late:
-            tile_load(n).wait()
-        value = jnp.dot(attended[...], weights[:, at], preferred_element_type=jnp.float32)
+        tile_load(n).wait()
+
+        @pl.when(n + 3 < tiles)
+        def _():
+            tile_load(n + 3).start()
+
+        value = jnp.dot(attended[...], weights[n], preferred_element_type=jnp.float32)
         y[:, at] = value
         done[:, at] = (x[:, at].astype(jnp.float32) + value).astype(jnp.bfloat16)
 
@@ -348,19 +352,16 @@
     late = out is not None
     shapes = (jax.ShapeDtypeStruct((total, dim), jnp.float32), jax.ShapeDtypeStruct(hidden.shape, hidden.dtype))
     specs = (VMEM, HBM)
-    if not late:
-        shapes += (jax.ShapeDtypeStruct(w_o.shape, w_o.dtype),)
-        specs += (VMEM,)
     return pl.pallas_call(
         functools.partial(finish_kernel, chunks, late),
         out_shape=shapes,
-        in_specs=[SMEM] + [VMEM] * len(parts) + ([VMEM, HBM, HBM] if late else [HBM, HBM]),
+        in_specs=[SMEM] + [VMEM] * len(parts) + [HBM, HBM] + [HBM] * late,
         out_specs=specs,
         input_output_aliases={len(parts) + 3: 1} if late else {},
-        scratch_shapes=[pltpu.VMEM((max(chunks) * HEADS, 128), jnp.float32), pltpu.VMEM((max(chunks) * HEADS, 128), jnp.float32),
+        scratch_shapes=[pltpu.VMEM((dim // HEAD, w_o.shape[0], HEAD), jnp.bfloat16), pltpu.VMEM((max(chunks) * HEADS, 128), jnp.float32), pltpu.VMEM((max(chunks) * HEADS, 128), jnp.float32),
                         pltpu.VMEM((total, w_o.shape[0]), jnp.bfloat16), pltpu.VMEM((total, dim), jnp.bfloat16),
                         pltpu.VMEM((total, dim), jnp.bfloat16), pltpu.SemaphoreType.DMA((2 + dim // HEAD,))],
-        compiler_params=pltpu.CompilerParams(vmem_limit_bytes=(24 if late else 40) << 20),
+        compiler_params=pltpu.CompilerParams(vmem_limit_bytes=26 << 20),
         cost_estimate=pl.CostEstimate(flops=2 * total * w_o.shape[0] * dim, bytes_accessed=10 << 20, transcendentals=0),
     )(row0, *parts, w_o, hidden, *([out] if late else []))
 
@@ -391,7 +392,7 @@
         out_specs=HBM,
         input_output_aliases={3: 0},
         scratch_shapes=[pltpu.VMEM((rows, dim), jnp.bfloat16), pltpu.VMEM((rows, dim), jnp.bfloat16), pltpu.SemaphoreType.DMA((2,))],
-        compiler_params=pltpu.CompilerParams(vmem_limit_bytes=16 << 20),
+        compiler_params=pltpu.CompilerParams(vmem_limit_bytes=12 << 20),
         cost_estimate=pl.CostEstimate(flops=rows * 2_000_000, bytes_accessed=rows * 16384, transcendentals=0),
     )(row0, y, hidden, out)
 
@@ -406,26 +407,21 @@
     across = [(0, 2), (2, 0), (1, 3), (3, 1)]
     q, k_new, v_new = project_call(hidden, w_norm, w_q, w_k, w_v, cache_len)
     outs, merged, theirs = (), [], []
-    chunks = (0,) + CHUNKS + (0,)
-    firsts = [sum(chunks[:i]) for i in range(len(chunks))]
-    taken = None
-    for i in range(len(chunks) - 1):
-        keep, send = chunks[i], chunks[i + 1]
-        scalars = jnp.stack([core * half + firsts[i], (1 - core) * half + firsts[i + 1], me * slots]).astype(jnp.int32)
-        results = attention_call(keep, send, scalars, cache_len, q, k_new, v_new, k_block, v_block, outs, merged[-1:])
-        outs, parts = results[:2], list(results[2:])
-        if keep:
-            merged.append(merge_call(keep, parts.pop(0), taken))
-            theirs.append(lax.ppermute(merged[-1], 'sp', across))
-        if send:
-            taken = lax.ppermute(parts.pop(0), 'sp', sibling)
+    first = 0
+    for rows in CHUNKS:
+        scalars = jnp.stack([core * half + first, (1 - core) * half + first, me * slots]).astype(jnp.int32)
+        *outs, kept, sent = attention_call(rows, rows, scalars, cache_len, q, k_new, v_new, k_block, v_block, outs, merged[-1:])
+        taken = lax.ppermute(sent, 'sp', sibling)
+        merged.append(merge_call(rows, kept, taken))
+        theirs.append(lax.ppermute(merged[-1], 'sp', across))
+        first += rows
     early = [p for pair in list(zip(merged, theirs))[:-1] for p in pair]
     late_first = half - CHUNKS[-1]
     mine, other = core * half, (1 - core) * half
     rows_of = lambda start: jnp.reshape(start, (1,)).astype(jnp.int32)
-    y_early, out, w_loaded = finish_call(CHUNKS[:-1], rows_of(mine), early, w_o, hidden, None)
+    y_early, out = finish_call(CHUNKS[:-1], rows_of(mine), early, w_o, hidden, None)
     other_early = lax.ppermute(y_early, 'sp', sibling)
-    y_late, out = finish_call(CHUNKS[-1:], rows_of(mine + late_first), [merged[-1], theirs[-1]], w_loaded, hidden, out)
+    y_late, out = finish_call(CHUNKS[-1:], rows_of(mine + late_first), [merged[-1], theirs[-1]], w_o, hidden, out)
     other_late = lax.ppermute(y_late, 'sp', sibling)
     out = place_call(rows_of(other), other_early, hidden, out)
     out = place_call(rows_of(other + late_first), other_late, hidden, out)

time: 158 us -> 173 us (1.095)
  waiting for transfers between devices: 35.6 us -> 48.5 us
  Pallas kernels: 102 us -> 96.8 us
  local copies, waits for them, and re-layouts: 10.7 us -> 15.8 us
  other arithmetic: 0.38 us -> 2.26 us
    ppermute x5 -> x4, waiting for transfers between devices: 33.8 us -> 44.4 us  [local_step(): theirs.append(lax.ppermute(merged[-1], 'sp', across))]
    unnamed x42 -> x26, local copies, waits for them, and re-layouts: 10.7 us -> 15.8 us
    pallas_call x5 -> x4, Pallas kernels: 4.59 us -> 1.32 us  [merge_call(): pl.pallas_call(functools.partial(merge_kernel, rows // GROUP), out_shape=...]
    ppermute x5 -> x4, waiting for transfers between devices: 1.76 us -> 4.09 us  [local_step(): taken = lax.ppermute(sent, 'sp', sibling)]
    another operation x5 -> x4, other arithmetic: 0.38 us -> 2.26 us  [local_step(): jnp.stack([core * half + first, (1 - core) * half + first, me * slots])]
    ppermute x5 -> x4, starting transfers between devices: 5.42 us -> 6.58 us  [local_step(): theirs.append(lax.ppermute(merged[-1], 'sp', across))]
    pallas_call x6 -> x4, Pallas kernels: 64.7 us -> 63.9 us  [attention_call(): pl.pallas_call(functools.partial(attention_kernel, keep // GROUP, send //...]
  transfers between devices with their start and end apart: 12 -> 10, of which waited for: 3 -> 5; matrix products, arithmetic and copies ran while one was open for 0% -> 1% of each run, Pallas kernels for 40% -> 11%
where the time goes in v2:
time: 173 us
  Pallas kernels  96.8 us (56%)
  waiting for transfers between devices  48.5 us (28%)
  local copies, waits for them, and re-layouts  15.8 us (9%)
  starting transfers between devices  8.64 us (5%)
  other arithmetic  2.26 us (1%)
    pallas_call x4, Pallas kernels, attention_call(): pl.pallas_call(functools.partial(attention_kernel, keep // GROUP, send //...  63.9 us
    ppermute x4, waiting for transfers between devices, local_step(): theirs.append(lax.ppermute(merged[-1], 'sp', across))  44.4 us
    unnamed x26, local copies, waits for them, and re-layouts  15.8 us
    pallas_call x1, Pallas kernels, project_call(): pl.pallas_call(project_kernel, in_specs=[HBM, VMEM, HBM, HBM, HBM, VMEM],...  15.2 us
    pallas_call x2, Pallas kernels, finish_call(): pl.pallas_call(functools.partial(finish_kernel, chunks, late), out_shape=...  12.7 us
    ppermute x4, starting transfers between devices, local_step(): theirs.append(lax.ppermute(merged[-1], 'sp', across))  6.58 us
    ppermute x4, waiting for transfers between devices, local_step(): taken = lax.ppermute(sent, 'sp', sibling)  4.09 us
    pallas_call x2, Pallas kernels, place_call(): pl.pallas_call(place_kernel, out_shape=jax.ShapeDtypeStruct(out.shape, ou...  3.76 us
  transfers between devices with their start and end apart: 10, of which 5 were waited for; matrix products, arithmetic and copies ran while one was open for 1% of the time, Pallas kernels for 11%

profile of v2, /device:TPU:0, one launch (start us, length us, event | category | flops | bytes accessed | tf_op | source)
XLA Modules:
  0.0 172.8 jit_solution(14666648327034677713)
XLA Ops:
  0.6 0.6 add_add_fusion.3.scalars
  1.2 15.2 %project.1 = (bf16[4096,256]{1,0:T(8,128)(2,1)}, f32[512,256]{1,0:T(8,128)}, f32[512,256]{1,0:T(8,128)}) custom-call(bf16[512,2048]{1,0:T(8,128)(2,1)} %hidden.5, bf16[16,128]{1,0:T(8,128)(2,1)} %bitcast.12, bf16[2048,2048]{1,0:T(8,128)(2,1)} %w_q.1, bf16[2048,256]{1,0:T(8,128)(2,1)} %w_k.1, bf16[2048,256]{1,0:T(8,128)(2,1)} %w_v.1, s32[4,128]{1,0:T(4,128)} %bitcast.11), custom_call_target="tpu_custom_call" | custom-call | flops 5368709120 | bytes 25165824 | tf_op jit(solution)/shard_map/project/pallas_call | solution.py:92
  16.4 15.6 %shard_map.112 = (bf16[512,128,256]{2,1,0:T(8,128)(2,1)}, bf16[512,128,256]{2,1,0:T(8,128)(2,1)}, f32[520,256]{1,0:T(8,128)}, f32[520,256]{1,0:T(8,128)}) custom-call(s32[3]{0:T(128)} %add_add_fusion.3.scalars, s32[512]{0:T(512)} %lengths.7, bf16[4096,256]{1,0:T(8,128)(2,1)} %get-tuple-element.26.q, f32[512,256]{1,0:T(8,128)} %get-tuple-element.27.k_new, ...), custom_call_target="tpu_custom_call" | custom-call | flops 1280000000 | bytes 33554432 | tf_op jit(solution)/shard_map/pallas_call | solution.py:242
  31.9 1.0 collective-permute-start
  32.9 0.6 add_add_fusion.2.scalars
  33.5 1.2 collective-permute-done.two
  34.7 1.0 copy-done.11
  36.1 0.8 copy-done.7
  36.9 18.9 %shard_map.114 = (bf16[512,128,256]{2,1,0:T(8,128)(2,1)}, bf16[512,128,256]{2,1,0:T(8,128)(2,1)}, f32[648,256]{1,0:T(8,128)}, f32[648,256]{1,0:T(8,128)}) custom-call(s32[3]{0:T(128)} %add_add_fusion.2.scalars, s32[512]{0:T(512)} %lengths.7, bf16[4096,256]{1,0:T(8,128)(2,1)} %get-tuple-element.26.q, ...), custom_call_target="tpu_custom_call", output_to_operand_aliasing={{0}: (7, {}), {1}: (8, {})} | custom-call | flops 1600000000 | bytes 41943040 | tf_op jit(solution)/shard_map/pallas_call | solution.py:242
  56.1 0.6 add_add_fusion.1.scalars
  56.6 1.5 collective-permute-done.1.two
  58.1 1.1 copy-done.9
  59.6 0.8 copy-done.5
  60.5 19.0 %shard_map.116 = (bf16[512,128,256]{2,1,0:T(8,128)(2,1)}, bf16[512,128,256]{2,1,0:T(8,128)(2,1)}, f32[648,256]{1,0:T(8,128)}, f32[648,256]{1,0:T(8,128)}) custom-call(s32[3]{0:T(128)} %add_add_fusion.1.scalars, s32[512]{0:T(512)} %lengths.7, bf16[4096,256]{1,0:T(8,128)(2,1)} %get-tuple-element.26.q, ...), custom_call_target="tpu_custom_call", output_to_operand_aliasing={{0}: (7, {}), {1}: (8, {})} | custom-call | flops 1600000000 | bytes 41943040 | tf_op jit(solution)/shard_map/pallas_call | solution.py:242
  79.6 2.6 %collective-permute-start.6 = (f32[648,256]{1,0:T(8,128)S(1)}, f32[648,256]{1,0:T(8,128)S(1)}, u32[]{:S(2)}, u32[]{:S(2)}) collective-permute-start(f32[648,256]{1,0:T(8,128)S(1)} %copy-done.6), channel_id=1, source_target_pairs={{0,2},{2,0},{1,3},{3,1},{4,6},{6,4},{5,7},{7,5}} | collective-permute-start | bytes 1990664 | tf_op jit(solution)/shard_map/ppermute | solution.py:416
  82.2 1.1 copy-done.10
  83.7 2.2 %collective-permute-start.7 = (f32[648,256]{1,0:T(8,128)S(1)}, f32[648,256]{1,0:T(8,128)S(1)}, u32[]{:S(2)}, u32[]{:S(2)}) collective-permute-start(f32[648,256]{1,0:T(8,128)S(1)} %shard_map.117.rest_2_.refs_5_), channel_id=1, source_target_pairs={{0,2},{2,0},{1,3},{3,1},{4,6},{6,4},{5,7},{7,5}} | collective-permute-start | bytes 1990664 | tf_op jit(solution)/shard_map/ppermute | solution.py:416
  85.9 37.4 %collective-permute-done.5.refs_2_ = f32[520,256]{1,0:T(8,128)S(1)} collective-permute-done((f32[520,256]{1,0:T(8,128)S(1)}, f32[520,256]{1,0:T(8,128)S(1)}, u32[]{:S(2)}, u32[]{:S(2)}) %collective-permute-start.5) | collective-permute-done | bytes 532512 | tf_op jit(solution)/shard_map/ppermute | solution.py:416
  123.3 3.4 %copy-done = bf16[2048,2048]{1,0:T(8,128)(2,1)S(1)} copy-done((bf16[2048,2048]{1,0:T(8,128)(2,1)S(1)}, bf16[2048,2048]{1,0:T(8,128)(2,1)}, u32[]{:S(2)}) %copy-start) | copy-done | bytes 8388632
  126.7 1.6 copy-done.2
  128.2 8.0 %shard_map.120 = (f32[224,2048]{1,0:T(8,128)}, bf16[512,2048]{1,0:T(8,128)(2,1)}) custom-call(s32[1]{0:T(128)} %bitcast.9.refs_0_, f32[520,256]{1,0:T(8,128)S(1)} %copy-done.8, f32[520,256]{1,0:T(8,128)S(1)} %collective-permute-done.5.refs_2_, f32[648,256]{1,0:T(8,128)S(1)} %copy-done.6, f32[648,256]{1,0:T(8,128)S(1)} %collective-permute-done.6.refs_4_, ...), custom_call_target="tpu_custom_call" | custom-call | flops 1879048192 | bytes 10485760 | tf_op jit(solution)/shard_map/pallas_call | solution.py:355
  136.3 0.6 add_add_fusion.scalars
  136.9 10.4 %shard_map.118 = (bf16[512,128,256]{2,1,0:T(8,128)(2,1)}, bf16[512,128,256]{2,1,0:T(8,128)(2,1)}, f32[264,256]{1,0:T(8,128)}, f32[264,256]{1,0:T(8,128)}) custom-call(s32[3]{0:T(128)} %add_add_fusion.scalars, s32[512]{0:T(512)} %lengths.7, bf16[4096,256]{1,0:T(8,128)(2,1)} %get-tuple-element.26.q, ...), custom_call_target="tpu_custom_call", output_to_operand_aliasing={{0}: (7, {}), {1}: (8, {})} | custom-call | flops 640000000 | bytes 16777216 | tf_op jit(solution)/shard_map/pallas_call | solution.py:242
  147.8 1.4 collective-permute-done.3.two
  149.2 1.0 copy-done.12
  150.4 1.8 %collective-permute-start.4 = (f32[264,256]{1,0:T(8,128)S(1)}, f32[264,256]{1,0:T(8,128)S(1)}, u32[]{:S(2)}, u32[]{:S(2)}) collective-permute-start(f32[264,256]{1,0:T(8,128)S(1)} %shard_map.119.refs_1_), channel_id=1, source_target_pairs={{0,2},{2,0},{1,3},{3,1},{4,6},{6,4},{5,7},{7,5}} | collective-permute-start | bytes 811016 | tf_op jit(solution)/shard_map/ppermute | solution.py:416
  152.2 7.0 %collective-permute-done.4.refs_2_ = f32[264,256]{1,0:T(8,128)S(1)} collective-permute-done((f32[264,256]{1,0:T(8,128)S(1)}, f32[264,256]{1,0:T(8,128)S(1)}, u32[]{:S(2)}, u32[]{:S(2)}) %collective-permute-start.4) | collective-permute-done | bytes 270368 | tf_op jit(solution)/shard_map/ppermute | solution.py:416
  159.2 3.4 %copy-done.1 = bf16[2048,2048]{1,0:T(8,128)(2,1)S(1)} copy-done((bf16[2048,2048]{1,0:T(8,128)(2,1)S(1)}, bf16[2048,2048]{1,0:T(8,128)(2,1)}, u32[]{:S(2)}) %copy-start.1) | copy-done | bytes 8388632
  162.6 1.6 copy-done.3
  164.2 4.7 %shard_map.121 = (f32[32,2048]{1,0:T(8,128)S(1)}, bf16[512,2048]{1,0:T(8,128)(2,1)}) custom-call(s32[1]{0:T(128)} %bitcast.1.refs_0_, f32[264,256]{1,0:T(8,128)S(1)} %shard_map.119.refs_1_, f32[264,256]{1,0:T(8,128)S(1)} %collective-permute-done.4.refs_2_, bf16[2048,2048]{1,0:T(8,128)(2,1)S(1)} %copy-done.1, ...), custom_call_target="tpu_custom_call", output_to_operand_aliasing={{1}: (5, {})} | custom-call | flops 268435456 | bytes 10485760 | tf_op jit(solution)/shard_map/pallas_call | solution.py:355
  169.0 2.9 %shard_map.122._ = bf16[512,2048]{1,0:T(8,128)(2,1)} custom-call(s32[1]{0:T(128)} %bitcast.10.row, f32[224,2048]{1,0:T(8,128)} %collective-permute-done.9.y, bf16[512,2048]{1,0:T(8,128)(2,1)S(1)} %copy-done.3, bf16[512,2048]{1,0:T(8,128)(2,1)} %get-tuple-element.46._), custom_call_target="tpu_custom_call", output_to_operand_aliasing={{}: (3, {})} | custom-call | flops 448000000 | bytes 3670016 | tf_op jit(solution)/shard_map/pallas_call | solution.py:388
  171.9 0.9 shard_map.123
  (31 shorter events, 2.5 us)
Async XLA Ops:
  31.9 2.7 %collective-permute-start = (f32[520,256]{1,0:T(8,128)}, f32[520,256]{1,0:T(8,128)S(1)}, u32[]{:S(2)}, u32[]{:S(2)}) collective-permute-start(f32[520,256]{1,0:T(8,128)} %get-tuple-element.32), channel_id=1, source_target_pairs={{0,1},{1,0},{2,3},{3,2},{4,5},{5,4},{6,7},{7,6}} | collective-permute-start | bytes 1597448 | tf_op jit(solution)/shard_map/ppermute | solution.py:414
  34.7 1.0 copy-start.11
  36.1 0.8 copy-start.7
  55.8 2.3 %collective-permute-start.1 = (f32[648,256]{1,0:T(8,128)}, f32[648,256]{1,0:T(8,128)S(1)}, u32[]{:S(2)}, u32[]{:S(2)}) collective-permute-start(f32[648,256]{1,0:T(8,128)} %get-tuple-element.36), channel_id=1, source_target_pairs={{0,1},{1,0},{2,3},{3,2},{4,5},{5,4},{6,7},{7,6}} | collective-permute-start | bytes 1990664 | tf_op jit(solution)/shard_map/ppermute | solution.py:414
  58.1 1.1 copy-start.9
  59.6 0.8 copy-start.5
  60.4 19.2 %copy-start.6 = (f32[648,256]{1,0:T(8,128)S(1)}, f32[648,256]{1,0:T(8,128)}, u32[]{:S(2)}) copy-start(f32[648,256]{1,0:T(8,128)} %copy-done.5) | copy-start | bytes 1990660
  60.4 25.4 %copy-start.8 = (f32[520,256]{1,0:T(8,128)S(1)}, f32[520,256]{1,0:T(8,128)}, u32[]{:S(2)}) copy-start(f32[520,256]{1,0:T(8,128)} %copy-done.7) | copy-start | bytes 1597444
  79.4 2.8 %collective-permute-start.2 = (f32[648,256]{1,0:T(8,128)}, f32[648,256]{1,0:T(8,128)S(1)}, u32[]{:S(2)}, u32[]{:S(2)}) collective-permute-start(f32[648,256]{1,0:T(8,128)} %get-tuple-element.40), channel_id=1, source_target_pairs={{0,1},{1,0},{2,3},{3,2},{4,5},{5,4},{6,7},{7,6}} | collective-permute-start | bytes 1990664 | tf_op jit(solution)/shard_map/ppermute | solution.py:414
  79.6 43.7 %collective-permute-start.6 = (f32[648,256]{1,0:T(8,128)S(1)}, f32[648,256]{1,0:T(8,128)S(1)}, u32[]{:S(2)}, u32[]{:S(2)}) collective-permute-start(f32[648,256]{1,0:T(8,128)S(1)} %copy-done.6), channel_id=1, source_target_pairs={{0,2},{2,0},{1,3},{3,1},{4,6},{6,4},{5,7},{7,5}} | collective-permute-start | bytes 1990664 | tf_op jit(solution)/shard_map/ppermute | solution.py:416
  82.2 1.1 copy-start.10
  83.7 53.2 %copy-start.4 = (f32[648,256]{1,0:T(8,128)}, f32[648,256]{1,0:T(8,128)S(1)}, u32[]{:S(2)}) copy-start(f32[648,256]{1,0:T(8,128)S(1)} %shard_map.117.rest_2_.refs_5_) | copy-start | bytes 1990660
  83.7 39.6 %collective-permute-start.7 = (f32[648,256]{1,0:T(8,128)S(1)}, f32[648,256]{1,0:T(8,128)S(1)}, u32[]{:S(2)}, u32[]{:S(2)}) collective-permute-start(f32[648,256]{1,0:T(8,128)S(1)} %shard_map.117.rest_2_.refs_5_), channel_id=1, source_target_pairs={{0,2},{2,0},{1,3},{3,1},{4,6},{6,4},{5,7},{7,5}} | collective-permute-start | bytes 1990664 | tf_op jit(solution)/shard_map/ppermute | solution.py:416
  85.9 37.4 %collective-permute-start.5 = (f32[520,256]{1,0:T(8,128)S(1)}, f32[520,256]{1,0:T(8,128)S(1)}, u32[]{:S(2)}, u32[]{:S(2)}) collective-permute-start(f32[520,256]{1,0:T(8,128)S(1)} %copy-done.8), channel_id=1, source_target_pairs={{0,2},{2,0},{1,3},{3,1},{4,6},{6,4},{5,7},{7,5}} | collective-permute-start | bytes 1597448 | tf_op jit(solution)/shard_map/ppermute | solution.py:416
  123.3 3.4 %copy-start = (bf16[2048,2048]{1,0:T(8,128)(2,1)S(1)}, bf16[2048,2048]{1,0:T(8,128)(2,1)}, u32[]{:S(2)}) copy-start(bf16[2048,2048]{1,0:T(8,128)(2,1)} %refs_3_.1) | copy-start | bytes 25165828
  126.7 1.6 copy-start.2
  136.2 32.7 %collective-permute-start.9 = (f32[224,2048]{1,0:T(8,128)}, f32[224,2048]{1,0:T(8,128)}, u32[]{:S(2)}, u32[]{:S(2)}) collective-permute-start(f32[224,2048]{1,0:T(8,128)} %get-tuple-element.45), channel_id=1, source_target_pairs={{0,1},{1,0},{2,3},{3,2},{4,5},{5,4},{6,7},{7,6}} | collective-permute-start | bytes 5505032 | tf_op jit(solution)/shard_map/ppermute | solution.py:423
  147.3 1.9 %collective-permute-start.3 = (f32[264,256]{1,0:T(8,128)}, f32[264,256]{1,0:T(8,128)S(1)}, u32[]{:S(2)}, u32[]{:S(2)}) collective-permute-start(f32[264,256]{1,0:T(8,128)} %get-tuple-element.42), channel_id=1, source_target_pairs={{0,1},{1,0},{2,3},{3,2},{4,5},{5,4},{6,7},{7,6}} | collective-permute-start | bytes 811016 | tf_op jit(solution)/shard_map/ppermute | solution.py:414
  149.2 1.0 copy-start.12
  150.4 8.8 %collective-permute-start.4 = (f32[264,256]{1,0:T(8,128)S(1)}, f32[264,256]{1,0:T(8,128)S(1)}, u32[]{:S(2)}, u32[]{:S(2)}) collective-permute-start(f32[264,256]{1,0:T(8,128)S(1)} %shard_map.119.refs_1_), channel_id=1, source_target_pairs={{0,2},{2,0},{1,3},{3,1},{4,6},{6,4},{5,7},{7,5}} | collective-permute-start | bytes 811016 | tf_op jit(solution)/shard_map/ppermute | solution.py:416
  159.2 3.4 %copy-start.1 = (bf16[2048,2048]{1,0:T(8,128)(2,1)S(1)}, bf16[2048,2048]{1,0:T(8,128)(2,1)}, u32[]{:S(2)}) copy-start(bf16[2048,2048]{1,0:T(8,128)(2,1)} %refs_3_.1) | copy-start | bytes 25165828
  162.6 1.6 copy-start.3
  168.9 2.9 %collective-permute-start.8 = (f32[32,2048]{1,0:T(8,128)S(1)}, f32[32,2048]{1,0:T(8,128)S(1)}, u32[]{:S(2)}, u32[]{:S(2)}) collective-permute-start(f32[32,2048]{1,0:T(8,128)S(1)} %get-tuple-element.44), channel_id=1, source_target_pairs={{0,1},{1,0},{2,3},{3,2},{4,5},{5,4},{6,7},{7,6}} | collective-permute-start | bytes 786440 | tf_op jit(solution)/shard_map/ppermute | solution.py:425

commit v3 on v2

--- a/solution.py
+++ b/solution.py
@@ -21,7 +21,7 @@
 SMEM = pl.BlockSpec(memory_space=pltpu.SMEM)
 
 
-def project_kernel(hidden, w_norm, w_q, w_k, w_v, lengths, q_out, k_out, v_out, x, wide, narrow, xn, cos_t, sin_t, q_low, q_high, sem):
+def project(hidden, w_norm, w_q, w_k, w_v, positions, x, wide, narrow, xn, cos_t, sin_t, q_rows, k_rows, v_rows, sem, start_more):
     rows = hidden.shape[0]
     half = HEAD // 2
     tiles = ([pltpu.make_async_copy(w_k, narrow.at[0], sem.at[0]), pltpu.make_async_copy(w_v, narrow.at[1], sem.at[1])]
@@ -30,12 +30,12 @@
     first.start()
     for copy in tiles[:2]:
         copy.start()
-    count = lengths.shape[0]
-    positions = jnp.concatenate([lengths[...], jnp.zeros((8 - count, 128), jnp.int32)], axis=0).astype(jnp.float32).T
+    count = positions.shape[0]
+    column = jnp.concatenate([positions[...], jnp.zeros((8 - count, 128), jnp.int32)], axis=0).astype(jnp.float32).T
     lane = lax.broadcasted_iota(jnp.int32, (1, half), 1).astype(jnp.float32)
     freq = jnp.exp(lane * (-2.0 / HEAD * math.log(ROPE_BASE)))
     for i in range(count):
-        angles = positions[:, i:i + 1] * freq
+        angles = column[:, i:i + 1] * freq
         cos_t[i * 128:(i + 1) * 128, :] = jnp.cos(angles)
         sin_t[i * 128:(i + 1) * 128, :] = jnp.sin(angles)
     gain = 1.0 + w_norm[...].astype(jnp.float32)
@@ -43,6 +43,7 @@
     first.wait()
     for copy in tiles[2:]:
         copy.start()
+    start_more()
 
     def norm(i, carry):
         at = pl.ds(pl.multiple_of(i * 32, 32), 32)
@@ -58,50 +59,26 @@
 
     def rotated(u):
         lower, upper = u[:, :half], u[:, half:]
-        return lower * cos_t[...] - upper * sin_t[...], upper * cos_t[...] + lower * sin_t[...]
+        return jnp.concatenate([lower * cos_t[...] - upper * sin_t[...], upper * cos_t[...] + lower * sin_t[...]], axis=1)
 
     tiles[0].wait()
-    lower, upper = rotated(product(narrow[0]))
-    k_out[:, :half] = lower.astype(jnp.bfloat16).astype(jnp.float32)
-    k_out[:, half:] = upper.astype(jnp.bfloat16).astype(jnp.float32)
+    k_rows[...] = rotated(product(narrow[0])).astype(jnp.bfloat16).astype(jnp.float32)
     tiles[1].wait()
-    v_out[...] = product(narrow[1])
+    v_rows[...] = product(narrow[1])
 
     def head(h, carry):
         pltpu.make_async_copy(w_k, wide.at[h], sem.at[2 + h]).wait()
-        lower, upper = rotated(product(wide[h]))
-        q_low[pl.ds(h, rows, stride=HEADS), :] = lower * HEAD ** -0.5
-        q_high[pl.ds(h, rows, stride=HEADS), :] = upper * HEAD ** -0.5
+        q_rows[:, pl.ds(pl.multiple_of(h * HEAD, HEAD), HEAD)] = (rotated(product(wide[h])) * HEAD ** -0.5).astype(jnp.bfloat16)
         return carry
 
     lax.fori_loop(0, HEADS, head, 0)
 
-    def pack(i, carry):
-        at = pl.ds(pl.multiple_of(i * 128, 128), 128)
-        q_out[at, :half] = q_low[at, :].astype(jnp.bfloat16)
-        q_out[at, half:] = q_high[at, :].astype(jnp.bfloat16)
-        return carry
-
-    lax.fori_loop(0, rows * HEADS // 128, pack, 0)
-
-
-def project_call(hidden, w_norm, w_q, w_k, w_v, cache_len):
-    rows, dim = hidden.shape
-    half_row = pltpu.VMEM((rows, HEAD // 2), jnp.float32)
-    half_q = pltpu.VMEM((rows * HEADS, HEAD // 2), jnp.float32)
-    return pl.pallas_call(
-        project_kernel,
-        in_specs=[HBM, VMEM, HBM, HBM, HBM, VMEM],
-        out_specs=(VMEM, VMEM, VMEM),
-        out_shape=(jax.ShapeDtypeStruct((rows * HEADS, HEAD), jnp.bfloat16), jax.ShapeDtypeStruct((rows, HEAD), jnp.float32),
-                   jax.ShapeDtypeStruct((rows, HEAD), jnp.float32)),
-        scratch_shapes=[pltpu.VMEM((rows, dim), jnp.bfloat16), pltpu.VMEM((HEADS, dim, HEAD), jnp.bfloat16),
-                        pltpu.VMEM((2, dim, HEAD), jnp.bfloat16), pltpu.VMEM((rows, dim), jnp.bfloat16), half_row, half_row, half_q, half_q,
-                        pltpu.SemaphoreType.DMA((3 + HEADS,))],
-        compiler_params=pltpu.CompilerParams(vmem_limit_bytes=62 << 20),
-        cost_estimate=pl.CostEstimate(flops=2 * rows * dim * 10 * HEAD, bytes_accessed=24 << 20, transcendentals=0),
-        name="project",
-    )(hidden, w_norm.reshape(dim // 128, 128), w_q, w_k, w_v, cache_len.reshape(rows // 128, 128))
+
+def reorder(by_row):
+    i = lax.broadcasted_iota(jnp.int32, (128, 128), 0)
+    j = lax.broadcasted_iota(jnp.int32, (128, 128), 1)
+    hit = j == (i % HEADS) * GROUP + i // HEADS if by_row else j == (i % GROUP) * HEADS + i // GROUP
+    return jnp.where(hit, 1.0, 0.0).astype(jnp.bfloat16)
 
 
 def attend_group(kbuf, vbuf, q, plane, slot_base, store):
@@ -130,25 +107,40 @@
     return top, total
 
 
-def attention_kernel(keep_groups, send_groups, after, chained, scalars, lengths, q, k_new, v_new, k_in, v_in, *rest):
-    rest = list(rest[2 * chained + after:])
-    k_out, v_out = rest[:2]
-    parts = rest[2:2 + (keep_groups > 0) + (send_groups > 0)]
-    kbuf, vbuf, qbuf, k_row, v_row, in_sem, out_sem, small_sem = rest[2 + len(parts):]
-    starts = [pl.multiple_of(scalars[0], GROUP), pl.multiple_of(scalars[1], GROUP)]
+def attention_kernel(first_row, groups, mode, scalars, lengths, *refs):
+    refs = list(refs)
+    take = lambda n: [refs.pop(0) for _ in range(n)]
+    half = lengths.shape[0] // 2
+    starts = [pl.multiple_of(scalars[side] * half + first_row, GROUP) for side in range(2)]
     slot_base = scalars[2]
+    if mode == 'first':
+        inputs = take(6)
+    else:
+        q_in, k_new, v_new = take(3)
+    k_in, v_in = take(2)
+    if mode != 'first':
+        take(3)
+    k_out, v_out = take(2)
+    parts = take(2)
+    if mode == 'first':
+        saved = take(3)
+    kbuf, vbuf, in_sem, out_sem = take(4)
     depth, _, slots, _ = kbuf.shape
-    groups = keep_groups + send_groups
-    ahead = min(3, groups)
+    total_groups = 2 * groups
+    ahead = min(5, total_groups)
 
     def row_of(g):
-        return pl.multiple_of(jnp.where(g < keep_groups, starts[0] + g * GROUP, starts[1] + (g - keep_groups) * GROUP), GROUP)
+        return pl.multiple_of(jnp.where(g < groups, starts[0] + g * GROUP, starts[1] + (g - groups) * GROUP), GROUP)
 
     def fetch(g):
         slot = lax.rem(g, depth)
         at = pl.ds(row_of(g), GROUP)
-        return (pltpu.make_async_copy(k_in.at[at], kbuf.at[slot], in_sem.at[0, slot]),
-                pltpu.make_async_copy(v_in.at[at], vbuf.at[slot], in_sem.at[1, slot]))
+        copies = [pltpu.make_async_copy(k_in.at[at], kbuf.at[slot], in_sem.at[0, slot]),
+                  pltpu.make_async_copy(v_in.at[at], vbuf.at[slot], in_sem.at[1, slot])]
+        if mode != 'first':
+            copies += [pltpu.make_async_copy(source.at[at], ring.at[slot], in_sem.at[2 + i, slot])
+                       for i, (source, ring) in enumerate(((q_in, q_ring), (k_new, k_ring), (v_new, v_ring)))]
+        return copies
 
     def flush(g):
         slot = lax.rem(g, depth)
@@ -156,32 +148,28 @@
         return (pltpu.make_async_copy(kbuf.at[slot], k_out.at[at], out_sem.at[0, slot]),
                 pltpu.make_async_copy(vbuf.at[slot], v_out.at[at], out_sem.at[1, slot]))
 
-    segments = []
-    if keep_groups:
-        segments.append((parts[0], 0, keep_groups, starts[0]))
-    if send_groups:
-        segments.append((parts[-1], keep_groups, send_groups, starts[1]))
-    small = []
-    for i, (_, first, count, start) in enumerate(segments):
-        rows = pl.ds(first * GROUP, count * GROUP)
-        small += [
-            pltpu.make_async_copy(q.at[pl.ds(pl.multiple_of(start * HEADS, 128), count * 128)], qbuf.at[pl.ds(first * 128, count * 128)], small_sem.at[3 * i]),
-            pltpu.make_async_copy(k_new.at[pl.ds(start, count * GROUP)], k_row.at[rows], small_sem.at[3 * i + 1]),
-            pltpu.make_async_copy(v_new.at[pl.ds(start, count * GROUP)], v_row.at[rows], small_sem.at[3 * i + 2])]
-    for copy in small:
-        copy.start()
-    for g in range(ahead):
-        for copy in fetch(g):
-            copy.start()
-    for part, _, count, _ in segments:
-        part[count * 128:, :] = jnp.zeros((8, HEAD), jnp.float32)
-    for copy in small:
-        copy.wait()
+    def start_all():
+        for g in range(ahead):
+            for copy in fetch(g):
+                copy.start()
+
+    keep = []
+    if mode == 'first':
+        save_sem, *scratch = take(11)
+        q_rows, k_rows, v_rows = scratch[6:9]
+        project(*inputs, *scratch, start_all)
+        keep = [pltpu.make_async_copy(ref, out, save_sem.at[i]) for i, (ref, out) in enumerate(zip((q_rows, k_rows, v_rows), saved))]
+    else:
+        q_ring, k_ring, v_ring = take(3)
+        start_all()
+    for part in parts:
+        part[groups * 128:, :] = jnp.zeros((8, HEAD), jnp.float32)
     row_in_tile = lax.broadcasted_iota(jnp.int32, (16, HEAD), 0)
     lane = lax.broadcasted_iota(jnp.int32, (1, 128), 1) // HEADS
     stat_row = lax.broadcasted_iota(jnp.int32, (8, HEAD), 0)
-
-    def one(part, first, count, g):
+    order = reorder(True)
+
+    def one(part, first, g):
         slot = lax.rem(g, depth)
         row0 = row_of(g)
         place = g - first
@@ -197,21 +185,28 @@
             def _():
                 tile = pl.multiple_of(local // 16 * 16, 16)
                 hit = row_in_tile == local - tile
-                for buf, new in ((kbuf, k_row), (vbuf, v_row)):
+                if mode == 'first':
+                    news = k_rows[pl.ds(row0 + b, 1), :], v_rows[pl.ds(row0 + b, 1), :]
+                else:
+                    news = k_ring[slot, pl.ds(b, 1), :], v_ring[slot, pl.ds(b, 1), :]
+                for buf, row in zip((kbuf, vbuf), news):
                     old = buf[slot, b, pl.ds(tile, 16), :].astype(jnp.float32)
-                    row = new[pl.ds(g * GROUP + b, 1), :]
                     buf[slot, b, pl.ds(tile, 16), :] = jnp.where(hit, row, old).astype(jnp.bfloat16)
 
         def store(pair, value):
             part[pl.ds(pl.multiple_of(place * 128, 128) + pair * 16, 16), :] = value
 
-        queries = qbuf[pl.ds(pl.multiple_of(g * 128, 128), 128), :]
+        if mode == 'first':
+            heads = [q_rows[pl.ds(row0, GROUP), h * HEAD:(h + 1) * HEAD] for h in range(HEADS)]
+        else:
+            heads = [q_ring[slot, :, h * HEAD:(h + 1) * HEAD] for h in range(HEADS)]
+        queries = jnp.dot(order, jnp.concatenate(heads, axis=0), preferred_element_type=jnp.float32).astype(jnp.bfloat16)
         top, total = attend_group(kbuf.at[slot], vbuf.at[slot], queries, plane, slot_base, store)
-        part[count * 128:, :] = jnp.where(stat_row == place, jnp.concatenate([top, total], axis=1), part[count * 128:, :])
+        part[groups * 128:, :] = jnp.where(stat_row == place, jnp.concatenate([top, total], axis=1), part[groups * 128:, :])
         for copy in flush(g):
             copy.start()
-        if groups > ahead:
-            @pl.when(g + ahead < groups)
+        if total_groups > ahead:
+            @pl.when(g + ahead < total_groups)
             def _():
                 @pl.when(g + ahead >= depth)
                 def _():
@@ -221,42 +216,59 @@
                 for copy in fetch(g + ahead):
                     copy.start()
 
-    for part, first, count, _ in segments:
-        def body(g, carry, part=part, first=first, count=count):
-            one(part, first, count, g)
+    for i, part in enumerate(parts):
+        def body(g, carry, part=part, first=i * groups):
+            one(part, first, g)
             return carry
 
-        lax.fori_loop(first, first + count, body, 0)
-    for g in range(max(groups - depth, 0), groups):
+        lax.fori_loop(i * groups, (i + 1) * groups, body, 0)
+        if i == 0:
+            for copy in keep:
+                copy.start()
+    for g in range(max(total_groups - depth, 0), total_groups):
         for copy in flush(g):
             copy.wait()
-
-
-def attention_call(keep, send, scalars, lengths, q, k_new, v_new, k_block, v_block, outs, after):
-    rows = keep + send
+    for copy in keep:
+        copy.wait()
+
+
+def attention_call(first_row, rows, scalars, lengths, tokens, k_block, v_block, outs, after):
+    mode = 'later' if outs else 'first'
     groups = rows // GROUP
-    depth = min(groups, 7)
+    depth = min(2 * groups, 8)
     slots = k_block.shape[1]
-    operands = [scalars, lengths, q, k_new, v_new, k_block, v_block, *outs, *after]
-    parts = tuple(jax.ShapeDtypeStruct((n * HEADS + 8, HEAD), jnp.float32) for n in (keep, send) if n)
+    part = jax.ShapeDtypeStruct((rows * HEADS + 8, HEAD), jnp.float32)
+    shapes = [jax.ShapeDtypeStruct(k_block.shape, k_block.dtype), jax.ShapeDtypeStruct(v_block.shape, v_block.dtype), part, part]
+    ring = pltpu.VMEM((depth, GROUP, slots, HEAD), jnp.bfloat16)
+    scratch = [ring, ring, pltpu.SemaphoreType.DMA((5, depth)), pltpu.SemaphoreType.DMA((2, depth))]
+    all_rows = lengths.shape[0]
+    dim = tokens[0].shape[1]
+    if mode == 'first':
+        token_specs = [HBM, VMEM, HBM, HBM, HBM, VMEM]
+        tokens = [tokens[0], tokens[1].reshape(dim // 128, 128), *tokens[2:], lengths.reshape(all_rows // 128, 128)]
+        saved = [jax.ShapeDtypeStruct((all_rows, HEADS * HEAD), jnp.bfloat16)] + [jax.ShapeDtypeStruct((all_rows, HEAD), jnp.float32)] * 2
+        shapes += saved
+        half_row = pltpu.VMEM((all_rows, HEAD // 2), jnp.float32)
+        scratch += [pltpu.SemaphoreType.DMA((3,)), pltpu.VMEM((all_rows, dim), jnp.bfloat16), pltpu.VMEM((HEADS, dim, HEAD), jnp.bfloat16),
+                    pltpu.VMEM((2, dim, HEAD), jnp.bfloat16), pltpu.VMEM((all_rows, dim), jnp.bfloat16), half_row, half_row,
+                    *(pltpu.VMEM(a.shape, a.dtype) for a in saved), pltpu.SemaphoreType.DMA((3 + HEADS,))]
+        operands = [scalars, lengths, *tokens, k_block, v_block]
+        specs = [SMEM, SMEM, *token_specs, HBM, HBM]
+        aliases = {}
+    else:
+        scratch += [pltpu.VMEM((depth, GROUP, HEADS * HEAD), jnp.bfloat16)] + [pltpu.VMEM((depth, GROUP, HEAD), jnp.float32)] * 2
+        operands = [scalars, lengths, *tokens, k_block, v_block, *outs, after]
+        specs = [SMEM, SMEM] + [HBM] * 7 + [ANY]
+        aliases = {7: 0, 8: 1}
     return pl.pallas_call(
-        functools.partial(attention_kernel, keep // GROUP, send // GROUP, len(after), bool(outs)),
-        out_shape=(jax.ShapeDtypeStruct(k_block.shape, k_block.dtype), jax.ShapeDtypeStruct(v_block.shape, v_block.dtype), *parts),
-        in_specs=[SMEM, SMEM] + [HBM] * (5 + len(outs)) + [ANY] * len(after),
-        out_specs=(HBM, HBM) + (VMEM,) * len(parts),
-        input_output_aliases={7: 0, 8: 1} if outs else {},
-        scratch_shapes=[
-            pltpu.VMEM((depth, GROUP, slots, HEAD), jnp.bfloat16),
-            pltpu.VMEM((depth, GROUP, slots, HEAD), jnp.bfloat16),
-            pltpu.VMEM((rows * HEADS, HEAD), jnp.bfloat16),
-            pltpu.VMEM((rows, HEAD), jnp.float32),
-            pltpu.VMEM((rows, HEAD), jnp.float32),
-            pltpu.SemaphoreType.DMA((2, depth)),
-            pltpu.SemaphoreType.DMA((2, depth)),
-            pltpu.SemaphoreType.DMA((6,)),
-        ],
+        functools.partial(attention_kernel, first_row, groups, mode),
+        out_shape=tuple(shapes),
+        in_specs=specs,
+        out_specs=(HBM, HBM, VMEM, VMEM) + (HBM,) * (len(shapes) - 4),
+        input_output_aliases=aliases,
+        scratch_shapes=scratch,
         compiler_params=pltpu.CompilerParams(vmem_limit_bytes=62 << 20),
-        cost_estimate=pl.CostEstimate(flops=rows * 10_000_000, bytes_accessed=rows * 262144, transcendentals=rows * 8 * slots),
+        cost_estimate=pl.CostEstimate(flops=rows * 20_000_000, bytes_accessed=rows * 524288, transcendentals=rows * 16 * slots),
     )(*operands)
 
 
@@ -299,7 +311,7 @@
     w_o, hidden = refs[2 * len(chunks):2 * len(chunks) + 2]
     rest = refs[2 * len(chunks) + 2 + late:]
     y, out = rest[:2]
-    weights, low, high, attended, x, done, sem = rest[-7:]
+    weights, attended, x, done, sem = rest[-5:]
     total = sum(chunks)
     tiles = y.shape[1] // HEAD
 
@@ -311,6 +323,7 @@
     load.start()
     for n in range(3):
         tile_load(n).start()
+    order = reorder(False)
     first = 0
     for i, rows in enumerate(chunks):
         groups = rows // GROUP
@@ -319,12 +332,9 @@
         for g in range(groups):
             at = pl.ds(g * 128, 128)
             value = one[at, :] * columns[:, g:g + 1] + two[at, :] * columns[:, 8 + g:9 + g]
-            low[at, :] = value[:, :128]
-            high[at, :] = value[:, 128:]
-        for h in range(HEADS):
-            for side, source in enumerate((low, high)):
-                column = h * HEAD + side * 128
-                attended[first:first + rows, column:column + 128] = source[pl.ds(h, rows, stride=HEADS), :].astype(jnp.bfloat16)
+            by_head = jnp.dot(order, value.astype(jnp.bfloat16), preferred_element_type=jnp.float32).astype(jnp.bfloat16)
+            for h in range(HEADS):
+                attended[first + g * GROUP:first + (g + 1) * GROUP, h * HEAD:(h + 1) * HEAD] = by_head[h * GROUP:(h + 1) * GROUP]
         first += rows
     load.wait()
 
@@ -358,10 +368,10 @@
         in_specs=[SMEM] + [VMEM] * len(parts) + [HBM, HBM] + [HBM] * late,
         out_specs=specs,
         input_output_aliases={len(parts) + 3: 1} if late else {},
-        scratch_shapes=[pltpu.VMEM((dim // HEAD, w_o.shape[0], HEAD), jnp.bfloat16), pltpu.VMEM((max(chunks) * HEADS, 128), jnp.float32), pltpu.VMEM((max(chunks) * HEADS, 128), jnp.float32),
+        scratch_shapes=[pltpu.VMEM((dim // HEAD, w_o.shape[0], HEAD), jnp.bfloat16),
                         pltpu.VMEM((total, w_o.shape[0]), jnp.bfloat16), pltpu.VMEM((total, dim), jnp.bfloat16),
                         pltpu.VMEM((total, dim), jnp.bfloat16), pltpu.SemaphoreType.DMA((2 + dim // HEAD,))],
-        compiler_params=pltpu.CompilerParams(vmem_limit_bytes=26 << 20),
+        compiler_params=pltpu.CompilerParams(vmem_limit_bytes=62 << 20),
         cost_estimate=pl.CostEstimate(flops=2 * total * w_o.shape[0] * dim, bytes_accessed=10 << 20, transcendentals=0),
     )(row0, *parts, w_o, hidden, *([out] if late else []))
 
@@ -405,12 +415,15 @@
     core = lax.rem(me, 2)
     sibling = [(0, 1), (1, 0), (2, 3), (3, 2)]
     across = [(0, 2), (2, 0), (1, 3), (3, 1)]
-    q, k_new, v_new = project_call(hidden, w_norm, w_q, w_k, w_v, cache_len)
+    scalars = jnp.stack([core, 1 - core, me * slots]).astype(jnp.int32)
+    tokens = (hidden, w_norm, w_q, w_k, w_v)
     outs, merged, theirs = (), [], []
     first = 0
-    for rows in CHUNKS:
-        scalars = jnp.stack([core * half + first, (1 - core) * half + first, me * slots]).astype(jnp.int32)
-        *outs, kept, sent = attention_call(rows, rows, scalars, cache_len, q, k_new, v_new, k_block, v_block, outs, merged[-1:])
+    for i, rows in enumerate(CHUNKS):
+        *outs, kept, sent = results = attention_call(
+            first, rows, scalars, cache_len, tokens, k_block, v_block, outs, merged[-1] if merged else None)
+        if i == 0:
+            outs, (kept, sent), tokens = results[:2], results[2:4], results[4:]
         taken = lax.ppermute(sent, 'sp', sibling)
         merged.append(merge_call(rows, kept, taken))
         theirs.append(lax.ppermute(merged[-1], 'sp', across))

time: 173 us -> 159 us (0.919)
  Pallas kernels: 96.8 us -> 88 us
  local copies, waits for them, and re-layouts: 15.8 us -> 10.5 us
    pallas_call x5 -> x4, Pallas kernels: 79 us -> 67.9 us  [attention_call(): pl.pallas_call(functools.partial(attention_kernel, first_row, groups, mod...]
    unnamed x26 -> x28, local copies, waits for them, and re-layouts: 15.8 us -> 10.5 us
    pallas_call x2, Pallas kernels: 12.7 us -> 16.5 us  [finish_call(): pl.pallas_call(functools.partial(finish_kernel, chunks, late), out_shape=...]
  transfers between devices with their start and end apart: 10 -> 10, of which waited for: 5 -> 5; matrix products, arithmetic and copies ran while one was open for 1% -> 0% of each run, Pallas kernels for 11% -> 11%
where the time goes in v3:
time: 159 us
  Pallas kernels  88 us (55%)
  waiting for transfers between devices  49.6 us (31%)
  local copies, waits for them, and re-layouts  10.5 us (7%)
  starting transfers between devices  9.1 us (6%)
    pallas_call x4, Pallas kernels, attention_call(): pl.pallas_call(functools.partial(attention_kernel, first_row, groups, mod...  67.9 us
    ppermute x4, waiting for transfers between devices, local_step(): theirs.append(lax.ppermute(merged[-1], 'sp', across))  44.5 us
    pallas_call x2, Pallas kernels, finish_call(): pl.pallas_call(functools.partial(finish_kernel, chunks, late), out_shape=...  16.5 us
    unnamed x28, local copies, waits for them, and re-layouts  10.5 us
    ppermute x4, starting transfers between devices, local_step(): theirs.append(lax.ppermute(merged[-1], 'sp', across))  6.5 us
    ppermute x4, waiting for transfers between devices, local_step(): taken = lax.ppermute(sent, 'sp', sibling)  5.09 us
  transfers between devices with their start and end apart: 10, of which 5 were waited for; matrix products, arithmetic and copies ran while one was open for 0% of the time, Pallas kernels for 11%

profile of v3, /device:TPU:0, one launch (start us, length us, event | category | flops | bytes accessed | tf_op | source)
XLA Modules:
  0.0 158.6 jit_solution(9862138339807509774)
XLA Ops:
  0.6 0.6 pad_add_fusion.scalars
  1.2 24.8 %shard_map.112 = (bf16[512,128,256]{2,1,0:T(8,128)(2,1)}, bf16[512,128,256]{2,1,0:T(8,128)(2,1)}, f32[520,256]{1,0:T(8,128)}, f32[520,256]{1,0:T(8,128)}, bf16[5...) custom-call(s32[3]{0:T(128)} %pad_add_fusion.scalars, s32[512]{0:T(512)} %lengths.7, ...), custom_call_target="tpu_custom_call" | custom-call | flops 1280000000 | bytes 33554432 | tf_op jit(solution)/shard_map/pallas_call | solution.py:263
  26.0 0.9 collective-permute-start
  26.9 1.8 %collective-permute-done.two = f32[520,256]{1,0:T(8,128)S(1)} collective-permute-done((f32[520,256]{1,0:T(8,128)}, f32[520,256]{1,0:T(8,128)S(1)}, u32[]{:S(2)}, u32[]{:S(2)}) %collective-permute-start) | collective-permute-done | bytes 532512 | tf_op jit(solution)/shard_map/ppermute | solution.py:427
  28.6 1.0 copy-done.9
  30.0 0.8 copy-done.4
  30.8 17.2 %shard_map.114 = (bf16[512,128,256]{2,1,0:T(8,128)(2,1)}, bf16[512,128,256]{2,1,0:T(8,128)(2,1)}, f32[648,256]{1,0:T(8,128)}, f32[648,256]{1,0:T(8,128)}) custom-call(s32[3]{0:T(128)} %pad_add_fusion.scalars, s32[512]{0:T(512)} %lengths.7, bf16[512,2048]{1,0:T(8,128)(2,1)} %get-tuple-element.26.refs_0_, ...), custom_call_target="tpu_custom_call", output_to_operand_aliasing={{0}: (7, {}), {1}: (8, {})} | custom-call | flops 1600000000 | bytes 41943040 | tf_op jit(solution)/shard_map/pallas_call | solution.py:263
  48.0 0.5 collective-permute-start.1
  48.5 1.9 %collective-permute-done.1.two = f32[648,256]{1,0:T(8,128)S(1)} collective-permute-done((f32[648,256]{1,0:T(8,128)}, f32[648,256]{1,0:T(8,128)S(1)}, u32[]{:S(2)}, u32[]{:S(2)}) %collective-permute-start.1) | collective-permute-done | bytes 663584 | tf_op jit(solution)/shard_map/ppermute | solution.py:427
  50.4 1.1 copy-done.8
  51.9 0.9 copy-done.1
  52.8 17.2 %shard_map.116 = (bf16[512,128,256]{2,1,0:T(8,128)(2,1)}, bf16[512,128,256]{2,1,0:T(8,128)(2,1)}, f32[648,256]{1,0:T(8,128)}, f32[648,256]{1,0:T(8,128)}) custom-call(s32[3]{0:T(128)} %pad_add_fusion.scalars, s32[512]{0:T(512)} %lengths.7, bf16[512,2048]{1,0:T(8,128)(2,1)} %get-tuple-element.26.refs_0_, ...), custom_call_target="tpu_custom_call", output_to_operand_aliasing={{0}: (7, {}), {1}: (8, {})} | custom-call | flops 1600000000 | bytes 41943040 | tf_op jit(solution)/shard_map/pallas_call | solution.py:263
  70.0 0.6 collective-permute-start.2
  70.5 2.7 %collective-permute-start.6 = (f32[648,256]{1,0:T(8,128)S(1)}, f32[648,256]{1,0:T(8,128)S(1)}, u32[]{:S(2)}, u32[]{:S(2)}) collective-permute-start(f32[648,256]{1,0:T(8,128)S(1)} %copy-done.2), channel_id=1, source_target_pairs={{0,2},{2,0},{1,3},{3,1},{4,6},{6,4},{5,7},{7,5}} | collective-permute-start | bytes 1990664 | tf_op jit(solution)/shard_map/ppermute | solution.py:429
  73.2 1.1 copy-done.7
  74.7 2.0 %collective-permute-start.7 = (f32[648,256]{1,0:T(8,128)S(1)}, f32[648,256]{1,0:T(8,128)S(1)}, u32[]{:S(2)}, u32[]{:S(2)}) collective-permute-start(f32[648,256]{1,0:T(8,128)S(1)} %shard_map.117.refs_7_.refs_5_), channel_id=1, source_target_pairs={{0,2},{2,0},{1,3},{3,1},{4,6},{6,4},{5,7},{7,5}} | collective-permute-start | bytes 1990664 | tf_op jit(solution)/shard_map/ppermute | solution.py:429
  76.7 37.5 %collective-permute-done.5.refs_2_ = f32[520,256]{1,0:T(8,128)} collective-permute-done((f32[520,256]{1,0:T(8,128)S(1)}, f32[520,256]{1,0:T(8,128)}, u32[]{:S(2)}, u32[]{:S(2)}) %collective-permute-start.5) | collective-permute-done | bytes 532512 | tf_op jit(solution)/shard_map/ppermute | solution.py:429
  114.2 0.8 copy-done.11
  115.1 0.8 copy-done.12
  115.9 9.3 %shard_map.120 = (f32[224,2048]{1,0:T(8,128)}, bf16[512,2048]{1,0:T(8,128)(2,1)}) custom-call(s32[1]{0:T(128)} %bitcast.7.refs_0_, f32[520,256]{1,0:T(8,128)} %copy-done.4, f32[520,256]{1,0:T(8,128)} %collective-permute-done.5.refs_2_, f32[648,256]{1,0:T(8,128)} %copy-done.1, f32[648,256]{1,0:T(8,128)} %copy-done.11, f32[648,256]{1,0:T(8,128)} %copy-done.3, ...), custom_call_target="tpu_custom_call" | custom-call | flops 1879048192 | bytes 10485760 | tf_op jit(solution)/shard_map/pallas_call | solution.py:365
  125.3 8.8 %shard_map.118 = (bf16[512,128,256]{2,1,0:T(8,128)(2,1)}, bf16[512,128,256]{2,1,0:T(8,128)(2,1)}, f32[264,256]{1,0:T(8,128)}, f32[264,256]{1,0:T(8,128)}) custom-call(s32[3]{0:T(128)} %pad_add_fusion.scalars, s32[512]{0:T(512)} %lengths.7, bf16[512,2048]{1,0:T(8,128)(2,1)} %get-tuple-element.26.refs_0_, ...), custom_call_target="tpu_custom_call", output_to_operand_aliasing={{0}: (7, {}), {1}: (8, {})} | custom-call | flops 640000000 | bytes 16777216 | tf_op jit(solution)/shard_map/pallas_call | solution.py:263
  134.1 0.6 collective-permute-start.3
  134.7 1.4 collective-permute-done.3.two
  136.1 1.0 copy-done.10
  137.3 0.7 copy-done.6
  138.0 1.8 %collective-permute-start.4 = (f32[264,256]{1,0:T(8,128)S(1)}, f32[264,256]{1,0:T(8,128)S(1)}, u32[]{:S(2)}, u32[]{:S(2)}) collective-permute-start(f32[264,256]{1,0:T(8,128)S(1)} %shard_map.119.refs_1_), channel_id=1, source_target_pairs={{0,2},{2,0},{1,3},{3,1},{4,6},{6,4},{5,7},{7,5}} | collective-permute-start | bytes 811016 | tf_op jit(solution)/shard_map/ppermute | solution.py:429
  139.8 7.0 %collective-permute-done.4.refs_2_ = f32[264,256]{1,0:T(8,128)S(1)} collective-permute-done((f32[264,256]{1,0:T(8,128)S(1)}, f32[264,256]{1,0:T(8,128)S(1)}, u32[]{:S(2)}, u32[]{:S(2)}) %collective-permute-start.4) | collective-permute-done | bytes 270368 | tf_op jit(solution)/shard_map/ppermute | solution.py:429
  146.8 0.7 copy-done.13
  147.5 7.1 %shard_map.121 = (f32[32,2048]{1,0:T(8,128)}, bf16[512,2048]{1,0:T(8,128)(2,1)}) custom-call(s32[1]{0:T(128)} %bitcast.1.refs_0_, f32[264,256]{1,0:T(8,128)} %copy-done.6, f32[264,256]{1,0:T(8,128)} %copy-done.13, bf16[2048,2048]{1,0:T(8,128)(2,1)} %refs_3_.9, bf16[512,2048]{1,0:T(8,128)(2,1)} %hidden.3, ...), custom_call_target="tpu_custom_call", output_to_operand_aliasing={{1}: (5, {})} | custom-call | flops 268435456 | bytes 10485760 | tf_op jit(solution)/shard_map/pallas_call | solution.py:365
  154.7 1.6 copy-done
  156.3 1.4 shard_map.122._
  157.7 0.9 shard_map.123
  (29 shorter events, 1.5 us)
Async XLA Ops:
  26.0 2.6 %collective-permute-start = (f32[520,256]{1,0:T(8,128)}, f32[520,256]{1,0:T(8,128)S(1)}, u32[]{:S(2)}, u32[]{:S(2)}) collective-permute-start(f32[520,256]{1,0:T(8,128)} %get-tuple-element.32), channel_id=1, source_target_pairs={{0,1},{1,0},{2,3},{3,2},{4,5},{5,4},{6,7},{7,6}} | collective-permute-start | bytes 1597448 | tf_op jit(solution)/shard_map/ppermute | solution.py:427
  28.6 1.0 copy-start.9
  30.0 0.8 copy-start.4
  48.0 2.5 %collective-permute-start.1 = (f32[648,256]{1,0:T(8,128)}, f32[648,256]{1,0:T(8,128)S(1)}, u32[]{:S(2)}, u32[]{:S(2)}) collective-permute-start(f32[648,256]{1,0:T(8,128)} %get-tuple-element.36), channel_id=1, source_target_pairs={{0,1},{1,0},{2,3},{3,2},{4,5},{5,4},{6,7},{7,6}} | collective-permute-start | bytes 1990664 | tf_op jit(solution)/shard_map/ppermute | solution.py:427
  50.4 1.1 copy-start.8
  51.9 0.9 copy-start.1
  52.7 17.8 %copy-start.2 = (f32[648,256]{1,0:T(8,128)S(1)}, f32[648,256]{1,0:T(8,128)}, u32[]{:S(2)}) copy-start(f32[648,256]{1,0:T(8,128)} %copy-done.1) | copy-start | bytes 1990660
  52.8 24.0 %copy-start.5 = (f32[520,256]{1,0:T(8,128)S(1)}, f32[520,256]{1,0:T(8,128)}, u32[]{:S(2)}) copy-start(f32[520,256]{1,0:T(8,128)} %copy-done.4) | copy-start | bytes 1597444
  70.0 3.2 %collective-permute-start.2 = (f32[648,256]{1,0:T(8,128)}, f32[648,256]{1,0:T(8,128)S(1)}, u32[]{:S(2)}, u32[]{:S(2)}) collective-permute-start(f32[648,256]{1,0:T(8,128)} %get-tuple-element.40), channel_id=1, source_target_pairs={{0,1},{1,0},{2,3},{3,2},{4,5},{5,4},{6,7},{7,6}} | collective-permute-start | bytes 1990664 | tf_op jit(solution)/shard_map/ppermute | solution.py:427
  70.5 43.7 %collective-permute-start.6 = (f32[648,256]{1,0:T(8,128)S(1)}, f32[648,256]{1,0:T(8,128)S(1)}, u32[]{:S(2)}, u32[]{:S(2)}) collective-permute-start(f32[648,256]{1,0:T(8,128)S(1)} %copy-done.2), channel_id=1, source_target_pairs={{0,2},{2,0},{1,3},{3,1},{4,6},{6,4},{5,7},{7,5}} | collective-permute-start | bytes 1990664 | tf_op jit(solution)/shard_map/ppermute | solution.py:429
  73.2 1.1 copy-start.7
  74.7 41.2 %copy-start.3 = (f32[648,256]{1,0:T(8,128)}, f32[648,256]{1,0:T(8,128)S(1)}, u32[]{:S(2)}) copy-start(f32[648,256]{1,0:T(8,128)S(1)} %shard_map.117.refs_7_.refs_5_) | copy-start | bytes 1990660
  74.7 39.5 %collective-permute-start.7 = (f32[648,256]{1,0:T(8,128)S(1)}, f32[648,256]{1,0:T(8,128)S(1)}, u32[]{:S(2)}, u32[]{:S(2)}) collective-permute-start(f32[648,256]{1,0:T(8,128)S(1)} %shard_map.117.refs_7_.refs_5_), channel_id=1, source_target_pairs={{0,2},{2,0},{1,3},{3,1},{4,6},{6,4},{5,7},{7,5}} | collective-permute-start | bytes 1990664 | tf_op jit(solution)/shard_map/ppermute | solution.py:429
  76.7 37.5 %collective-permute-start.5 = (f32[520,256]{1,0:T(8,128)S(1)}, f32[520,256]{1,0:T(8,128)}, u32[]{:S(2)}, u32[]{:S(2)}) collective-permute-start(f32[520,256]{1,0:T(8,128)S(1)} %copy-done.5), channel_id=1, source_target_pairs={{0,2},{2,0},{1,3},{3,1},{4,6},{6,4},{5,7},{7,5}} | collective-permute-start | bytes 1597448 | tf_op jit(solution)/shard_map/ppermute | solution.py:429
  114.2 0.9 copy-start.11
  115.1 0.8 copy-start.12
  125.3 29.5 %collective-permute-start.9 = (f32[224,2048]{1,0:T(8,128)}, f32[224,2048]{1,0:T(8,128)S(1)}, u32[]{:S(2)}, u32[]{:S(2)}) collective-permute-start(f32[224,2048]{1,0:T(8,128)} %get-tuple-element.45), channel_id=1, source_target_pairs={{0,1},{1,0},{2,3},{3,2},{4,5},{5,4},{6,7},{7,6}} | collective-permute-start | bytes 5505032 | tf_op jit(solution)/shard_map/ppermute | solution.py:436
  134.1 2.0 %collective-permute-start.3 = (f32[264,256]{1,0:T(8,128)}, f32[264,256]{1,0:T(8,128)S(1)}, u32[]{:S(2)}, u32[]{:S(2)}) collective-permute-start(f32[264,256]{1,0:T(8,128)} %get-tuple-element.42), channel_id=1, source_target_pairs={{0,1},{1,0},{2,3},{3,2},{4,5},{5,4},{6,7},{7,6}} | collective-permute-start | bytes 811016 | tf_op jit(solution)/shard_map/ppermute | solution.py:427
  136.1 1.0 copy-start.10
  137.3 0.7 copy-start.6
  138.0 8.8 %collective-permute-start.4 = (f32[264,256]{1,0:T(8,128)S(1)}, f32[264,256]{1,0:T(8,128)S(1)}, u32[]{:S(2)}, u32[]{:S(2)}) collective-permute-start(f32[264,256]{1,0:T(8,128)S(1)} %shard_map.119.refs_1_), channel_id=1, source_target_pairs={{0,2},{2,0},{1,3},{3,1},{4,6},{6,4},{5,7},{7,5}} | collective-permute-start | bytes 811016 | tf_op jit(solution)/shard_map/ppermute | solution.py:429
  146.8 0.7 copy-start.13
  154.7 3.0 %collective-permute-start.8 = (f32[32,2048]{1,0:T(8,128)}, f32[32,2048]{1,0:T(8,128)S(1)}, u32[]{:S(2)}, u32[]{:S(2)}) collective-permute-start(f32[32,2048]{1,0:T(8,128)} %get-tuple-element.44), channel_id=1, source_target_pairs={{0,1},{1,0},{2,3},{3,2},{4,5},{5,4},{6,7},{7,6}} | collective-permute-start | bytes 786440 | tf_op jit(solution)/shard_map/ppermute | solution.py:438
  154.7 1.6 %copy-start = (bf16[512,2048]{1,0:T(8,128)(2,1)S(1)}, bf16[512,2048]{1,0:T(8,128)(2,1)}, u32[]{:S(2)}) copy-start(bf16[512,2048]{1,0:T(8,128)(2,1)} %hidden.3) | copy-start | bytes 6291460

commit v4 on v3

--- a/solution.py
+++ b/solution.py
@@ -25,7 +25,7 @@
     rows = hidden.shape[0]
     half = HEAD // 2
     tiles = ([pltpu.make_async_copy(w_k, narrow.at[0], sem.at[0]), pltpu.make_async_copy(w_v, narrow.at[1], sem.at[1])]
-             + [pltpu.make_async_copy(w_q.at[:, h * HEAD:(h + 1) * HEAD], wide.at[h], sem.at[2 + h]) for h in range(HEADS)])
+             + [pltpu.make_async_copy(w_q.at[h * HEAD:(h + 1) * HEAD], wide.at[h * HEAD:(h + 1) * HEAD], sem.at[2 + h]) for h in range(HEADS)])
     first = pltpu.make_async_copy(hidden, x, sem.at[2 + HEADS])
     first.start()
     for copy in tiles[:2]:
@@ -43,7 +43,6 @@
     first.wait()
     for copy in tiles[2:]:
         copy.start()
-    start_more()
 
     def norm(i, carry):
         at = pl.ds(pl.multiple_of(i * 32, 32), 32)
@@ -65,10 +64,13 @@
     k_rows[...] = rotated(product(narrow[0])).astype(jnp.bfloat16).astype(jnp.float32)
     tiles[1].wait()
     v_rows[...] = product(narrow[1])
+    start_more()
+    for copy in tiles[2:]:
+        copy.wait()
 
     def head(h, carry):
-        pltpu.make_async_copy(w_k, wide.at[h], sem.at[2 + h]).wait()
-        q_rows[:, pl.ds(pl.multiple_of(h * HEAD, HEAD), HEAD)] = (rotated(product(wide[h])) * HEAD ** -0.5).astype(jnp.bfloat16)
+        at = pl.ds(pl.multiple_of(h * HEAD, HEAD), HEAD)
+        q_rows[:, at] = (rotated(product(wide[:, at])) * HEAD ** -0.5).astype(jnp.bfloat16)
         return carry
 
     lax.fori_loop(0, HEADS, head, 0)
@@ -249,7 +251,7 @@
         saved = [jax.ShapeDtypeStruct((all_rows, HEADS * HEAD), jnp.bfloat16)] + [jax.ShapeDtypeStruct((all_rows, HEAD), jnp.float32)] * 2
         shapes += saved
         half_row = pltpu.VMEM((all_rows, HEAD // 2), jnp.float32)
-        scratch += [pltpu.SemaphoreType.DMA((3,)), pltpu.VMEM((all_rows, dim), jnp.bfloat16), pltpu.VMEM((HEADS, dim, HEAD), jnp.bfloat16),
+        scratch += [pltpu.SemaphoreType.DMA((3,)), pltpu.VMEM((all_rows, dim), jnp.bfloat16), pltpu.VMEM((dim, HEADS * HEAD), jnp.bfloat16),
                     pltpu.VMEM((2, dim, HEAD), jnp.bfloat16), pltpu.VMEM((all_rows, dim), jnp.bfloat16), half_row, half_row,
                     *(pltpu.VMEM(a.shape, a.dtype) for a in saved), pltpu.SemaphoreType.DMA((3 + HEADS,))]
         operands = [scalars, lengths, *tokens, k_block, v_block]
@@ -315,14 +317,12 @@
     total = sum(chunks)
     tiles = y.shape[1] // HEAD
 
-    def tile_load(n):
-        at = pl.ds(pl.multiple_of(n * HEAD, HEAD), HEAD)
-        return pltpu.make_async_copy(w_o.at[:, at], weights.at[n], sem.at[2 + n])
-
+    loads = [pltpu.make_async_copy(w_o.at[n * HEAD:(n + 1) * HEAD], weights.at[n * HEAD:(n + 1) * HEAD], sem.at[2 + n])
+             for n in range(w_o.shape[0] // HEAD)]
     load = pltpu.make_async_copy(hidden.at[pl.ds(row0, total)], x, sem.at[0])
     load.start()
-    for n in range(3):
-        tile_load(n).start()
+    for copy in loads:
+        copy.start()
     order = reorder(False)
     first = 0
     for i, rows in enumerate(chunks):
@@ -337,17 +337,13 @@
                 attended[first + g * GROUP:first + (g + 1) * GROUP, h * HEAD:(h + 1) * HEAD] = by_head[h * GROUP:(h + 1) * GROUP]
         first += rows
     load.wait()
+    for copy in loads:
+        copy.wait()
 
     @pl.loop(0, tiles)
     def _(n):
         at = pl.ds(pl.multiple_of(n * HEAD, HEAD), HEAD)
-        tile_load(n).wait()
-
-        @pl.when(n + 3 < tiles)
-        def _():
-            tile_load(n + 3).start()
-
-        value = jnp.dot(attended[...], weights[n], preferred_element_type=jnp.float32)
+        value = jnp.dot(attended[...], weights[:, at], preferred_element_type=jnp.float32)
         y[:, at] = value
         done[:, at] = (x[:, at].astype(jnp.float32) + value).astype(jnp.bfloat16)
 
@@ -368,9 +364,9 @@
         in_specs=[SMEM] + [VMEM] * len(parts) + [HBM, HBM] + [HBM] * late,
         out_specs=specs,
         input_output_aliases={len(parts) + 3: 1} if late else {},
-        scratch_shapes=[pltpu.VMEM((dim // HEAD, w_o.shape[0], HEAD), jnp.bfloat16),
+        scratch_shapes=[pltpu.VMEM(w_o.shape, w_o.dtype),
                         pltpu.VMEM((total, w_o.shape[0]), jnp.bfloat16), pltpu.VMEM((total, dim), jnp.bfloat16),
-                        pltpu.VMEM((total, dim), jnp.bfloat16), pltpu.SemaphoreType.DMA((2 + dim // HEAD,))],
+                        pltpu.VMEM((total, dim), jnp.bfloat16), pltpu.SemaphoreType.DMA((2 + w_o.shape[0] // HEAD,))],
         compiler_params=pltpu.CompilerParams(vmem_limit_bytes=62 << 20),
         cost_estimate=pl.CostEstimate(flops=2 * total * w_o.shape[0] * dim, bytes_accessed=10 << 20, transcendentals=0),
     )(row0, *parts, w_o, hidden, *([out] if late else []))

time: 159 us -> 162 us (1.019)
  Pallas kernels: 88 us -> 91.5 us
    pallas_call x2, Pallas kernels: 16.5 us -> 19.8 us  [finish_call(): pl.pallas_call(functools.partial(finish_kernel, chunks, late), out_shape=...]
  transfers between devices with their start and end apart: 10 -> 10, of which waited for: 5 -> 5; matrix products, arithmetic and copies ran while one was open for 0% -> 0% of each run, Pallas kernels for 11% -> 12%
where the time goes in v4:
time: 162 us
  Pallas kernels  91.5 us (56%)
  waiting for transfers between devices  49.6 us (31%)
  local copies, waits for them, and re-layouts  10.5 us (6%)
  starting transfers between devices  9.04 us (6%)
    pallas_call x4, Pallas kernels, attention_call(): pl.pallas_call(functools.partial(attention_kernel, first_row, groups, mod...  68.2 us
    ppermute x4, waiting for transfers between devices, local_step(): theirs.append(lax.ppermute(merged[-1], 'sp', across))  44.5 us
    pallas_call x2, Pallas kernels, finish_call(): pl.pallas_call(functools.partial(finish_kernel, chunks, late), out_shape=...  19.8 us
    unnamed x28, local copies, waits for them, and re-layouts  10.5 us
    ppermute x4, starting transfers between devices, local_step(): theirs.append(lax.ppermute(merged[-1], 'sp', across))  6.46 us
    ppermute x4, waiting for transfers between devices, local_step(): taken = lax.ppermute(sent, 'sp', sibling)  5.09 us
  transfers between devices with their start and end apart: 10, of which 5 were waited for; matrix products, arithmetic and copies ran while one was open for 0% of the time, Pallas kernels for 12%

profile of v4, /device:TPU:0, one launch (start us, length us, event | category | flops | bytes accessed | tf_op | source)
XLA Modules:
  0.0 162.1 jit_solution(16440024631433575791)
XLA Ops:
  0.6 0.6 pad_add_fusion.scalars
  1.2 25.0 %shard_map.112 = (bf16[512,128,256]{2,1,0:T(8,128)(2,1)}, bf16[512,128,256]{2,1,0:T(8,128)(2,1)}, f32[520,256]{1,0:T(8,128)}, f32[520,256]{1,0:T(8,128)}, bf16[5...) custom-call(s32[3]{0:T(128)} %pad_add_fusion.scalars, s32[512]{0:T(512)} %lengths.7, ...), custom_call_target="tpu_custom_call" | custom-call | flops 1280000000 | bytes 33554432 | tf_op jit(solution)/shard_map/pallas_call | solution.py:265
  26.2 0.8 collective-permute-start
  27.1 1.8 %collective-permute-done.two = f32[520,256]{1,0:T(8,128)S(1)} collective-permute-done((f32[520,256]{1,0:T(8,128)}, f32[520,256]{1,0:T(8,128)S(1)}, u32[]{:S(2)}, u32[]{:S(2)}) %collective-permute-start) | collective-permute-done | bytes 532512 | tf_op jit(solution)/shard_map/ppermute | solution.py:423
  28.8 1.0 copy-done.9
  30.2 0.8 copy-done.4
  31.0 17.2 %shard_map.114 = (bf16[512,128,256]{2,1,0:T(8,128)(2,1)}, bf16[512,128,256]{2,1,0:T(8,128)(2,1)}, f32[648,256]{1,0:T(8,128)}, f32[648,256]{1,0:T(8,128)}) custom-call(s32[3]{0:T(128)} %pad_add_fusion.scalars, s32[512]{0:T(512)} %lengths.7, bf16[512,2048]{1,0:T(8,128)(2,1)} %get-tuple-element.26.refs_0_, ...), custom_call_target="tpu_custom_call", output_to_operand_aliasing={{0}: (7, {}), {1}: (8, {})} | custom-call | flops 1600000000 | bytes 41943040 | tf_op jit(solution)/shard_map/pallas_call | solution.py:265
  48.2 0.5 collective-permute-start.1
  48.7 1.9 %collective-permute-done.1.two = f32[648,256]{1,0:T(8,128)S(1)} collective-permute-done((f32[648,256]{1,0:T(8,128)}, f32[648,256]{1,0:T(8,128)S(1)}, u32[]{:S(2)}, u32[]{:S(2)}) %collective-permute-start.1) | collective-permute-done | bytes 663584 | tf_op jit(solution)/shard_map/ppermute | solution.py:423
  50.6 1.1 copy-done.8
  52.1 0.9 copy-done.1
  53.0 17.2 %shard_map.116 = (bf16[512,128,256]{2,1,0:T(8,128)(2,1)}, bf16[512,128,256]{2,1,0:T(8,128)(2,1)}, f32[648,256]{1,0:T(8,128)}, f32[648,256]{1,0:T(8,128)}) custom-call(s32[3]{0:T(128)} %pad_add_fusion.scalars, s32[512]{0:T(512)} %lengths.7, bf16[512,2048]{1,0:T(8,128)(2,1)} %get-tuple-element.26.refs_0_, ...), custom_call_target="tpu_custom_call", output_to_operand_aliasing={{0}: (7, {}), {1}: (8, {})} | custom-call | flops 1600000000 | bytes 41943040 | tf_op jit(solution)/shard_map/pallas_call | solution.py:265
  70.2 0.6 collective-permute-start.2
  70.8 2.6 %collective-permute-start.6 = (f32[648,256]{1,0:T(8,128)S(1)}, f32[648,256]{1,0:T(8,128)S(1)}, u32[]{:S(2)}, u32[]{:S(2)}) collective-permute-start(f32[648,256]{1,0:T(8,128)S(1)} %copy-done.2), channel_id=1, source_target_pairs={{0,2},{2,0},{1,3},{3,1},{4,6},{6,4},{5,7},{7,5}} | collective-permute-start | bytes 1990664 | tf_op jit(solution)/shard_map/ppermute | solution.py:425
  73.4 1.1 copy-done.7
  74.9 2.0 %collective-permute-start.7 = (f32[648,256]{1,0:T(8,128)S(1)}, f32[648,256]{1,0:T(8,128)S(1)}, u32[]{:S(2)}, u32[]{:S(2)}) collective-permute-start(f32[648,256]{1,0:T(8,128)S(1)} %shard_map.117.refs_7_.refs_5_), channel_id=1, source_target_pairs={{0,2},{2,0},{1,3},{3,1},{4,6},{6,4},{5,7},{7,5}} | collective-permute-start | bytes 1990664 | tf_op jit(solution)/shard_map/ppermute | solution.py:425
  76.9 37.5 %collective-permute-done.5.refs_2_ = f32[520,256]{1,0:T(8,128)} collective-permute-done((f32[520,256]{1,0:T(8,128)S(1)}, f32[520,256]{1,0:T(8,128)}, u32[]{:S(2)}, u32[]{:S(2)}) %collective-permute-start.5) | collective-permute-done | bytes 532512 | tf_op jit(solution)/shard_map/ppermute | solution.py:425
  114.4 0.8 copy-done.11
  115.3 0.8 copy-done.12
  116.1 11.4 %shard_map.120 = (f32[224,2048]{1,0:T(8,128)}, bf16[512,2048]{1,0:T(8,128)(2,1)}) custom-call(s32[1]{0:T(128)} %bitcast.7.refs_0_, f32[520,256]{1,0:T(8,128)} %copy-done.4, f32[520,256]{1,0:T(8,128)} %collective-permute-done.5.refs_2_, f32[648,256]{1,0:T(8,128)} %copy-done.1, f32[648,256]{1,0:T(8,128)} %copy-done.11, f32[648,256]{1,0:T(8,128)} %copy-done.3, ...), custom_call_target="tpu_custom_call" | custom-call | flops 1879048192 | bytes 10485760 | tf_op jit(solution)/shard_map/pallas_call | solution.py:361
  127.6 8.8 %shard_map.118 = (bf16[512,128,256]{2,1,0:T(8,128)(2,1)}, bf16[512,128,256]{2,1,0:T(8,128)(2,1)}, f32[264,256]{1,0:T(8,128)}, f32[264,256]{1,0:T(8,128)}) custom-call(s32[3]{0:T(128)} %pad_add_fusion.scalars, s32[512]{0:T(512)} %lengths.7, bf16[512,2048]{1,0:T(8,128)(2,1)} %get-tuple-element.26.refs_0_, ...), custom_call_target="tpu_custom_call", output_to_operand_aliasing={{0}: (7, {}), {1}: (8, {})} | custom-call | flops 640000000 | bytes 16777216 | tf_op jit(solution)/shard_map/pallas_call | solution.py:265
  136.3 0.6 collective-permute-start.3
  137.0 1.4 collective-permute-done.3.two
  138.3 1.0 copy-done.10
  139.6 0.7 copy-done.6
  140.3 1.8 %collective-permute-start.4 = (f32[264,256]{1,0:T(8,128)S(1)}, f32[264,256]{1,0:T(8,128)S(1)}, u32[]{:S(2)}, u32[]{:S(2)}) collective-permute-start(f32[264,256]{1,0:T(8,128)S(1)} %shard_map.119.refs_1_), channel_id=1, source_target_pairs={{0,2},{2,0},{1,3},{3,1},{4,6},{6,4},{5,7},{7,5}} | collective-permute-start | bytes 811016 | tf_op jit(solution)/shard_map/ppermute | solution.py:425
  142.0 7.0 %collective-permute-done.4.refs_2_ = f32[264,256]{1,0:T(8,128)S(1)} collective-permute-done((f32[264,256]{1,0:T(8,128)S(1)}, f32[264,256]{1,0:T(8,128)S(1)}, u32[]{:S(2)}, u32[]{:S(2)}) %collective-permute-start.4) | collective-permute-done | bytes 270368 | tf_op jit(solution)/shard_map/ppermute | solution.py:425
  149.1 0.7 copy-done.13
  149.8 8.4 %shard_map.121 = (f32[32,2048]{1,0:T(8,128)}, bf16[512,2048]{1,0:T(8,128)(2,1)}) custom-call(s32[1]{0:T(128)} %bitcast.1.refs_0_, f32[264,256]{1,0:T(8,128)} %copy-done.6, f32[264,256]{1,0:T(8,128)} %copy-done.13, bf16[2048,2048]{1,0:T(8,128)(2,1)} %refs_3_.9, bf16[512,2048]{1,0:T(8,128)(2,1)} %hidden.3, ...), custom_call_target="tpu_custom_call", output_to_operand_aliasing={{1}: (5, {})} | custom-call | flops 268435456 | bytes 10485760 | tf_op jit(solution)/shard_map/pallas_call | solution.py:361
  158.2 1.6 copy-done
  159.8 1.4 shard_map.122._
  161.2 0.9 shard_map.123
  (29 shorter events, 1.5 us)
Async XLA Ops:
  26.2 2.6 %collective-permute-start = (f32[520,256]{1,0:T(8,128)}, f32[520,256]{1,0:T(8,128)S(1)}, u32[]{:S(2)}, u32[]{:S(2)}) collective-permute-start(f32[520,256]{1,0:T(8,128)} %get-tuple-element.32), channel_id=1, source_target_pairs={{0,1},{1,0},{2,3},{3,2},{4,5},{5,4},{6,7},{7,6}} | collective-permute-start | bytes 1597448 | tf_op jit(solution)/shard_map/ppermute | solution.py:423
  28.8 1.0 copy-start.9
  30.2 0.8 copy-start.4
  48.2 2.5 %collective-permute-start.1 = (f32[648,256]{1,0:T(8,128)}, f32[648,256]{1,0:T(8,128)S(1)}, u32[]{:S(2)}, u32[]{:S(2)}) collective-permute-start(f32[648,256]{1,0:T(8,128)} %get-tuple-element.36), channel_id=1, source_target_pairs={{0,1},{1,0},{2,3},{3,2},{4,5},{5,4},{6,7},{7,6}} | collective-permute-start | bytes 1990664 | tf_op jit(solution)/shard_map/ppermute | solution.py:423
  50.6 1.1 copy-start.8
  52.1 0.9 copy-start.1
  53.0 17.8 %copy-start.2 = (f32[648,256]{1,0:T(8,128)S(1)}, f32[648,256]{1,0:T(8,128)}, u32[]{:S(2)}) copy-start(f32[648,256]{1,0:T(8,128)} %copy-done.1) | copy-start | bytes 1990660
  53.0 23.9 %copy-start.5 = (f32[520,256]{1,0:T(8,128)S(1)}, f32[520,256]{1,0:T(8,128)}, u32[]{:S(2)}) copy-start(f32[520,256]{1,0:T(8,128)} %copy-done.4) | copy-start | bytes 1597444
  70.2 3.2 %collective-permute-start.2 = (f32[648,256]{1,0:T(8,128)}, f32[648,256]{1,0:T(8,128)S(1)}, u32[]{:S(2)}, u32[]{:S(2)}) collective-permute-start(f32[648,256]{1,0:T(8,128)} %get-tuple-element.40), channel_id=1, source_target_pairs={{0,1},{1,0},{2,3},{3,2},{4,5},{5,4},{6,7},{7,6}} | collective-permute-start | bytes 1990664 | tf_op jit(solution)/shard_map/ppermute | solution.py:423
  70.8 43.6 %collective-permute-start.6 = (f32[648,256]{1,0:T(8,128)S(1)}, f32[648,256]{1,0:T(8,128)S(1)}, u32[]{:S(2)}, u32[]{:S(2)}) collective-permute-start(f32[648,256]{1,0:T(8,128)S(1)} %copy-done.2), channel_id=1, source_target_pairs={{0,2},{2,0},{1,3},{3,1},{4,6},{6,4},{5,7},{7,5}} | collective-permute-start | bytes 1990664 | tf_op jit(solution)/shard_map/ppermute | solution.py:425
  73.4 1.1 copy-start.7
  74.9 41.2 %copy-start.3 = (f32[648,256]{1,0:T(8,128)}, f32[648,256]{1,0:T(8,128)S(1)}, u32[]{:S(2)}) copy-start(f32[648,256]{1,0:T(8,128)S(1)} %shard_map.117.refs_7_.refs_5_) | copy-start | bytes 1990660
  74.9 39.5 %collective-permute-start.7 = (f32[648,256]{1,0:T(8,128)S(1)}, f32[648,256]{1,0:T(8,128)S(1)}, u32[]{:S(2)}, u32[]{:S(2)}) collective-permute-start(f32[648,256]{1,0:T(8,128)S(1)} %shard_map.117.refs_7_.refs_5_), channel_id=1, source_target_pairs={{0,2},{2,0},{1,3},{3,1},{4,6},{6,4},{5,7},{7,5}} | collective-permute-start | bytes 1990664 | tf_op jit(solution)/shard_map/ppermute | solution.py:425
  76.9 37.5 %collective-permute-start.5 = (f32[520,256]{1,0:T(8,128)S(1)}, f32[520,256]{1,0:T(8,128)}, u32[]{:S(2)}, u32[]{:S(2)}) collective-permute-start(f32[520,256]{1,0:T(8,128)S(1)} %copy-done.5), channel_id=1, source_target_pairs={{0,2},{2,0},{1,3},{3,1},{4,6},{6,4},{5,7},{7,5}} | collective-permute-start | bytes 1597448 | tf_op jit(solution)/shard_map/ppermute | solution.py:425
  114.4 0.9 copy-start.11
  115.3 0.8 copy-start.12
  127.5 30.7 %collective-permute-start.9 = (f32[224,2048]{1,0:T(8,128)}, f32[224,2048]{1,0:T(8,128)S(1)}, u32[]{:S(2)}, u32[]{:S(2)}) collective-permute-start(f32[224,2048]{1,0:T(8,128)} %get-tuple-element.45), channel_id=1, source_target_pairs={{0,1},{1,0},{2,3},{3,2},{4,5},{5,4},{6,7},{7,6}} | collective-permute-start | bytes 5505032 | tf_op jit(solution)/shard_map/ppermute | solution.py:432
  136.3 2.0 %collective-permute-start.3 = (f32[264,256]{1,0:T(8,128)}, f32[264,256]{1,0:T(8,128)S(1)}, u32[]{:S(2)}, u32[]{:S(2)}) collective-permute-start(f32[264,256]{1,0:T(8,128)} %get-tuple-element.42), channel_id=1, source_target_pairs={{0,1},{1,0},{2,3},{3,2},{4,5},{5,4},{6,7},{7,6}} | collective-permute-start | bytes 811016 | tf_op jit(solution)/shard_map/ppermute | solution.py:423
  138.3 1.0 copy-start.10
  139.6 0.7 copy-start.6
  140.3 8.8 %collective-permute-start.4 = (f32[264,256]{1,0:T(8,128)S(1)}, f32[264,256]{1,0:T(8,128)S(1)}, u32[]{:S(2)}, u32[]{:S(2)}) collective-permute-start(f32[264,256]{1,0:T(8,128)S(1)} %shard_map.119.refs_1_), channel_id=1, source_target_pairs={{0,2},{2,0},{1,3},{3,1},{4,6},{6,4},{5,7},{7,5}} | collective-permute-start | bytes 811016 | tf_op jit(solution)/shard_map/ppermute | solution.py:425
  149.0 0.7 copy-start.13
  158.1 3.0 %collective-permute-start.8 = (f32[32,2048]{1,0:T(8,128)}, f32[32,2048]{1,0:T(8,128)S(1)}, u32[]{:S(2)}, u32[]{:S(2)}) collective-permute-start(f32[32,2048]{1,0:T(8,128)} %get-tuple-element.44), channel_id=1, source_target_pairs={{0,1},{1,0},{2,3},{3,2},{4,5},{5,4},{6,7},{7,6}} | collective-permute-start | bytes 786440 | tf_op jit(solution)/shard_map/ppermute | solution.py:434
  158.2 1.6 copy-start

commit v5 on v4

--- a/solution.py
+++ b/solution.py
@@ -14,7 +14,7 @@
 HEAD = 256
 GROUP = 16
 LOWEST = float(jnp.finfo(jnp.float32).min)
-CHUNKS = (64, 80, 80, 32)
+CHUNKS = (64, 80, 64, 48)
 HBM = pl.BlockSpec(memory_space=pltpu.HBM)
 ANY = pl.BlockSpec(memory_space=pl.ANY)
 VMEM = pl.BlockSpec(memory_space=pltpu.VMEM)
@@ -129,7 +129,7 @@
     kbuf, vbuf, in_sem, out_sem = take(4)
     depth, _, slots, _ = kbuf.shape
     total_groups = 2 * groups
-    ahead = min(5, total_groups)
+    ahead = min(8 if mode == 'first' else 5, total_groups)
 
     def row_of(g):
         return pl.multiple_of(jnp.where(g < groups, starts[0] + g * GROUP, starts[1] + (g - groups) * GROUP), GROUP)
@@ -306,106 +306,147 @@
     )(one, two)
 
 
-def finish_kernel(chunks, late, *refs):
+def tail_kernel(chunks, late, *refs):
     refs = list(refs)
-    row0 = pl.multiple_of(refs.pop(0)[0], GROUP)
-    parts = refs[:2 * len(chunks)]
-    w_o, hidden = refs[2 * len(chunks):2 * len(chunks) + 2]
-    rest = refs[2 * len(chunks) + 2 + late:]
-    y, out = rest[:2]
-    weights, attended, x, done, sem = rest[-5:]
-    total = sum(chunks)
-    tiles = y.shape[1] // HEAD
-
-    loads = [pltpu.make_async_copy(w_o.at[n * HEAD:(n + 1) * HEAD], weights.at[n * HEAD:(n + 1) * HEAD], sem.at[2 + n])
-             for n in range(w_o.shape[0] // HEAD)]
-    load = pltpu.make_async_copy(hidden.at[pl.ds(row0, total)], x, sem.at[0])
-    load.start()
-    for copy in loads:
+    take = lambda n: [refs.pop(0) for _ in range(n)]
+    kept, sent = take(2)
+    pairs = take(2 * len(chunks))
+    w_o, hidden = take(2)
+    out, = take(1)
+    near_buf, kept_buf, merged, far_buf, one, two, weights, x, attended, y_early, y_late, got_early, got_late = take(13)
+    local_sem, send_sem, recv_sem, tile_send, tile_recv = take(5)
+    early = sum(chunks)
+    half = early + late
+    tiles = weights.shape[1] // HEAD
+    me = lax.axis_index('sp')
+    core = lax.rem(me, 2)
+    group = lax.axis_index('dp')
+    sibling, across = (group, me + 1 - 2 * core), (group, lax.rem(me + 2, 4))
+    remote = functools.partial(pltpu.make_async_remote_copy, device_id_type=pl.DeviceIdType.MESH)
+
+    load_kept = pltpu.make_async_copy(kept, kept_buf, local_sem.at[0])
+    load_kept.start()
+    barrier = pltpu.get_barrier_semaphore()
+    for device in (sibling, across):
+        pl.semaphore_signal(barrier, inc=1, device_id=device, device_id_type=pl.DeviceIdType.MESH)
+    pl.semaphore_wait(barrier, 2)
+    near = remote(src_ref=sent, dst_ref=near_buf, send_sem=send_sem.at[0], recv_sem=recv_sem.at[0], device_id=sibling)
+    near.start()
+    loads, starts, at = [], [], 0
+    for i, rows in enumerate(chunks):
+        size = rows * HEADS + 8
+        starts.append(at)
+        for j, buf in enumerate((one, two)):
+            loads.append(pltpu.make_async_copy(pairs[2 * i + j], buf.at[at:at + size], local_sem.at[1 + 2 * i + j]))
+        at += size
+    load_x = pltpu.make_async_copy(hidden, x, local_sem.at[1 + 2 * len(chunks)])
+    load_w = pltpu.make_async_copy(w_o, weights, local_sem.at[2 + 2 * len(chunks)])
+    for copy in (*loads, load_w, load_x):
         copy.start()
     order = reorder(False)
-    first = 0
-    for i, rows in enumerate(chunks):
+
+    def attend_rows(first, rows, a, b):
         groups = rows // GROUP
-        one, two = parts[2 * i], parts[2 * i + 1]
-        columns, _, _ = merge_scales(one, two, groups, True)
+        columns, _, _ = merge_scales(a, b, groups, True)
         for g in range(groups):
-            at = pl.ds(g * 128, 128)
-            value = one[at, :] * columns[:, g:g + 1] + two[at, :] * columns[:, 8 + g:9 + g]
+            part = pl.ds(g * 128, 128)
+            value = a[part, :] * columns[:, g:g + 1] + b[part, :] * columns[:, 8 + g:9 + g]
             by_head = jnp.dot(order, value.astype(jnp.bfloat16), preferred_element_type=jnp.float32).astype(jnp.bfloat16)
             for h in range(HEADS):
                 attended[first + g * GROUP:first + (g + 1) * GROUP, h * HEAD:(h + 1) * HEAD] = by_head[h * GROUP:(h + 1) * GROUP]
-        first += rows
-    load.wait()
-    for copy in loads:
-        copy.wait()
-
-    @pl.loop(0, tiles)
-    def _(n):
-        at = pl.ds(pl.multiple_of(n * HEAD, HEAD), HEAD)
-        value = jnp.dot(attended[...], weights[:, at], preferred_element_type=jnp.float32)
-        y[:, at] = value
-        done[:, at] = (x[:, at].astype(jnp.float32) + value).astype(jnp.bfloat16)
-
-    save = pltpu.make_async_copy(done, out.at[pl.ds(row0, total)], sem.at[1])
-    save.start()
-    save.wait()
-
-
-def finish_call(chunks, row0, parts, w_o, hidden, out):
-    total = sum(chunks)
-    dim = w_o.shape[1]
-    late = out is not None
-    shapes = (jax.ShapeDtypeStruct((total, dim), jnp.float32), jax.ShapeDtypeStruct(hidden.shape, hidden.dtype))
-    specs = (VMEM, HBM)
+
+    def early_rows(i):
+        loads[2 * i].wait()
+        loads[2 * i + 1].wait()
+        size = chunks[i] * HEADS + 8
+        view = pl.ds(starts[i], size)
+        attend_rows(sum(chunks[:i]), chunks[i], one.at[view], two.at[view])
+
+    load_kept.wait()
+    near.wait_recv()
+    merge_kernel(late // GROUP, kept_buf, near_buf, merged)
+    early_rows(0)
+    far = remote(src_ref=merged, dst_ref=far_buf, send_sem=send_sem.at[1], recv_sem=recv_sem.at[1], device_id=across)
+    far.start()
+    for i in range(1, len(chunks)):
+        early_rows(i)
+    load_w.wait()
+
+    def tile_copy(n):
+        return remote(src_ref=y_early.at[n], dst_ref=got_early.at[n], send_sem=tile_send.at[n], recv_sem=tile_recv.at[n], device_id=sibling)
+
+    def early_tile(n, carry):
+        columns = pl.ds(pl.multiple_of(n * HEAD, HEAD), HEAD)
+        y_early[n] = jnp.dot(attended[:early, :], weights[:, columns], preferred_element_type=jnp.float32)
+
+        @pl.when(n > 0)
+        def _():
+            tile_copy(n - 1).start()
+
+        return carry
+
+    lax.fori_loop(0, tiles, early_tile, 0)
+    load_x.wait()
+
+    def add_rows(base, count, tile_of):
+        def step(i, carry):
+            rows = pl.ds(pl.multiple_of(base + i * GROUP, GROUP), GROUP)
+            for n in range(tiles):
+                columns = slice(n * HEAD, (n + 1) * HEAD)
+                out[rows, columns] = (x[rows, columns].astype(jnp.float32) + tile_of(n, pl.ds(pl.multiple_of(i * GROUP, GROUP), GROUP))).astype(jnp.bfloat16)
+            return carry
+
+        lax.fori_loop(0, count // GROUP, step, 0)
+
+    mine, other = core * half, (1 - core) * half
+    add_rows(mine, early, lambda n, rows: y_early[n, rows, :])
+    tile_copy(tiles - 1).start()
+    for n in range(tiles):
+        tile_copy(n).wait_recv()
+    add_rows(other, early, lambda n, rows: got_early[n, rows, :])
+    far.wait_recv()
+    attend_rows(early, late, merged, far_buf)
+
+    def late_tile(n, carry):
+        columns = pl.ds(pl.multiple_of(n * HEAD, HEAD), HEAD)
+        y_late[n] = jnp.dot(attended[early:, :], weights[:, columns], preferred_element_type=jnp.float32)
+        return carry
+
+    lax.fori_loop(0, tiles, late_tile, 0)
+    add_rows(mine + early, late, lambda n, rows: y_late[n, rows, :])
+    swap = remote(src_ref=y_late, dst_ref=got_late, send_sem=send_sem.at[2], recv_sem=recv_sem.at[2], device_id=sibling)
+    swap.start()
+    near.wait_send()
+    far.wait_send()
+    for n in range(tiles):
+        tile_copy(n).wait_send()
+    swap.wait_recv()
+    add_rows(other + early, late, lambda n, rows: got_late[n, rows, :])
+    swap.wait_send()
+
+
+def tail_call(chunks, late, kept, sent, pairs, w_o, hidden):
+    early = sum(chunks)
+    tiles = w_o.shape[1] // HEAD
+    part = pltpu.VMEM(kept.shape, jnp.float32)
+    stacked = pltpu.VMEM((early * HEADS + 8 * len(chunks), HEAD), jnp.float32)
+    y_early, y_late = (pltpu.VMEM((tiles, rows, HEAD), jnp.float32) for rows in (early, late))
     return pl.pallas_call(
-        functools.partial(finish_kernel, chunks, late),
-        out_shape=shapes,
-        in_specs=[SMEM] + [VMEM] * len(parts) + [HBM, HBM] + [HBM] * late,
-        out_specs=specs,
-        input_output_aliases={len(parts) + 3: 1} if late else {},
-        scratch_shapes=[pltpu.VMEM(w_o.shape, w_o.dtype),
-                        pltpu.VMEM((total, w_o.shape[0]), jnp.bfloat16), pltpu.VMEM((total, dim), jnp.bfloat16),
-                        pltpu.VMEM((total, dim), jnp.bfloat16), pltpu.SemaphoreType.DMA((2 + w_o.shape[0] // HEAD,))],
-        compiler_params=pltpu.CompilerParams(vmem_limit_bytes=62 << 20),
-        cost_estimate=pl.CostEstimate(flops=2 * total * w_o.shape[0] * dim, bytes_accessed=10 << 20, transcendentals=0),
-    )(row0, *parts, w_o, hidden, *([out] if late else []))
-
-
-def place_kernel(row, y, hidden, _, out, x, done, sem):
-    rows = y.shape[0]
-    row0 = pl.multiple_of(row[0], GROUP)
-    load = pltpu.make_async_copy(hidden.at[pl.ds(row0, rows)], x, sem.at[0])
-    load.start()
-    load.wait()
-
-    @pl.loop(0, rows // GROUP)
-    def _(i):
-        at = pl.ds(pl.multiple_of(i * GROUP, GROUP), GROUP)
-        done[at, :] = (x[at, :].astype(jnp.float32) + y[at, :]).astype(jnp.bfloat16)
-
-    save = pltpu.make_async_copy(done, out.at[pl.ds(row0, rows)], sem.at[1])
-    save.start()
-    save.wait()
-
-
-def place_call(row0, y, hidden, out):
-    rows, dim = y.shape
-    return pl.pallas_call(
-        place_kernel,
-        out_shape=jax.ShapeDtypeStruct(out.shape, out.dtype),
-        in_specs=[SMEM, VMEM, HBM, HBM],
-        out_specs=HBM,
-        input_output_aliases={3: 0},
-        scratch_shapes=[pltpu.VMEM((rows, dim), jnp.bfloat16), pltpu.VMEM((rows, dim), jnp.bfloat16), pltpu.SemaphoreType.DMA((2,))],
-        compiler_params=pltpu.CompilerParams(vmem_limit_bytes=12 << 20),
-        cost_estimate=pl.CostEstimate(flops=rows * 2_000_000, bytes_accessed=rows * 16384, transcendentals=0),
-    )(row0, y, hidden, out)
+        functools.partial(tail_kernel, chunks, late),
+        out_shape=jax.ShapeDtypeStruct(hidden.shape, hidden.dtype),
+        in_specs=[HBM] * (4 + len(pairs)),
+        out_specs=VMEM,
+        scratch_shapes=[part, part, part, part, stacked, stacked, pltpu.VMEM(w_o.shape, w_o.dtype), pltpu.VMEM(hidden.shape, hidden.dtype),
+                        pltpu.VMEM((early + late, w_o.shape[0]), jnp.bfloat16), y_early, y_late, y_early, y_late,
+                        pltpu.SemaphoreType.DMA((3 + len(pairs),)), pltpu.SemaphoreType.DMA((3,)), pltpu.SemaphoreType.DMA((3,)),
+                        pltpu.SemaphoreType.DMA((tiles,)), pltpu.SemaphoreType.DMA((tiles,))],
+        compiler_params=pltpu.CompilerParams(vmem_limit_bytes=62 << 20, collective_id=0, has_side_effects=True),
+        cost_estimate=pl.CostEstimate(flops=4_000_000_000, bytes_accessed=20 << 20, transcendentals=0),
+        name="tail",
+    )(kept, sent, *pairs, w_o, hidden)
 
 
 def local_step(hidden, w_norm, w_q, w_k, w_v, w_o, k_block, v_block, cache_len):
-    num_rows = hidden.shape[0]
-    half = num_rows // 2
     slots = k_block.shape[1]
     me = lax.axis_index('sp')
     core = lax.rem(me, 2)
@@ -420,20 +461,14 @@
             first, rows, scalars, cache_len, tokens, k_block, v_block, outs, merged[-1] if merged else None)
         if i == 0:
             outs, (kept, sent), tokens = results[:2], results[2:4], results[4:]
+        if i == len(CHUNKS) - 1:
+            break
         taken = lax.ppermute(sent, 'sp', sibling)
         merged.append(merge_call(rows, kept, taken))
         theirs.append(lax.ppermute(merged[-1], 'sp', across))
         first += rows
-    early = [p for pair in list(zip(merged, theirs))[:-1] for p in pair]
-    late_first = half - CHUNKS[-1]
-    mine, other = core * half, (1 - core) * half
-    rows_of = lambda start: jnp.reshape(start, (1,)).astype(jnp.int32)
-    y_early, out = finish_call(CHUNKS[:-1], rows_of(mine), early, w_o, hidden, None)
-    other_early = lax.ppermute(y_early, 'sp', sibling)
-    y_late, out = finish_call(CHUNKS[-1:], rows_of(mine + late_first), [merged[-1], theirs[-1]], w_o, hidden, out)
-    other_late = lax.ppermute(y_late, 'sp', sibling)
-    out = place_call(rows_of(other), other_early, hidden, out)
-    out = place_call(rows_of(other + late_first), other_late, hidden, out)
+    pairs = [p for pair in zip(merged, theirs) for p in pair]
+    out = tail_call(CHUNKS[:-1], CHUNKS[-1], kept, sent, pairs, w_o, hidden)
     return out, outs[0], outs[1]
 
 

time: 162 us -> 132 us (0.81)
  waiting for transfers between devices: 49.6 us -> 26.7 us
  Pallas kernels: 91.5 us -> 88.7 us
  local copies, waits for them, and re-layouts: 10.5 us -> 7.96 us
  starting transfers between devices: 9.04 us -> 6.9 us
    ppermute x4 -> x3, waiting for transfers between devices: 44.5 us -> 23 us  [local_step(): theirs.append(lax.ppermute(merged[-1], 'sp', across))]
    unnamed x28 -> x17, local copies, waits for them, and re-layouts: 10.5 us -> 7.96 us
    pallas_call x4 -> x1, Pallas kernels: 22 us -> 20.3 us  [tail_call(): pl.pallas_call(functools.partial(tail_kernel, chunks, late), out_shape=ja...]
    ppermute x4 -> x3, starting transfers between devices: 6.46 us -> 4.72 us  [local_step(): theirs.append(lax.ppermute(merged[-1], 'sp', across))]
    ppermute x4 -> x3, waiting for transfers between devices: 5.09 us -> 3.71 us  [local_step(): taken = lax.ppermute(sent, 'sp', sibling)]
  transfers between devices with their start and end apart: 10 -> 6, of which waited for: 5 -> 4; matrix products, arithmetic and copies ran while one was open for 0% -> 0% of each run, Pallas kernels for 12% -> 9%
where the time goes in v5:
time: 132 us
  Pallas kernels  88.7 us (67%)
  waiting for transfers between devices  26.7 us (20%)
  local copies, waits for them, and re-layouts  7.96 us (6%)
  starting transfers between devices  6.9 us (5%)
    pallas_call x4, Pallas kernels, attention_call(): pl.pallas_call(functools.partial(attention_kernel, first_row, groups, mod...  67.4 us
    ppermute x3, waiting for transfers between devices, local_step(): theirs.append(lax.ppermute(merged[-1], 'sp', across))  23 us
    pallas_call x1, Pallas kernels, tail_call(): pl.pallas_call(functools.partial(tail_kernel, chunks, late), out_shape=ja...  20.3 us
    unnamed x17, local copies, waits for them, and re-layouts  7.96 us
    ppermute x3, starting transfers between devices, local_step(): theirs.append(lax.ppermute(merged[-1], 'sp', across))  4.72 us
    ppermute x3, waiting for transfers between devices, local_step(): taken = lax.ppermute(sent, 'sp', sibling)  3.71 us
  transfers between devices with their start and end apart: 6, of which 4 were waited for; matrix products, arithmetic and copies ran while one was open for 0% of the time, Pallas kernels for 9%

profile of v5, /device:TPU:0, one launch (start us, length us, event | category | flops | bytes accessed | tf_op | source)
XLA Modules:
  0.0 131.6 jit_solution(3087360241453379381)
XLA Ops:
  0.6 0.6 pad_add_fusion.scalars
  1.3 23.5 %shard_map.112 = (bf16[512,128,256]{2,1,0:T(8,128)(2,1)}, bf16[512,128,256]{2,1,0:T(8,128)(2,1)}, f32[520,256]{1,0:T(8,128)}, f32[520,256]{1,0:T(8,128)}, bf16[5...) custom-call(s32[3]{0:T(128)} %pad_add_fusion.scalars, s32[512]{0:T(512)} %lengths.7, ...), custom_call_target="tpu_custom_call" | custom-call | flops 1280000000 | bytes 33554432 | tf_op jit(solution)/shard_map/pallas_call | solution.py:265
  24.8 1.1 collective-permute-start
  25.9 1.8 %collective-permute-done.two = f32[520,256]{1,0:T(8,128)S(1)} collective-permute-done((f32[520,256]{1,0:T(8,128)}, f32[520,256]{1,0:T(8,128)S(1)}, u32[]{:S(2)}, u32[]{:S(2)}) %collective-permute-start) | collective-permute-done | bytes 532512 | tf_op jit(solution)/shard_map/ppermute | solution.py:466
  27.7 1.0 copy-done.7
  28.7 0.3 shard_map.113.refs_7_.refs_2_
  29.0 0.0 copy-start.2
  29.0 0.8 copy-done.2
  29.8 17.2 %shard_map.114 = (bf16[512,128,256]{2,1,0:T(8,128)(2,1)}, bf16[512,128,256]{2,1,0:T(8,128)(2,1)}, f32[648,256]{1,0:T(8,128)}, f32[648,256]{1,0:T(8,128)}) custom-call(s32[3]{0:T(128)} %pad_add_fusion.scalars, s32[512]{0:T(512)} %lengths.7, bf16[512,2048]{1,0:T(8,128)(2,1)} %get-tuple-element.22.refs_0_, ...), custom_call_target="tpu_custom_call", output_to_operand_aliasing={{0}: (7, {}), {1}: (8, {})} | custom-call | flops 1600000000 | bytes 41943040 | tf_op jit(solution)/shard_map/pallas_call | solution.py:265
  47.0 0.5 collective-permute-start.1
  47.5 1.9 %collective-permute-done.1.two = f32[648,256]{1,0:T(8,128)S(1)} collective-permute-done((f32[648,256]{1,0:T(8,128)}, f32[648,256]{1,0:T(8,128)S(1)}, u32[]{:S(2)}, u32[]{:S(2)}) %collective-permute-start.1) | collective-permute-done | bytes 663584 | tf_op jit(solution)/shard_map/ppermute | solution.py:466
  49.5 1.1 copy-done.5
  50.6 0.4 shard_map.115.refs_7_.refs_4_
  50.9 0.0 copy-start
  50.9 0.8 copy-done
  51.8 14.9 %shard_map.116 = (bf16[512,128,256]{2,1,0:T(8,128)(2,1)}, bf16[512,128,256]{2,1,0:T(8,128)(2,1)}, f32[520,256]{1,0:T(8,128)}, f32[520,256]{1,0:T(8,128)}) custom-call(s32[3]{0:T(128)} %pad_add_fusion.scalars, s32[512]{0:T(512)} %lengths.7, bf16[512,2048]{1,0:T(8,128)(2,1)} %get-tuple-element.22.refs_0_, ...), custom_call_target="tpu_custom_call", output_to_operand_aliasing={{0}: (7, {}), {1}: (8, {})} | custom-call | flops 1280000000 | bytes 33554432 | tf_op jit(solution)/shard_map/pallas_call | solution.py:265
  66.7 0.6 collective-permute-start.2
  67.3 0.0 copy-done.1
  67.3 2.7 %collective-permute-start.4 = (f32[648,256]{1,0:T(8,128)S(1)}, f32[648,256]{1,0:T(8,128)}, u32[]{:S(2)}, u32[]{:S(2)}) collective-permute-start(f32[648,256]{1,0:T(8,128)S(1)} %copy-done.1), channel_id=1, source_target_pairs={{0,2},{2,0},{1,3},{3,1},{4,6},{6,4},{5,7},{7,5}} | collective-permute-start | bytes 1990664 | tf_op jit(solution)/shard_map/ppermute | solution.py:468
  70.0 0.0 copy-done.3
  70.0 0.0 collective-permute-start.3
  70.0 0.0 collective-permute-done.2.two
  70.0 1.0 copy-done.6
  71.0 0.3 shard_map.117.refs_7_.refs_6_
  71.4 0.0 copy-start.4
  71.4 2.0 %collective-permute-start.5 = (f32[520,256]{1,0:T(8,128)S(1)}, f32[520,256]{1,0:T(8,128)}, u32[]{:S(2)}, u32[]{:S(2)}) collective-permute-start(f32[520,256]{1,0:T(8,128)S(1)} %shard_map.117.refs_7_.refs_6_), channel_id=1, source_target_pairs={{0,2},{2,0},{1,3},{3,1},{4,6},{6,4},{5,7},{7,5}} | collective-permute-start | bytes 1597448 | tf_op jit(solution)/shard_map/ppermute | solution.py:468
  73.4 11.7 %shard_map.118 = (bf16[512,128,256]{2,1,0:T(8,128)(2,1)}, bf16[512,128,256]{2,1,0:T(8,128)(2,1)}, f32[392,256]{1,0:T(8,128)}, f32[392,256]{1,0:T(8,128)}) custom-call(s32[3]{0:T(128)} %pad_add_fusion.scalars, s32[512]{0:T(512)} %lengths.7, bf16[512,2048]{1,0:T(8,128)(2,1)} %get-tuple-element.22.refs_0_, ...), custom_call_target="tpu_custom_call", output_to_operand_aliasing={{0}: (7, {}), {1}: (8, {})} | custom-call | flops 960000000 | bytes 25165824 | tf_op jit(solution)/shard_map/pallas_call | solution.py:265
  85.1 12.1 %collective-permute-done.3.refs_3_ = f32[520,256]{1,0:T(8,128)} collective-permute-done((f32[520,256]{1,0:T(8,128)S(1)}, f32[520,256]{1,0:T(8,128)}, u32[]{:S(2)}, u32[]{:S(2)}) %collective-permute-start.3) | collective-permute-done | bytes 532512 | tf_op jit(solution)/shard_map/ppermute | solution.py:468
  97.2 0.0 collective-permute-done.4.refs_5_
  97.2 10.9 %collective-permute-done.5.refs_7_ = f32[520,256]{1,0:T(8,128)} collective-permute-done((f32[520,256]{1,0:T(8,128)S(1)}, f32[520,256]{1,0:T(8,128)}, u32[]{:S(2)}, u32[]{:S(2)}) %collective-permute-start.5) | collective-permute-done | bytes 532512 | tf_op jit(solution)/shard_map/ppermute | solution.py:468
  108.2 20.3 %tail.1 = bf16[512,2048]{1,0:T(8,128)(2,1)} custom-call(f32[392,256]{1,0:T(8,128)} %get-tuple-element.37.refs_0_, f32[392,256]{1,0:T(8,128)} %get-tuple-element.38.refs_1_, f32[520,256]{1,0:T(8,128)} %copy-done.2, f32[520,256]{1,0:T(8,128)} %collective-permute-done.3.refs_3_, f32[648,256]{1,0:T(8,128)} %copy-done, ...), custom_call_target="tpu_custom_call" | custom-call | flops 4000000000 | bytes 20971520 | tf_op jit(solution)/shard_map/tail/pallas_call | solution.py:434
  128.4 3.2 %copy.25 = bf16[512,2048]{1,0:T(8,128)(2,1)} copy(bf16[512,2048]{1,0:T(8,128)(2,1)} %tail.1) | data formatting | bytes 4194304
  (6 shorter events, 0.0 us)
Async XLA Ops:
  24.8 2.8 %collective-permute-start = (f32[520,256]{1,0:T(8,128)}, f32[520,256]{1,0:T(8,128)S(1)}, u32[]{:S(2)}, u32[]{:S(2)}) collective-permute-start(f32[520,256]{1,0:T(8,128)} %get-tuple-element.28), channel_id=1, source_target_pairs={{0,1},{1,0},{2,3},{3,2},{4,5},{5,4},{6,7},{7,6}} | collective-permute-start | bytes 1597448 | tf_op jit(solution)/shard_map/ppermute | solution.py:466
  27.7 1.0 copy-start.7
  29.0 0.8 copy-start.2
  47.0 2.4 %collective-permute-start.1 = (f32[648,256]{1,0:T(8,128)}, f32[648,256]{1,0:T(8,128)S(1)}, u32[]{:S(2)}, u32[]{:S(2)}) collective-permute-start(f32[648,256]{1,0:T(8,128)} %get-tuple-element.32), channel_id=1, source_target_pairs={{0,1},{1,0},{2,3},{3,2},{4,5},{5,4},{6,7},{7,6}} | collective-permute-start | bytes 1990664 | tf_op jit(solution)/shard_map/ppermute | solution.py:466
  49.5 1.1 copy-start.5
  50.9 0.8 copy-start
  51.8 15.5 %copy-start.1 = (f32[648,256]{1,0:T(8,128)S(1)}, f32[648,256]{1,0:T(8,128)}, u32[]{:S(2)}) copy-start(f32[648,256]{1,0:T(8,128)} %copy-done) | copy-start | bytes 1990660
  51.8 18.2 %copy-start.3 = (f32[520,256]{1,0:T(8,128)S(1)}, f32[520,256]{1,0:T(8,128)}, u32[]{:S(2)}) copy-start(f32[520,256]{1,0:T(8,128)} %copy-done.2) | copy-start | bytes 1597444
  66.7 3.3 %collective-permute-start.2 = (f32[520,256]{1,0:T(8,128)}, f32[520,256]{1,0:T(8,128)S(1)}, u32[]{:S(2)}, u32[]{:S(2)}) collective-permute-start(f32[520,256]{1,0:T(8,128)} %get-tuple-element.36), channel_id=1, source_target_pairs={{0,1},{1,0},{2,3},{3,2},{4,5},{5,4},{6,7},{7,6}} | collective-permute-start | bytes 1597448 | tf_op jit(solution)/shard_map/ppermute | solution.py:466
  67.3 29.9 %collective-permute-start.4 = (f32[648,256]{1,0:T(8,128)S(1)}, f32[648,256]{1,0:T(8,128)}, u32[]{:S(2)}, u32[]{:S(2)}) collective-permute-start(f32[648,256]{1,0:T(8,128)S(1)} %copy-done.1), channel_id=1, source_target_pairs={{0,2},{2,0},{1,3},{3,1},{4,6},{6,4},{5,7},{7,5}} | collective-permute-start | bytes 1990664 | tf_op jit(solution)/shard_map/ppermute | solution.py:468
  70.0 27.3 %collective-permute-start.3 = (f32[520,256]{1,0:T(8,128)S(1)}, f32[520,256]{1,0:T(8,128)}, u32[]{:S(2)}, u32[]{:S(2)}) collective-permute-start(f32[520,256]{1,0:T(8,128)S(1)} %copy-done.3), channel_id=1, source_target_pairs={{0,2},{2,0},{1,3},{3,1},{4,6},{6,4},{5,7},{7,5}} | collective-permute-start | bytes 1597448 | tf_op jit(solution)/shard_map/ppermute | solution.py:468
  70.0 1.0 copy-start.6
  71.4 2.0 %copy-start.4 = (f32[520,256]{1,0:T(8,128)}, f32[520,256]{1,0:T(8,128)S(1)}, u32[]{:S(2)}) copy-start(f32[520,256]{1,0:T(8,128)S(1)} %shard_map.117.refs_7_.refs_6_) | copy-start | bytes 1597444
  71.4 36.8 %collective-permute-start.5 = (f32[520,256]{1,0:T(8,128)S(1)}, f32[520,256]{1,0:T(8,128)}, u32[]{:S(2)}, u32[]{:S(2)}) collective-permute-start(f32[520,256]{1,0:T(8,128)S(1)} %shard_map.117.refs_7_.refs_6_), channel_id=1, source_target_pairs={{0,2},{2,0},{1,3},{3,1},{4,6},{6,4},{5,7},{7,5}} | collective-permute-start | bytes 1597448 | tf_op jit(solution)/shard_map/ppermute | solution.py:468

commit v6 on v5

--- a/solution.py
+++ b/solution.py
@@ -14,7 +14,7 @@
 HEAD = 256
 GROUP = 16
 LOWEST = float(jnp.finfo(jnp.float32).min)
-CHUNKS = (64, 80, 64, 48)
+CHUNKS = (112, 80, 64)
 HBM = pl.BlockSpec(memory_space=pltpu.HBM)
 ANY = pl.BlockSpec(memory_space=pl.ANY)
 VMEM = pl.BlockSpec(memory_space=pltpu.VMEM)
@@ -24,7 +24,7 @@
 def project(hidden, w_norm, w_q, w_k, w_v, positions, x, wide, narrow, xn, cos_t, sin_t, q_rows, k_rows, v_rows, sem, start_more):
     rows = hidden.shape[0]
     half = HEAD // 2
-    tiles = ([pltpu.make_async_copy(w_k, narrow.at[0], sem.at[0]), pltpu.make_async_copy(w_v, narrow.at[1], sem.at[1])]
+    tiles = ([pltpu.make_async_copy(w_k, narrow.at[:, :HEAD], sem.at[0]), pltpu.make_async_copy(w_v, narrow.at[:, HEAD:], sem.at[1])]
              + [pltpu.make_async_copy(w_q.at[h * HEAD:(h + 1) * HEAD], wide.at[h * HEAD:(h + 1) * HEAD], sem.at[2 + h]) for h in range(HEADS)])
     first = pltpu.make_async_copy(hidden, x, sem.at[2 + HEADS])
     first.start()
@@ -51,7 +51,7 @@
         xn[at, :] = (row * scale * gain).astype(jnp.bfloat16)
         return carry
 
-    lax.fori_loop(0, rows // 32, norm, 0)
+    lax.fori_loop(0, rows // 32, norm, 0, unroll=4)
 
     def product(w):
         return jnp.dot(xn[...], w, preferred_element_type=jnp.float32).astype(jnp.bfloat16).astype(jnp.float32)
@@ -60,20 +60,23 @@
         lower, upper = u[:, :half], u[:, half:]
         return jnp.concatenate([lower * cos_t[...] - upper * sin_t[...], upper * cos_t[...] + lower * sin_t[...]], axis=1)
 
-    tiles[0].wait()
-    k_rows[...] = rotated(product(narrow[0])).astype(jnp.bfloat16).astype(jnp.float32)
-    tiles[1].wait()
-    v_rows[...] = product(narrow[1])
+    for copy in tiles[:2]:
+        copy.wait()
+    both = product(narrow[...])
+    k_rows[...] = rotated(both[:, :HEAD]).astype(jnp.bfloat16).astype(jnp.float32)
+    v_rows[...] = both[:, HEAD:]
     start_more()
     for copy in tiles[2:]:
         copy.wait()
 
-    def head(h, carry):
-        at = pl.ds(pl.multiple_of(h * HEAD, HEAD), HEAD)
-        q_rows[:, at] = (rotated(product(wide[:, at])) * HEAD ** -0.5).astype(jnp.bfloat16)
+    def heads(i, carry):
+        at = pl.ds(pl.multiple_of(i * 2 * HEAD, 2 * HEAD), 2 * HEAD)
+        both = product(wide[:, at])
+        pair = jnp.concatenate([rotated(both[:, :HEAD]), rotated(both[:, HEAD:])], axis=1)
+        q_rows[:, at] = (pair * HEAD ** -0.5).astype(jnp.bfloat16)
         return carry
 
-    lax.fori_loop(0, HEADS, head, 0)
+    lax.fori_loop(0, HEADS // 2, heads, 0)
 
 
 def reorder(by_row):
@@ -109,12 +112,13 @@
     return top, total
 
 
-def attention_kernel(first_row, groups, mode, scalars, lengths, *refs):
+def attention_kernel(first_row, groups, mode, lengths, *refs):
     refs = list(refs)
     take = lambda n: [refs.pop(0) for _ in range(n)]
     half = lengths.shape[0] // 2
-    starts = [pl.multiple_of(scalars[side] * half + first_row, GROUP) for side in range(2)]
-    slot_base = scalars[2]
+    me = lax.axis_index('sp')
+    core = lax.rem(me, 2)
+    starts = [pl.multiple_of(side * half + first_row, GROUP) for side in (core, 1 - core)]
     if mode == 'first':
         inputs = take(6)
     else:
@@ -128,6 +132,7 @@
         saved = take(3)
     kbuf, vbuf, in_sem, out_sem = take(4)
     depth, _, slots, _ = kbuf.shape
+    slot_base = me * slots
     total_groups = 2 * groups
     ahead = min(8 if mode == 'first' else 5, total_groups)
 
@@ -234,7 +239,7 @@
         copy.wait()
 
 
-def attention_call(first_row, rows, scalars, lengths, tokens, k_block, v_block, outs, after):
+def attention_call(first_row, rows, lengths, tokens, k_block, v_block, outs, after):
     mode = 'later' if outs else 'first'
     groups = rows // GROUP
     depth = min(2 * groups, 8)
@@ -252,16 +257,16 @@
         shapes += saved
         half_row = pltpu.VMEM((all_rows, HEAD // 2), jnp.float32)
         scratch += [pltpu.SemaphoreType.DMA((3,)), pltpu.VMEM((all_rows, dim), jnp.bfloat16), pltpu.VMEM((dim, HEADS * HEAD), jnp.bfloat16),
-                    pltpu.VMEM((2, dim, HEAD), jnp.bfloat16), pltpu.VMEM((all_rows, dim), jnp.bfloat16), half_row, half_row,
+                    pltpu.VMEM((dim, 2 * HEAD), jnp.bfloat16), pltpu.VMEM((all_rows, dim), jnp.bfloat16), half_row, half_row,
                     *(pltpu.VMEM(a.shape, a.dtype) for a in saved), pltpu.SemaphoreType.DMA((3 + HEADS,))]
-        operands = [scalars, lengths, *tokens, k_block, v_block]
-        specs = [SMEM, SMEM, *token_specs, HBM, HBM]
+        operands = [lengths, *tokens, k_block, v_block]
+        specs = [SMEM, *token_specs, HBM, HBM]
         aliases = {}
     else:
         scratch += [pltpu.VMEM((depth, GROUP, HEADS * HEAD), jnp.bfloat16)] + [pltpu.VMEM((depth, GROUP, HEAD), jnp.float32)] * 2
-        operands = [scalars, lengths, *tokens, k_block, v_block, *outs, after]
-        specs = [SMEM, SMEM] + [HBM] * 7 + [ANY]
-        aliases = {7: 0, 8: 1}
+        operands = [lengths, *tokens, k_block, v_block, *outs, after]
+        specs = [SMEM] + [HBM] * 7 + [ANY]
+        aliases = {6: 0, 7: 1}
     return pl.pallas_call(
         functools.partial(attention_kernel, first_row, groups, mode),
         out_shape=tuple(shapes),
@@ -446,19 +451,41 @@
     )(kept, sent, *pairs, w_o, hidden)
 
 
+def emit_kernel(source, out, buf, in_sem, out_sem):
+    rows = source.shape[0] // 8
+    parts = [pl.ds(i * rows, rows) for i in range(8)]
+    loads = [pltpu.make_async_copy(source.at[at], buf.at[at], in_sem.at[i]) for i, at in enumerate(parts)]
+    stores = [pltpu.make_async_copy(buf.at[at], out.at[at], out_sem.at[i]) for i, at in enumerate(parts)]
+    for copy in loads:
+        copy.start()
+    for load, store in zip(loads, stores):
+        load.wait()
+        store.start()
+    for copy in stores:
+        copy.wait()
+
+
+def emit_call(source):
+    return pl.pallas_call(
+        emit_kernel,
+        out_shape=jax.ShapeDtypeStruct(source.shape, source.dtype),
+        in_specs=[HBM],
+        out_specs=HBM,
+        scratch_shapes=[pltpu.VMEM(source.shape, source.dtype), pltpu.SemaphoreType.DMA((8,)), pltpu.SemaphoreType.DMA((8,))],
+        compiler_params=pltpu.CompilerParams(vmem_limit_bytes=62 << 20),
+        name="emit",
+    )(source)
+
+
 def local_step(hidden, w_norm, w_q, w_k, w_v, w_o, k_block, v_block, cache_len):
-    slots = k_block.shape[1]
-    me = lax.axis_index('sp')
-    core = lax.rem(me, 2)
     sibling = [(0, 1), (1, 0), (2, 3), (3, 2)]
     across = [(0, 2), (2, 0), (1, 3), (3, 1)]
-    scalars = jnp.stack([core, 1 - core, me * slots]).astype(jnp.int32)
     tokens = (hidden, w_norm, w_q, w_k, w_v)
     outs, merged, theirs = (), [], []
     first = 0
     for i, rows in enumerate(CHUNKS):
         *outs, kept, sent = results = attention_call(
-            first, rows, scalars, cache_len, tokens, k_block, v_block, outs, merged[-1] if merged else None)
+            first, rows, cache_len, tokens, k_block, v_block, outs, merged[-1] if merged else None)
         if i == 0:
             outs, (kept, sent), tokens = results[:2], results[2:4], results[4:]
         if i == len(CHUNKS) - 1:
@@ -469,7 +496,7 @@
         first += rows
     pairs = [p for pair in zip(merged, theirs) for p in pair]
     out = tail_call(CHUNKS[:-1], CHUNKS[-1], kept, sent, pairs, w_o, hidden)
-    return out, outs[0], outs[1]
+    return emit_call(out), outs[0], outs[1]
 
 
 def solution(mesh):

time: 132 us -> 125 us (0.947)
  waiting for transfers between devices: 26.7 us -> 19.2 us
  Pallas kernels: 88.7 us -> 95.3 us
  local copies, waits for them, and re-layouts: 7.96 us -> 3.22 us
    ppermute x3 -> x2, waiting for transfers between devices: 23 us -> 16.9 us  [local_step(): theirs.append(lax.ppermute(merged[-1], 'sp', across))]
    unnamed x17 -> x10, local copies, waits for them, and re-layouts: 7.96 us -> 3.22 us
    pallas_call x1, Pallas kernels: 20.3 us -> 23.8 us  [tail_call(): pl.pallas_call(functools.partial(tail_kernel, chunks, late), out_shape=ja...]
    pallas_call x0 -> x1, Pallas kernels: none -> 2.39 us  [emit_call(): pl.pallas_call(emit_kernel, out_shape=jax.ShapeDtypeStruct(source.shape,...]
    ppermute x3 -> x2, waiting for transfers between devices: 3.71 us -> 2.32 us  [local_step(): taken = lax.ppermute(sent, 'sp', sibling)]
    pallas_call x4 -> x3, Pallas kernels: 67.4 us -> 68.4 us  [attention_call(): pl.pallas_call(functools.partial(attention_kernel, first_row, groups, mod...]
    ppermute x3 -> x2, starting transfers between devices: 4.72 us -> 4.67 us  [local_step(): theirs.append(lax.ppermute(merged[-1], 'sp', across))]
  transfers between devices with their start and end apart: 6 -> 4, of which waited for: 4 -> 3; matrix products, arithmetic and copies ran while one was open for 0% -> 0% of each run, Pallas kernels for 9% -> 12%
where the time goes in v6:
time: 125 us
  Pallas kernels  95.3 us (76%)
  waiting for transfers between devices  19.2 us (15%)
  starting transfers between devices  6.45 us (5%)
  local copies, waits for them, and re-layouts  3.22 us (3%)
    pallas_call x3, Pallas kernels, attention_call(): pl.pallas_call(functools.partial(attention_kernel, first_row, groups, mod...  68.4 us
    pallas_call x1, Pallas kernels, tail_call(): pl.pallas_call(functools.partial(tail_kernel, chunks, late), out_shape=ja...  23.8 us
    ppermute x2, waiting for transfers between devices, local_step(): theirs.append(lax.ppermute(merged[-1], 'sp', across))  16.9 us
    ppermute x2, starting transfers between devices, local_step(): theirs.append(lax.ppermute(merged[-1], 'sp', across))  4.67 us
    unnamed x10, local copies, waits for them, and re-layouts  3.22 us
  transfers between devices with their start and end apart: 4, of which 3 were waited for; matrix products, arithmetic and copies ran while one was open for 0% of the time, Pallas kernels for 12%

profile of v6, /device:TPU:0, one launch (start us, length us, event | category | flops | bytes accessed | tf_op | source)
XLA Modules:
  0.0 124.9 jit_solution(8883526120094822829)
XLA Ops:
  0.6 36.2 %shard_map.112 = (bf16[512,128,256]{2,1,0:T(8,128)(2,1)}, bf16[512,128,256]{2,1,0:T(8,128)(2,1)}, f32[904,256]{1,0:T(8,128)}, f32[904,256]{1,0:T(8,128)}, bf16[5...) custom-call(s32[512]{0:T(512)} %lengths.5, bf16[512,2048]{1,0:T(8,128)(2,1)} %refs_7_.3, ...), custom_call_target="tpu_custom_call" | custom-call | flops 2240000000 | bytes 58720256 | tf_op jit(solution)/shard_map/pallas_call | solution.py:270
  36.9 1.3 %collective-permute-start = (f32[904,256]{1,0:T(8,128)}, f32[904,256]{1,0:T(8,128)S(1)}, u32[]{:S(2)}, u32[]{:S(2)}) collective-permute-start(f32[904,256]{1,0:T(8,128)} %get-tuple-element.24), channel_id=1, source_target_pairs={{0,1},{1,0},{2,3},{3,2},{4,5},{5,4},{6,7},{7,6}} | collective-permute-start | bytes 2777096 | tf_op jit(solution)/shard_map/ppermute | solution.py:493
  38.2 2.3 %collective-permute-done.two = f32[904,256]{1,0:T(8,128)S(1)} collective-permute-done((f32[904,256]{1,0:T(8,128)}, f32[904,256]{1,0:T(8,128)S(1)}, u32[]{:S(2)}, u32[]{:S(2)}) %collective-permute-start) | collective-permute-done | bytes 925728 | tf_op jit(solution)/shard_map/ppermute | solution.py:493
  40.5 0.0 copy-start.3
  40.5 1.2 copy-done.3
  41.7 0.4 shard_map.113.refs_7_.refs_2_
  42.2 0.0 copy-start
  42.2 0.9 copy-done
  43.1 0.0 copy-start.1
  43.1 17.4 %shard_map.114 = (bf16[512,128,256]{2,1,0:T(8,128)(2,1)}, bf16[512,128,256]{2,1,0:T(8,128)(2,1)}, f32[648,256]{1,0:T(8,128)}, f32[648,256]{1,0:T(8,128)}) custom-call(s32[512]{0:T(512)} %lengths.5, bf16[512,2048]{1,0:T(8,128)(2,1)} %get-tuple-element.18.refs_0_, f32[512,256]{1,0:T(8,128)} %get-tuple-element.19.refs_1_, ...), custom_call_target="tpu_custom_call", output_to_operand_aliasing={{0}: (6, {}), {1}: (7, {})} | custom-call | flops 1600000000 | bytes 41943040 | tf_op jit(solution)/shard_map/pallas_call | solution.py:270
  60.5 0.4 collective-permute-start.1
  60.9 0.0 copy-done.1
  60.9 2.6 %collective-permute-start.2 = (f32[904,256]{1,0:T(8,128)S(1)}, f32[904,256]{1,0:T(8,128)}, u32[]{:S(2)}, u32[]{:S(2)}) collective-permute-start(f32[904,256]{1,0:T(8,128)S(1)} %copy-done.1), channel_id=1, source_target_pairs={{0,2},{2,0},{1,3},{3,1},{4,6},{6,4},{5,7},{7,5}} | collective-permute-start | bytes 2777096 | tf_op jit(solution)/shard_map/ppermute | solution.py:495
  63.5 0.0 collective-permute-done.1.two
  63.5 0.0 copy-start.4
  63.5 1.1 copy-done.4
  64.6 0.4 shard_map.115.refs_7_.refs_4_
  64.9 0.0 copy-start.2
  65.0 2.1 %collective-permute-start.3 = (f32[648,256]{1,0:T(8,128)S(1)}, f32[648,256]{1,0:T(8,128)}, u32[]{:S(2)}, u32[]{:S(2)}) collective-permute-start(f32[648,256]{1,0:T(8,128)S(1)} %shard_map.115.refs_7_.refs_4_), channel_id=1, source_target_pairs={{0,2},{2,0},{1,3},{3,1},{4,6},{6,4},{5,7},{7,5}} | collective-permute-start | bytes 1990664 | tf_op jit(solution)/shard_map/ppermute | solution.py:495
  67.1 0.0 copy-done.2
  67.1 14.8 %shard_map.116 = (bf16[512,128,256]{2,1,0:T(8,128)(2,1)}, bf16[512,128,256]{2,1,0:T(8,128)(2,1)}, f32[520,256]{1,0:T(8,128)}, f32[520,256]{1,0:T(8,128)}) custom-call(s32[512]{0:T(512)} %lengths.5, bf16[512,2048]{1,0:T(8,128)(2,1)} %get-tuple-element.18.refs_0_, f32[512,256]{1,0:T(8,128)} %get-tuple-element.19.refs_1_, ...), custom_call_target="tpu_custom_call", output_to_operand_aliasing={{0}: (6, {}), {1}: (7, {})} | custom-call | flops 1280000000 | bytes 33554432 | tf_op jit(solution)/shard_map/pallas_call | solution.py:270
  81.8 3.1 %collective-permute-done.2.refs_3_ = f32[904,256]{1,0:T(8,128)} collective-permute-done((f32[904,256]{1,0:T(8,128)S(1)}, f32[904,256]{1,0:T(8,128)}, u32[]{:S(2)}, u32[]{:S(2)}) %collective-permute-start.2) | collective-permute-done | bytes 925728 | tf_op jit(solution)/shard_map/ppermute | solution.py:495
  85.0 13.8 %collective-permute-done.3.refs_5_ = f32[648,256]{1,0:T(8,128)} collective-permute-done((f32[648,256]{1,0:T(8,128)S(1)}, f32[648,256]{1,0:T(8,128)}, u32[]{:S(2)}, u32[]{:S(2)}) %collective-permute-start.3) | collective-permute-done | bytes 663584 | tf_op jit(solution)/shard_map/ppermute | solution.py:495
  98.8 23.8 %tail.1.source = bf16[512,2048]{1,0:T(8,128)(2,1)} custom-call(f32[520,256]{1,0:T(8,128)} %get-tuple-element.29.refs_0_, f32[520,256]{1,0:T(8,128)} %get-tuple-element.30.refs_1_, f32[904,256]{1,0:T(8,128)} %copy-done, f32[904,256]{1,0:T(8,128)} %collective-permute-done.2.refs_3_, f32[648,256]{1,0:T(8,128)} %copy-done.2, ...), custom_call_target="tpu_custom_call" | custom-call | flops 4000000000 | bytes 20971520 | tf_op jit(solution)/shard_map/tail/pallas_call | solution.py:439
  122.5 2.4 %emit.1 = bf16[512,2048]{1,0:T(8,128)(2,1)} custom-call(bf16[512,2048]{1,0:T(8,128)(2,1)} %tail.1.source), custom_call_target="tpu_custom_call" | custom-call | tf_op jit(solution)/shard_map/emit/pallas_call | solution.py:469
Async XLA Ops:
  36.9 3.7 %collective-permute-start = (f32[904,256]{1,0:T(8,128)}, f32[904,256]{1,0:T(8,128)S(1)}, u32[]{:S(2)}, u32[]{:S(2)}) collective-permute-start(f32[904,256]{1,0:T(8,128)} %get-tuple-element.24), channel_id=1, source_target_pairs={{0,1},{1,0},{2,3},{3,2},{4,5},{5,4},{6,7},{7,6}} | collective-permute-start | bytes 2777096 | tf_op jit(solution)/shard_map/ppermute | solution.py:493
  40.5 1.2 copy-start.3
  42.2 1.0 copy-start
  43.1 17.8 %copy-start.1 = (f32[904,256]{1,0:T(8,128)S(1)}, f32[904,256]{1,0:T(8,128)}, u32[]{:S(2)}) copy-start(f32[904,256]{1,0:T(8,128)} %copy-done) | copy-start | bytes 2777092
  60.5 3.0 %collective-permute-start.1 = (f32[648,256]{1,0:T(8,128)}, f32[648,256]{1,0:T(8,128)S(1)}, u32[]{:S(2)}, u32[]{:S(2)}) collective-permute-start(f32[648,256]{1,0:T(8,128)} %get-tuple-element.28), channel_id=1, source_target_pairs={{0,1},{1,0},{2,3},{3,2},{4,5},{5,4},{6,7},{7,6}} | collective-permute-start | bytes 1990664 | tf_op jit(solution)/shard_map/ppermute | solution.py:493
  60.9 24.0 %collective-permute-start.2 = (f32[904,256]{1,0:T(8,128)S(1)}, f32[904,256]{1,0:T(8,128)}, u32[]{:S(2)}, u32[]{:S(2)}) collective-permute-start(f32[904,256]{1,0:T(8,128)S(1)} %copy-done.1), channel_id=1, source_target_pairs={{0,2},{2,0},{1,3},{3,1},{4,6},{6,4},{5,7},{7,5}} | collective-permute-start | bytes 2777096 | tf_op jit(solution)/shard_map/ppermute | solution.py:495
  63.5 1.1 copy-start.4
  64.9 2.1 %copy-start.2 = (f32[648,256]{1,0:T(8,128)}, f32[648,256]{1,0:T(8,128)S(1)}, u32[]{:S(2)}) copy-start(f32[648,256]{1,0:T(8,128)S(1)} %shard_map.115.refs_7_.refs_4_) | copy-start | bytes 1990660
  65.0 33.8 %collective-permute-start.3 = (f32[648,256]{1,0:T(8,128)S(1)}, f32[648,256]{1,0:T(8,128)}, u32[]{:S(2)}, u32[]{:S(2)}) collective-permute-start(f32[648,256]{1,0:T(8,128)S(1)} %shard_map.115.refs_7_.refs_4_), channel_id=1, source_target_pairs={{0,2},{2,0},{1,3},{3,1},{4,6},{6,4},{5,7},{7,5}} | collective-permute-start | bytes 1990664 | tf_op jit(solution)/shard_map/ppermute | solution.py:495

commit v7 on v6

--- a/solution.py
+++ b/solution.py
@@ -127,14 +127,25 @@
     if mode != 'first':
         take(3)
     k_out, v_out = take(2)
-    parts = take(2)
+    part_out = take(2)
     if mode == 'first':
         saved = take(3)
-    kbuf, vbuf, in_sem, out_sem = take(4)
+    kbuf, vbuf, part_buf, in_sem, out_sem, part_sem = take(6)
+    parts = [part_buf.at[0], part_buf.at[1]]
+
+    def part_copy(i, place):
+        at = pl.ds(pl.multiple_of(place * 128, 128), 128)
+        return pltpu.make_async_copy(part_buf.at[i, at], part_out[i].at[at], part_sem.at[i, place])
+
+    def stats_copy(i):
+        at = pl.ds(groups * 128, 8)
+        return pltpu.make_async_copy(part_buf.at[i, at], part_out[i].at[at], part_sem.at[i, groups])
+
     depth, _, slots, _ = kbuf.shape
     slot_base = me * slots
     total_groups = 2 * groups
-    ahead = min(8 if mode == 'first' else 5, total_groups)
+    ahead = min(7, total_groups)
+    initial = min(depth if mode == 'first' else ahead, total_groups)
 
     def row_of(g):
         return pl.multiple_of(jnp.where(g < groups, starts[0] + g * GROUP, starts[1] + (g - groups) * GROUP), GROUP)
@@ -156,7 +167,7 @@
                 pltpu.make_async_copy(vbuf.at[slot], v_out.at[at], out_sem.at[1, slot]))
 
     def start_all():
-        for g in range(ahead):
+        for g in range(initial):
             for copy in fetch(g):
                 copy.start()
 
@@ -176,10 +187,15 @@
     stat_row = lax.broadcasted_iota(jnp.int32, (8, HEAD), 0)
     order = reorder(True)
 
-    def one(part, first, g):
+    def one(i, part, first, g):
         slot = lax.rem(g, depth)
         row0 = row_of(g)
         place = g - first
+
+        @pl.when(place > 0)
+        def _():
+            part_copy(i, place - 1).start()
+
         for copy in fetch(g):
             copy.wait()
         plane = jnp.zeros((1, 128), jnp.int32)
@@ -212,8 +228,8 @@
         part[groups * 128:, :] = jnp.where(stat_row == place, jnp.concatenate([top, total], axis=1), part[groups * 128:, :])
         for copy in flush(g):
             copy.start()
-        if total_groups > ahead:
-            @pl.when(g + ahead < total_groups)
+        if total_groups > initial:
+            @pl.when(jnp.logical_and(g + ahead >= initial, g + ahead < total_groups))
             def _():
                 @pl.when(g + ahead >= depth)
                 def _():
@@ -224,11 +240,13 @@
                     copy.start()
 
     for i, part in enumerate(parts):
-        def body(g, carry, part=part, first=i * groups):
-            one(part, first, g)
+        def body(g, carry, i=i, part=part, first=i * groups):
+            one(i, part, first, g)
             return carry
 
         lax.fori_loop(i * groups, (i + 1) * groups, body, 0)
+        part_copy(i, groups - 1).start()
+        stats_copy(i).start()
         if i == 0:
             for copy in keep:
                 copy.start()
@@ -237,17 +255,22 @@
             copy.wait()
     for copy in keep:
         copy.wait()
+    for i in range(2):
+        for place in range(groups):
+            part_copy(i, place).wait()
+        stats_copy(i).wait()
 
 
 def attention_call(first_row, rows, lengths, tokens, k_block, v_block, outs, after):
     mode = 'later' if outs else 'first'
     groups = rows // GROUP
-    depth = min(2 * groups, 8)
+    depth = min(2 * groups, 11 if mode == 'first' else 12)
     slots = k_block.shape[1]
     part = jax.ShapeDtypeStruct((rows * HEADS + 8, HEAD), jnp.float32)
     shapes = [jax.ShapeDtypeStruct(k_block.shape, k_block.dtype), jax.ShapeDtypeStruct(v_block.shape, v_block.dtype), part, part]
     ring = pltpu.VMEM((depth, GROUP, slots, HEAD), jnp.bfloat16)
-    scratch = [ring, ring, pltpu.SemaphoreType.DMA((5, depth)), pltpu.SemaphoreType.DMA((2, depth))]
+    scratch = [ring, ring, pltpu.VMEM((2, *part.shape), jnp.float32), pltpu.SemaphoreType.DMA((5, depth)), pltpu.SemaphoreType.DMA((2, depth)),
+               pltpu.SemaphoreType.DMA((2, groups + 1))]
     all_rows = lengths.shape[0]
     dim = tokens[0].shape[1]
     if mode == 'first':
@@ -271,7 +294,7 @@
         functools.partial(attention_kernel, first_row, groups, mode),
         out_shape=tuple(shapes),
         in_specs=specs,
-        out_specs=(HBM, HBM, VMEM, VMEM) + (HBM,) * (len(shapes) - 4),
+        out_specs=(HBM,) * len(shapes),
         input_output_aliases=aliases,
         scratch_shapes=scratch,
         compiler_params=pltpu.CompilerParams(vmem_limit_bytes=62 << 20),

time: 125 us -> 117 us (0.936)
  Pallas kernels: 95.3 us -> 86.5 us
    pallas_call x3, Pallas kernels: 68.4 us -> 59.5 us  [attention_call(): pl.pallas_call(functools.partial(attention_kernel, first_row, groups, mod...]
  transfers between devices with their start and end apart: 4 -> 4, of which waited for: 3 -> 3; matrix products, arithmetic and copies ran while one was open for 0% -> 0% of each run, Pallas kernels for 12% -> 13%
where the time goes in v7:
time: 117 us
  Pallas kernels  86.5 us (74%)
  waiting for transfers between devices  19.7 us (17%)
  starting transfers between devices  6.69 us (6%)
  local copies, waits for them, and re-layouts  3.22 us (3%)
    pallas_call x3, Pallas kernels, attention_call(): pl.pallas_call(functools.partial(attention_kernel, first_row, groups, mod...  59.5 us
    pallas_call x1, Pallas kernels, tail_call(): pl.pallas_call(functools.partial(tail_kernel, chunks, late), out_shape=ja...  23.8 us
    ppermute x2, waiting for transfers between devices, local_step(): theirs.append(lax.ppermute(merged[-1], 'sp', across))  17.4 us
    ppermute x2, starting transfers between devices, local_step(): theirs.append(lax.ppermute(merged[-1], 'sp', across))  4.93 us
    unnamed x10, local copies, waits for them, and re-layouts  3.22 us
    pallas_call x1, Pallas kernels, emit_call(): pl.pallas_call(emit_kernel, out_shape=jax.ShapeDtypeStruct(source.shape,...  2.39 us
  transfers between devices with their start and end apart: 4, of which 3 were waited for; matrix products, arithmetic and copies ran while one was open for 0% of the time, Pallas kernels for 13%

profile of v7, /device:TPU:0, one launch (start us, length us, event | category | flops | bytes accessed | tf_op | source)
XLA Modules:
  0.0 116.8 jit_solution(9108895723654322903)
XLA Ops:
  0.6 28.3 %shard_map.112 = (bf16[512,128,256]{2,1,0:T(8,128)(2,1)}, bf16[512,128,256]{2,1,0:T(8,128)(2,1)}, f32[904,256]{1,0:T(8,128)}, f32[904,256]{1,0:T(8,128)}, bf16[5...) custom-call(s32[512]{0:T(512)} %lengths.5, bf16[512,2048]{1,0:T(8,128)(2,1)} %refs_7_.3, ...), custom_call_target="tpu_custom_call" | custom-call | flops 2240000000 | bytes 58720256 | tf_op jit(solution)/shard_map/pallas_call | solution.py:293
  29.0 1.3 %collective-permute-start = (f32[904,256]{1,0:T(8,128)}, f32[904,256]{1,0:T(8,128)S(1)}, u32[]{:S(2)}, u32[]{:S(2)}) collective-permute-start(f32[904,256]{1,0:T(8,128)} %get-tuple-element.24), channel_id=1, source_target_pairs={{0,1},{1,0},{2,3},{3,2},{4,5},{5,4},{6,7},{7,6}} | collective-permute-start | bytes 2777096 | tf_op jit(solution)/shard_map/ppermute | solution.py:516
  30.3 2.3 %collective-permute-done.two = f32[904,256]{1,0:T(8,128)S(1)} collective-permute-done((f32[904,256]{1,0:T(8,128)}, f32[904,256]{1,0:T(8,128)S(1)}, u32[]{:S(2)}, u32[]{:S(2)}) %collective-permute-start) | collective-permute-done | bytes 925728 | tf_op jit(solution)/shard_map/ppermute | solution.py:516
  32.6 0.0 copy-start.3
  32.6 1.2 %copy-done.3 = f32[904,256]{1,0:T(8,128)S(1)} copy-done((f32[904,256]{1,0:T(8,128)S(1)}, f32[904,256]{1,0:T(8,128)}, u32[]{:S(2)}) %copy-start.3) | copy-done | bytes 925720
  33.8 0.4 shard_map.113.refs_7_.refs_2_
  34.3 0.0 copy-start
  34.3 0.9 copy-done
  35.2 0.0 copy-start.1
  35.2 16.8 %shard_map.114 = (bf16[512,128,256]{2,1,0:T(8,128)(2,1)}, bf16[512,128,256]{2,1,0:T(8,128)(2,1)}, f32[648,256]{1,0:T(8,128)}, f32[648,256]{1,0:T(8,128)}) custom-call(s32[512]{0:T(512)} %lengths.5, bf16[512,2048]{1,0:T(8,128)(2,1)} %get-tuple-element.18.refs_0_, f32[512,256]{1,0:T(8,128)} %get-tuple-element.19.refs_1_, ...), custom_call_target="tpu_custom_call", output_to_operand_aliasing={{0}: (6, {}), {1}: (7, {})} | custom-call | flops 1600000000 | bytes 41943040 | tf_op jit(solution)/shard_map/pallas_call | solution.py:293
  52.1 0.4 collective-permute-start.1
  52.5 0.0 copy-done.1
  52.5 2.6 %collective-permute-start.2 = (f32[904,256]{1,0:T(8,128)S(1)}, f32[904,256]{1,0:T(8,128)}, u32[]{:S(2)}, u32[]{:S(2)}) collective-permute-start(f32[904,256]{1,0:T(8,128)S(1)} %copy-done.1), channel_id=1, source_target_pairs={{0,2},{2,0},{1,3},{3,1},{4,6},{6,4},{5,7},{7,5}} | collective-permute-start | bytes 2777096 | tf_op jit(solution)/shard_map/ppermute | solution.py:518
  55.1 0.0 collective-permute-done.1.two
  55.2 0.0 copy-start.4
  55.2 1.1 copy-done.4
  56.2 0.4 shard_map.115.refs_7_.refs_4_
  56.6 0.0 copy-start.2
  56.6 2.3 %collective-permute-start.3 = (f32[648,256]{1,0:T(8,128)S(1)}, f32[648,256]{1,0:T(8,128)}, u32[]{:S(2)}, u32[]{:S(2)}) collective-permute-start(f32[648,256]{1,0:T(8,128)S(1)} %shard_map.115.refs_7_.refs_4_), channel_id=1, source_target_pairs={{0,2},{2,0},{1,3},{3,1},{4,6},{6,4},{5,7},{7,5}} | collective-permute-start | bytes 1990664 | tf_op jit(solution)/shard_map/ppermute | solution.py:518
  58.9 0.0 copy-done.2
  58.9 14.3 %shard_map.116 = (bf16[512,128,256]{2,1,0:T(8,128)(2,1)}, bf16[512,128,256]{2,1,0:T(8,128)(2,1)}, f32[520,256]{1,0:T(8,128)}, f32[520,256]{1,0:T(8,128)}) custom-call(s32[512]{0:T(512)} %lengths.5, bf16[512,2048]{1,0:T(8,128)(2,1)} %get-tuple-element.18.refs_0_, f32[512,256]{1,0:T(8,128)} %get-tuple-element.19.refs_1_, ...), custom_call_target="tpu_custom_call", output_to_operand_aliasing={{0}: (6, {}), {1}: (7, {})} | custom-call | flops 1280000000 | bytes 33554432 | tf_op jit(solution)/shard_map/pallas_call | solution.py:293
  73.2 3.4 %collective-permute-done.2.refs_3_ = f32[904,256]{1,0:T(8,128)} collective-permute-done((f32[904,256]{1,0:T(8,128)S(1)}, f32[904,256]{1,0:T(8,128)}, u32[]{:S(2)}, u32[]{:S(2)}) %collective-permute-start.2) | collective-permute-done | bytes 925728 | tf_op jit(solution)/shard_map/ppermute | solution.py:518
  76.6 14.0 %collective-permute-done.3.refs_5_ = f32[648,256]{1,0:T(8,128)} collective-permute-done((f32[648,256]{1,0:T(8,128)S(1)}, f32[648,256]{1,0:T(8,128)}, u32[]{:S(2)}, u32[]{:S(2)}) %collective-permute-start.3) | collective-permute-done | bytes 663584 | tf_op jit(solution)/shard_map/ppermute | solution.py:518
  90.6 23.8 %tail.1.source = bf16[512,2048]{1,0:T(8,128)(2,1)} custom-call(f32[520,256]{1,0:T(8,128)} %get-tuple-element.29.refs_0_, f32[520,256]{1,0:T(8,128)} %get-tuple-element.30.refs_1_, f32[904,256]{1,0:T(8,128)} %copy-done, f32[904,256]{1,0:T(8,128)} %collective-permute-done.2.refs_3_, f32[648,256]{1,0:T(8,128)} %copy-done.2, ...), custom_call_target="tpu_custom_call" | custom-call | flops 4000000000 | bytes 20971520 | tf_op jit(solution)/shard_map/tail/pallas_call | solution.py:462
  114.4 2.4 %emit.1 = bf16[512,2048]{1,0:T(8,128)(2,1)} custom-call(bf16[512,2048]{1,0:T(8,128)(2,1)} %tail.1.source), custom_call_target="tpu_custom_call" | custom-call | tf_op jit(solution)/shard_map/emit/pallas_call | solution.py:492
Async XLA Ops:
  29.0 3.6 %collective-permute-start = (f32[904,256]{1,0:T(8,128)}, f32[904,256]{1,0:T(8,128)S(1)}, u32[]{:S(2)}, u32[]{:S(2)}) collective-permute-start(f32[904,256]{1,0:T(8,128)} %get-tuple-element.24), channel_id=1, source_target_pairs={{0,1},{1,0},{2,3},{3,2},{4,5},{5,4},{6,7},{7,6}} | collective-permute-start | bytes 2777096 | tf_op jit(solution)/shard_map/ppermute | solution.py:516
  32.6 1.2 %copy-start.3 = (f32[904,256]{1,0:T(8,128)S(1)}, f32[904,256]{1,0:T(8,128)}, u32[]{:S(2)}) copy-start(f32[904,256]{1,0:T(8,128)} %get-tuple-element.23.one) | copy-start | bytes 2777092
  34.3 1.0 copy-start
  35.2 17.3 %copy-start.1 = (f32[904,256]{1,0:T(8,128)S(1)}, f32[904,256]{1,0:T(8,128)}, u32[]{:S(2)}) copy-start(f32[904,256]{1,0:T(8,128)} %copy-done) | copy-start | bytes 2777092
  52.1 3.1 %collective-permute-start.1 = (f32[648,256]{1,0:T(8,128)}, f32[648,256]{1,0:T(8,128)S(1)}, u32[]{:S(2)}, u32[]{:S(2)}) collective-permute-start(f32[648,256]{1,0:T(8,128)} %get-tuple-element.28), channel_id=1, source_target_pairs={{0,1},{1,0},{2,3},{3,2},{4,5},{5,4},{6,7},{7,6}} | collective-permute-start | bytes 1990664 | tf_op jit(solution)/shard_map/ppermute | solution.py:516
  52.5 24.1 %collective-permute-start.2 = (f32[904,256]{1,0:T(8,128)S(1)}, f32[904,256]{1,0:T(8,128)}, u32[]{:S(2)}, u32[]{:S(2)}) collective-permute-start(f32[904,256]{1,0:T(8,128)S(1)} %copy-done.1), channel_id=1, source_target_pairs={{0,2},{2,0},{1,3},{3,1},{4,6},{6,4},{5,7},{7,5}} | collective-permute-start | bytes 2777096 | tf_op jit(solution)/shard_map/ppermute | solution.py:518
  55.2 1.1 copy-start.4
  56.6 2.3 %copy-start.2 = (f32[648,256]{1,0:T(8,128)}, f32[648,256]{1,0:T(8,128)S(1)}, u32[]{:S(2)}) copy-start(f32[648,256]{1,0:T(8,128)S(1)} %shard_map.115.refs_7_.refs_4_) | copy-start | bytes 1990660
  56.6 34.0 %collective-permute-start.3 = (f32[648,256]{1,0:T(8,128)S(1)}, f32[648,256]{1,0:T(8,128)}, u32[]{:S(2)}, u32[]{:S(2)}) collective-permute-start(f32[648,256]{1,0:T(8,128)S(1)} %shard_map.115.refs_7_.refs_4_), channel_id=1, source_target_pairs={{0,2},{2,0},{1,3},{3,1},{4,6},{6,4},{5,7},{7,5}} | collective-permute-start | bytes 1990664 | tf_op jit(solution)/shard_map/ppermute | solution.py:518

commit v8 on v7

--- a/solution.py
+++ b/solution.py
@@ -339,18 +339,19 @@
     take = lambda n: [refs.pop(0) for _ in range(n)]
     kept, sent = take(2)
     pairs = take(2 * len(chunks))
-    w_o, hidden = take(2)
-    out, = take(1)
-    near_buf, kept_buf, merged, far_buf, one, two, weights, x, attended, y_early, y_late, got_early, got_late = take(13)
-    local_sem, send_sem, recv_sem, tile_send, tile_recv = take(5)
+    w_o, hidden, result = take(3)
+    near_buf, kept_buf, merged, far_buf, one, two, weights, x, out, attended, y_early, y_late, got_early, got_late = take(14)
+    local_sem, near_send, near_recv, far_send, far_recv, tile_send, tile_recv, late_send, late_recv, out_sem = take(10)
     early = sum(chunks)
     half = early + late
-    tiles = weights.shape[1] // HEAD
+    groups = late // GROUP
+    tiles, _, width = y_early.shape
     me = lax.axis_index('sp')
     core = lax.rem(me, 2)
     group = lax.axis_index('dp')
     sibling, across = (group, me + 1 - 2 * core), (group, lax.rem(me + 2, 4))
     remote = functools.partial(pltpu.make_async_remote_copy, device_id_type=pl.DeviceIdType.MESH)
+    pieces = [pl.ds(g * 128, 128) for g in range(groups)] + [pl.ds(groups * 128, 8)]
 
     load_kept = pltpu.make_async_copy(kept, kept_buf, local_sem.at[0])
     load_kept.start()
@@ -358,8 +359,12 @@
     for device in (sibling, across):
         pl.semaphore_signal(barrier, inc=1, device_id=device, device_id_type=pl.DeviceIdType.MESH)
     pl.semaphore_wait(barrier, 2)
-    near = remote(src_ref=sent, dst_ref=near_buf, send_sem=send_sem.at[0], recv_sem=recv_sem.at[0], device_id=sibling)
-    near.start()
+    near = [remote(src_ref=sent.at[at], dst_ref=near_buf.at[at], send_sem=near_send.at[i], recv_sem=near_recv.at[i], device_id=sibling)
+            for i, at in enumerate(pieces)]
+    far = [remote(src_ref=merged.at[at], dst_ref=far_buf.at[at], send_sem=far_send.at[i], recv_sem=far_recv.at[i], device_id=across)
+           for i, at in enumerate(pieces)]
+    for copy in (near[groups], *near[:groups]):
+        copy.start()
     loads, starts, at = [], [], 0
     for i, rows in enumerate(chunks):
         size = rows * HEADS + 8
@@ -373,101 +378,119 @@
         copy.start()
     order = reorder(False)
 
-    def attend_rows(first, rows, a, b):
-        groups = rows // GROUP
-        columns, _, _ = merge_scales(a, b, groups, True)
-        for g in range(groups):
-            part = pl.ds(g * 128, 128)
-            value = a[part, :] * columns[:, g:g + 1] + b[part, :] * columns[:, 8 + g:9 + g]
-            by_head = jnp.dot(order, value.astype(jnp.bfloat16), preferred_element_type=jnp.float32).astype(jnp.bfloat16)
-            for h in range(HEADS):
-                attended[first + g * GROUP:first + (g + 1) * GROUP, h * HEAD:(h + 1) * HEAD] = by_head[h * GROUP:(h + 1) * GROUP]
-
-    def early_rows(i):
+    load_kept.wait()
+    near[groups].wait_recv()
+    columns, top, total = merge_scales(kept_buf, near_buf, groups, False)
+    merged[groups * 128:, :128] = top
+    merged[groups * 128:, 128:] = total
+    for g in range(groups):
+        near[g].wait_recv()
+        at = pieces[g]
+        merged[at, :] = kept_buf[at, :] * columns[:, g:g + 1] + near_buf[at, :] * columns[:, 8 + g:9 + g]
+        far[groups if g == 0 else g - 1].start()
+
+    def attend_group_rows(first, a, b, columns, g):
+        part = pl.ds(g * 128, 128)
+        value = a[part, :] * columns[:, g:g + 1] + b[part, :] * columns[:, 8 + g:9 + g]
+        by_head = jnp.dot(order, value.astype(jnp.bfloat16), preferred_element_type=jnp.float32).astype(jnp.bfloat16)
+        for h in range(HEADS):
+            attended[first:first + GROUP, h * HEAD:(h + 1) * HEAD] = by_head[h * GROUP:(h + 1) * GROUP]
+
+    far[groups - 1].start()
+    for i, rows in enumerate(chunks):
         loads[2 * i].wait()
         loads[2 * i + 1].wait()
-        size = chunks[i] * HEADS + 8
-        view = pl.ds(starts[i], size)
-        attend_rows(sum(chunks[:i]), chunks[i], one.at[view], two.at[view])
-
-    load_kept.wait()
-    near.wait_recv()
-    merge_kernel(late // GROUP, kept_buf, near_buf, merged)
-    early_rows(0)
-    far = remote(src_ref=merged, dst_ref=far_buf, send_sem=send_sem.at[1], recv_sem=recv_sem.at[1], device_id=across)
-    far.start()
-    for i in range(1, len(chunks)):
-        early_rows(i)
+        view = pl.ds(starts[i], rows * HEADS + 8)
+        a, b = one.at[view], two.at[view]
+        columns, _, _ = merge_scales(a, b, rows // GROUP, True)
+        for g in range(rows // GROUP):
+            attend_group_rows(sum(chunks[:i]) + g * GROUP, a, b, columns, g)
     load_w.wait()
 
     def tile_copy(n):
         return remote(src_ref=y_early.at[n], dst_ref=got_early.at[n], send_sem=tile_send.at[n], recv_sem=tile_recv.at[n], device_id=sibling)
 
-    def early_tile(n, carry):
-        columns = pl.ds(pl.multiple_of(n * HEAD, HEAD), HEAD)
-        y_early[n] = jnp.dot(attended[:early, :], weights[:, columns], preferred_element_type=jnp.float32)
-
-        @pl.when(n > 0)
-        def _():
-            tile_copy(n - 1).start()
-
-        return carry
-
-    lax.fori_loop(0, tiles, early_tile, 0)
+    def late_copy(n):
+        return remote(src_ref=y_late.at[n], dst_ref=got_late.at[n], send_sem=late_send.at[n], recv_sem=late_recv.at[n], device_id=sibling)
+
+    def products(rows, y, copy_of):
+        def step(n, carry):
+            at = pl.ds(pl.multiple_of(n * width, width), width)
+            y[n] = jnp.dot(attended[rows, :], weights[:, at], preferred_element_type=jnp.float32)
+
+            @pl.when(n > 0)
+            def _():
+                copy_of(n - 1).start()
+
+            return carry
+
+        lax.fori_loop(0, tiles, step, 0)
+
+    products(slice(0, early), y_early, tile_copy)
     load_x.wait()
 
-    def add_rows(base, count, tile_of):
-        def step(i, carry):
-            rows = pl.ds(pl.multiple_of(base + i * GROUP, GROUP), GROUP)
+    def add_rows(base, count, y, i):
+        def step(r, carry):
+            local = pl.ds(pl.multiple_of(r * GROUP, GROUP), GROUP)
+            rows = pl.ds(pl.multiple_of(base + r * GROUP, GROUP), GROUP)
             for n in range(tiles):
-                columns = slice(n * HEAD, (n + 1) * HEAD)
-                out[rows, columns] = (x[rows, columns].astype(jnp.float32) + tile_of(n, pl.ds(pl.multiple_of(i * GROUP, GROUP), GROUP))).astype(jnp.bfloat16)
+                at = slice(n * width, (n + 1) * width)
+                out[rows, at] = (x[rows, at].astype(jnp.float32) + y[n, local, :]).astype(jnp.bfloat16)
             return carry
 
         lax.fori_loop(0, count // GROUP, step, 0)
+        at = pl.ds(pl.multiple_of(base, GROUP), count)
+        return pltpu.make_async_copy(out.at[at], result.at[at], out_sem.at[i])
 
     mine, other = core * half, (1 - core) * half
-    add_rows(mine, early, lambda n, rows: y_early[n, rows, :])
     tile_copy(tiles - 1).start()
+    saves = [add_rows(mine, early, y_early, 0)]
     for n in range(tiles):
         tile_copy(n).wait_recv()
-    add_rows(other, early, lambda n, rows: got_early[n, rows, :])
-    far.wait_recv()
-    attend_rows(early, late, merged, far_buf)
-
-    def late_tile(n, carry):
-        columns = pl.ds(pl.multiple_of(n * HEAD, HEAD), HEAD)
-        y_late[n] = jnp.dot(attended[early:, :], weights[:, columns], preferred_element_type=jnp.float32)
-        return carry
-
-    lax.fori_loop(0, tiles, late_tile, 0)
-    add_rows(mine + early, late, lambda n, rows: y_late[n, rows, :])
-    swap = remote(src_ref=y_late, dst_ref=got_late, send_sem=send_sem.at[2], recv_sem=recv_sem.at[2], device_id=sibling)
-    swap.start()
-    near.wait_send()
-    far.wait_send()
+    saves[0].start()
+    saves.append(add_rows(other, early, got_early, 1))
+    far[groups].wait_recv()
+    saves[1].start()
+    columns, _, _ = merge_scales(merged, far_buf, groups, True)
+    for g in range(groups):
+        far[g].wait_recv()
+        attend_group_rows(early + g * GROUP, merged, far_buf, columns, g)
+    products(slice(early, half), y_late, late_copy)
+    late_copy(tiles - 1).start()
+    saves.append(add_rows(mine + early, late, y_late, 2))
+    for copy in (*near, *far):
+        copy.wait_send()
     for n in range(tiles):
         tile_copy(n).wait_send()
-    swap.wait_recv()
-    add_rows(other + early, late, lambda n, rows: got_late[n, rows, :])
-    swap.wait_send()
+    saves[2].start()
+    for n in range(tiles):
+        late_copy(n).wait_recv()
+    saves.append(add_rows(other + early, late, got_late, 3))
+    for n in range(tiles):
+        late_copy(n).wait_send()
+    saves[3].start()
+    for copy in saves:
+        copy.wait()
 
 
 def tail_call(chunks, late, kept, sent, pairs, w_o, hidden):
     early = sum(chunks)
-    tiles = w_o.shape[1] // HEAD
+    width = 2 * HEAD
+    tiles = w_o.shape[1] // width
     part = pltpu.VMEM(kept.shape, jnp.float32)
     stacked = pltpu.VMEM((early * HEADS + 8 * len(chunks), HEAD), jnp.float32)
-    y_early, y_late = (pltpu.VMEM((tiles, rows, HEAD), jnp.float32) for rows in (early, late))
+    y_early, y_late = (pltpu.VMEM((tiles, rows, width), jnp.float32) for rows in (early, late))
+    dma = lambda n: pltpu.SemaphoreType.DMA((n,))
+    count = late // GROUP + 1
+    whole = pltpu.VMEM(hidden.shape, hidden.dtype)
     return pl.pallas_call(
         functools.partial(tail_kernel, chunks, late),
         out_shape=jax.ShapeDtypeStruct(hidden.shape, hidden.dtype),
         in_specs=[HBM] * (4 + len(pairs)),
-        out_specs=VMEM,
-        scratch_shapes=[part, part, part, part, stacked, stacked, pltpu.VMEM(w_o.shape, w_o.dtype), pltpu.VMEM(hidden.shape, hidden.dtype),
+        out_specs=HBM,
+        scratch_shapes=[part, part, part, part, stacked, stacked, pltpu.VMEM(w_o.shape, w_o.dtype), whole, whole,
                         pltpu.VMEM((early + late, w_o.shape[0]), jnp.bfloat16), y_early, y_late, y_early, y_late,
-                        pltpu.SemaphoreType.DMA((3 + len(pairs),)), pltpu.SemaphoreType.DMA((3,)), pltpu.SemaphoreType.DMA((3,)),
-                        pltpu.SemaphoreType.DMA((tiles,)), pltpu.SemaphoreType.DMA((tiles,))],
+                        dma(3 + len(pairs)), *[dma(count)] * 4, *[dma(tiles)] * 4, dma(4)],
         compiler_params=pltpu.CompilerParams(vmem_limit_bytes=62 << 20, collective_id=0, has_side_effects=True),
         cost_estimate=pl.CostEstimate(flops=4_000_000_000, bytes_accessed=20 << 20, transcendentals=0),
         name="tail",

time: 117 us -> 114 us (0.974)
  Pallas kernels: 86.5 us -> 83.3 us
    pallas_call x1, Pallas kernels: 23.8 us -> 20.6 us  [tail_call(): pl.pallas_call(functools.partial(tail_kernel, chunks, late), out_shape=ja...]
where the time goes in v8:
time: 114 us
  Pallas kernels  83.3 us (73%)
  waiting for transfers between devices  19.7 us (17%)
  starting transfers between devices  6.69 us (6%)
  local copies, waits for them, and re-layouts  3.22 us (3%)
    pallas_call x3, Pallas kernels, attention_call(): pl.pallas_call(functools.partial(attention_kernel, first_row, groups, mod...  59.5 us
    pallas_call x1, Pallas kernels, tail_call(): pl.pallas_call(functools.partial(tail_kernel, chunks, late), out_shape=ja...  20.6 us
    ppermute x2, waiting for transfers between devices, local_step(): theirs.append(lax.ppermute(merged[-1], 'sp', across))  17.4 us
    ppermute x2, starting transfers between devices, local_step(): theirs.append(lax.ppermute(merged[-1], 'sp', across))  4.93 us
    unnamed x10, local copies, waits for them, and re-layouts  3.22 us
    pallas_call x1, Pallas kernels, emit_call(): pl.pallas_call(emit_kernel, out_shape=jax.ShapeDtypeStruct(source.shape,...  2.39 us
    ppermute x2, waiting for transfers between devices, local_step(): taken = lax.ppermute(sent, 'sp', sibling)  2.32 us
  transfers between devices with their start and end apart: 4, of which 3 were waited for; matrix products, arithmetic and copies ran while one was open for 0% of the time, Pallas kernels for 13%

profile of v8, /device:TPU:0, one launch (start us, length us, event | category | flops | bytes accessed | tf_op | source)
XLA Modules:
  0.0 113.6 jit_solution(18357460781570165878)
XLA Ops:
  0.6 28.3 %shard_map.112 = (bf16[512,128,256]{2,1,0:T(8,128)(2,1)}, bf16[512,128,256]{2,1,0:T(8,128)(2,1)}, f32[904,256]{1,0:T(8,128)}, f32[904,256]{1,0:T(8,128)}, bf16[5...) custom-call(s32[512]{0:T(512)} %lengths.5, bf16[512,2048]{1,0:T(8,128)(2,1)} %refs_7_.3, ...), custom_call_target="tpu_custom_call" | custom-call | flops 2240000000 | bytes 58720256 | tf_op jit(solution)/shard_map/pallas_call | solution.py:293
  29.0 1.3 %collective-permute-start = (f32[904,256]{1,0:T(8,128)}, f32[904,256]{1,0:T(8,128)S(1)}, u32[]{:S(2)}, u32[]{:S(2)}) collective-permute-start(f32[904,256]{1,0:T(8,128)} %get-tuple-element.24), channel_id=1, source_target_pairs={{0,1},{1,0},{2,3},{3,2},{4,5},{5,4},{6,7},{7,6}} | collective-permute-start | bytes 2777096 | tf_op jit(solution)/shard_map/ppermute | solution.py:539
  30.3 2.3 %collective-permute-done.two = f32[904,256]{1,0:T(8,128)S(1)} collective-permute-done((f32[904,256]{1,0:T(8,128)}, f32[904,256]{1,0:T(8,128)S(1)}, u32[]{:S(2)}, u32[]{:S(2)}) %collective-permute-start) | collective-permute-done | bytes 925728 | tf_op jit(solution)/shard_map/ppermute | solution.py:539
  32.6 0.0 copy-start.3
  32.6 1.2 %copy-done.3 = f32[904,256]{1,0:T(8,128)S(1)} copy-done((f32[904,256]{1,0:T(8,128)S(1)}, f32[904,256]{1,0:T(8,128)}, u32[]{:S(2)}) %copy-start.3) | copy-done | bytes 925720
  33.8 0.4 shard_map.113.refs_7_.refs_2_
  34.3 0.0 copy-start
  34.3 0.9 copy-done
  35.2 0.0 copy-start.1
  35.2 16.8 %shard_map.114 = (bf16[512,128,256]{2,1,0:T(8,128)(2,1)}, bf16[512,128,256]{2,1,0:T(8,128)(2,1)}, f32[648,256]{1,0:T(8,128)}, f32[648,256]{1,0:T(8,128)}) custom-call(s32[512]{0:T(512)} %lengths.5, bf16[512,2048]{1,0:T(8,128)(2,1)} %get-tuple-element.18.refs_0_, f32[512,256]{1,0:T(8,128)} %get-tuple-element.19.refs_1_, ...), custom_call_target="tpu_custom_call", output_to_operand_aliasing={{0}: (6, {}), {1}: (7, {})} | custom-call | flops 1600000000 | bytes 41943040 | tf_op jit(solution)/shard_map/pallas_call | solution.py:293
  52.1 0.4 collective-permute-start.1
  52.5 0.0 copy-done.1
  52.5 2.6 %collective-permute-start.2 = (f32[904,256]{1,0:T(8,128)S(1)}, f32[904,256]{1,0:T(8,128)}, u32[]{:S(2)}, u32[]{:S(2)}) collective-permute-start(f32[904,256]{1,0:T(8,128)S(1)} %copy-done.1), channel_id=1, source_target_pairs={{0,2},{2,0},{1,3},{3,1},{4,6},{6,4},{5,7},{7,5}} | collective-permute-start | bytes 2777096 | tf_op jit(solution)/shard_map/ppermute | solution.py:541
  55.1 0.0 collective-permute-done.1.two
  55.2 0.0 copy-start.4
  55.2 1.1 copy-done.4
  56.2 0.4 shard_map.115.refs_7_.refs_4_
  56.6 0.0 copy-start.2
  56.6 2.3 %collective-permute-start.3 = (f32[648,256]{1,0:T(8,128)S(1)}, f32[648,256]{1,0:T(8,128)}, u32[]{:S(2)}, u32[]{:S(2)}) collective-permute-start(f32[648,256]{1,0:T(8,128)S(1)} %shard_map.115.refs_7_.refs_4_), channel_id=1, source_target_pairs={{0,2},{2,0},{1,3},{3,1},{4,6},{6,4},{5,7},{7,5}} | collective-permute-start | bytes 1990664 | tf_op jit(solution)/shard_map/ppermute | solution.py:541
  58.9 0.0 copy-done.2
  58.9 14.3 %shard_map.116 = (bf16[512,128,256]{2,1,0:T(8,128)(2,1)}, bf16[512,128,256]{2,1,0:T(8,128)(2,1)}, f32[520,256]{1,0:T(8,128)}, f32[520,256]{1,0:T(8,128)}) custom-call(s32[512]{0:T(512)} %lengths.5, bf16[512,2048]{1,0:T(8,128)(2,1)} %get-tuple-element.18.refs_0_, f32[512,256]{1,0:T(8,128)} %get-tuple-element.19.refs_1_, ...), custom_call_target="tpu_custom_call", output_to_operand_aliasing={{0}: (6, {}), {1}: (7, {})} | custom-call | flops 1280000000 | bytes 33554432 | tf_op jit(solution)/shard_map/pallas_call | solution.py:293
  73.2 3.4 %collective-permute-done.2.refs_3_ = f32[904,256]{1,0:T(8,128)} collective-permute-done((f32[904,256]{1,0:T(8,128)S(1)}, f32[904,256]{1,0:T(8,128)}, u32[]{:S(2)}, u32[]{:S(2)}) %collective-permute-start.2) | collective-permute-done | bytes 925728 | tf_op jit(solution)/shard_map/ppermute | solution.py:541
  76.6 14.0 %collective-permute-done.3.refs_5_ = f32[648,256]{1,0:T(8,128)} collective-permute-done((f32[648,256]{1,0:T(8,128)S(1)}, f32[648,256]{1,0:T(8,128)}, u32[]{:S(2)}, u32[]{:S(2)}) %collective-permute-start.3) | collective-permute-done | bytes 663584 | tf_op jit(solution)/shard_map/ppermute | solution.py:541
  90.6 20.6 %tail.1.source = bf16[512,2048]{1,0:T(8,128)(2,1)} custom-call(f32[520,256]{1,0:T(8,128)} %get-tuple-element.29.refs_0_, f32[520,256]{1,0:T(8,128)} %get-tuple-element.30.refs_1_, f32[904,256]{1,0:T(8,128)} %copy-done, f32[904,256]{1,0:T(8,128)} %collective-permute-done.2.refs_3_, f32[648,256]{1,0:T(8,128)} %copy-done.2, ...), custom_call_target="tpu_custom_call" | custom-call | flops 4000000000 | bytes 20971520 | tf_op jit(solution)/shard_map/tail/pallas_call | solution.py:486
  111.2 2.4 %emit.1 = bf16[512,2048]{1,0:T(8,128)(2,1)} custom-call(bf16[512,2048]{1,0:T(8,128)(2,1)} %tail.1.source), custom_call_target="tpu_custom_call" | custom-call | tf_op jit(solution)/shard_map/emit/pallas_call | solution.py:515
Async XLA Ops:
  29.0 3.6 %collective-permute-start = (f32[904,256]{1,0:T(8,128)}, f32[904,256]{1,0:T(8,128)S(1)}, u32[]{:S(2)}, u32[]{:S(2)}) collective-permute-start(f32[904,256]{1,0:T(8,128)} %get-tuple-element.24), channel_id=1, source_target_pairs={{0,1},{1,0},{2,3},{3,2},{4,5},{5,4},{6,7},{7,6}} | collective-permute-start | bytes 2777096 | tf_op jit(solution)/shard_map/ppermute | solution.py:539
  32.6 1.2 %copy-start.3 = (f32[904,256]{1,0:T(8,128)S(1)}, f32[904,256]{1,0:T(8,128)}, u32[]{:S(2)}) copy-start(f32[904,256]{1,0:T(8,128)} %get-tuple-element.23.one) | copy-start | bytes 2777092
  34.3 1.0 copy-start
  35.2 17.3 %copy-start.1 = (f32[904,256]{1,0:T(8,128)S(1)}, f32[904,256]{1,0:T(8,128)}, u32[]{:S(2)}) copy-start(f32[904,256]{1,0:T(8,128)} %copy-done) | copy-start | bytes 2777092
  52.1 3.1 %collective-permute-start.1 = (f32[648,256]{1,0:T(8,128)}, f32[648,256]{1,0:T(8,128)S(1)}, u32[]{:S(2)}, u32[]{:S(2)}) collective-permute-start(f32[648,256]{1,0:T(8,128)} %get-tuple-element.28), channel_id=1, source_target_pairs={{0,1},{1,0},{2,3},{3,2},{4,5},{5,4},{6,7},{7,6}} | collective-permute-start | bytes 1990664 | tf_op jit(solution)/shard_map/ppermute | solution.py:539
  52.5 24.1 %collective-permute-start.2 = (f32[904,256]{1,0:T(8,128)S(1)}, f32[904,256]{1,0:T(8,128)}, u32[]{:S(2)}, u32[]{:S(2)}) collective-permute-start(f32[904,256]{1,0:T(8,128)S(1)} %copy-done.1), channel_id=1, source_target_pairs={{0,2},{2,0},{1,3},{3,1},{4,6},{6,4},{5,7},{7,5}} | collective-permute-start | bytes 2777096 | tf_op jit(solution)/shard_map/ppermute | solution.py:541
  55.2 1.1 copy-start.4
  56.6 2.3 %copy-start.2 = (f32[648,256]{1,0:T(8,128)}, f32[648,256]{1,0:T(8,128)S(1)}, u32[]{:S(2)}) copy-start(f32[648,256]{1,0:T(8,128)S(1)} %shard_map.115.refs_7_.refs_4_) | copy-start | bytes 1990660
  56.6 34.0 %collective-permute-start.3 = (f32[648,256]{1,0:T(8,128)S(1)}, f32[648,256]{1,0:T(8,128)}, u32[]{:S(2)}, u32[]{:S(2)}) collective-permute-start(f32[648,256]{1,0:T(8,128)S(1)} %shard_map.115.refs_7_.refs_4_), channel_id=1, source_target_pairs={{0,2},{2,0},{1,3},{3,1},{4,6},{6,4},{5,7},{7,5}} | collective-permute-start | bytes 1990664 | tf_op jit(solution)/shard_map/ppermute | solution.py:541
